TPU v7x, 1024 devices: a whole 4x8x16 slice. The times are simulated.
1024 devices in a mesh: gx: 8 (over y), gy: 16 (over z), gz: 8 (over x, core).
Axes of the slice: x: 4, y: 8, z: 16, core: 2. Of those that a mesh axis runs over, the one named last changes fastest.
Arguments:
- density: float32 [96, 256, 1024], P('gx', 'gy', 'gz'), may hold values from 0.5 to 8
- potential: float32 [96, 256, 1024], P('gx', 'gy', 'gz'), may hold values from -6 to 6
Outputs:
- corrected: float32 [96, 256, 1024], P('gx', 'gy', 'gz')
All inputs are finite; a program needn't handle non-finite values.
Results may differ from a plain program's by a relative error of at most 0.00005.
Values sent between devices are 32-bit elements; how exact they have to be, the bound alone decides.
No kernel may reach another device: no remote copies, remote signals or barrier semaphores. Data moves between devices by JAX's collectives and lax.ppermute only.
A program may use at most 64 MiB of HBM per device.

v0:
```python
import jax
import jax.numpy as jnp
from jax import lax
from jax.sharding import Mesh
from jax.sharding import PartitionSpec as P

SWEEPS = 2
GX_GY_GZ = ("gx", "gy", "gz_0", "gz_1")
GZ = ("gz_0", "gz_1")


def with_halo(cells, sides, width):
    for axis, dim in sides:
        count = lax.axis_size(axis)
        head = lax.slice_in_dim(cells, 0, width, axis=dim)
        tail = lax.slice_in_dim(cells, cells.shape[dim] - width, cells.shape[dim], axis=dim)
        cells = jnp.concatenate(
            [
                lax.ppermute(tail, axis, [(i, (i + 1) % count) for i in range(count)]),
                cells,
                lax.ppermute(head, axis, [((i + 1) % count, i) for i in range(count)]),
            ],
            axis=dim,
        )
    return cells


def over_axes(array, axes):
    for axis in axes:
        array = lax.psum(array, axis)
    return array


def joined_along(parts, dim):
    parts = jnp.moveaxis(parts, 0, dim)
    dims = parts.shape
    return parts.reshape(*dims[:dim], dims[dim] * dims[dim + 1], *dims[dim + 2 :])


def sent_to_all(array, axis):
    peers = lax.axis_size(axis)
    return lax.all_to_all(
        jnp.broadcast_to(array[None], (peers, *array.shape)), axis, 0, 0, tiled=True
    )


def gathered_copies(array, axis, dim):
    return joined_along(sent_to_all(array, axis), dim)


def inner_sum(padded):
    total = padded[2:, 1:-1, 1:-1] + padded[:-2, 1:-1, 1:-1]
    total = total + padded[1:-1, 2:, 1:-1] + padded[1:-1, :-2, 1:-1]
    return total + padded[1:-1, 1:-1, 2:] + padded[1:-1, 1:-1, :-2]


def colour(shape, offset):
    summed = lax.broadcasted_iota(jnp.int32, shape, 0) + lax.broadcasted_iota(jnp.int32, shape, 1)
    summed = summed + lax.broadcasted_iota(jnp.int32, shape, 2) + offset
    return summed % 2 == 0


def basis(count):
    rows = lax.broadcasted_iota(jnp.int32, (count, count), 0).astype(jnp.float32)
    cols = lax.broadcasted_iota(jnp.int32, (count, count), 1)
    freq = ((cols + 1) // 2).astype(jnp.float32)
    angle = 2.0 * jnp.pi * freq * rows / count
    full = jnp.sqrt(2.0 / count)
    single = 1.0 / jnp.sqrt(jnp.float32(count))
    top = 2 * ((cols + 1) // 2) == count
    table = jnp.where(cols % 2 == 1, jnp.cos(angle) * full, jnp.sin(angle) * full)
    table = jnp.where(top, jnp.cos(angle) * single, table)
    table = jnp.where(cols == 0, single, table)
    modes = ((jnp.arange(count, dtype=jnp.int32) + 1) // 2).astype(jnp.float32)
    return (table, 2.0 - 2.0 * jnp.cos(2.0 * jnp.pi * modes / count))


def coarse_solve(blocks, weight_x, weight_y, weight_z):
    nx, ny, nz = blocks.shape
    qx, lx = basis(nx)
    qy, ly = basis(ny)
    qz, lz = basis(nz)
    hi = lax.Precision.HIGHEST
    spectrum = jnp.einsum("ia,jb,kc,ijk->abc", qx, qy, qz, blocks, precision=hi)
    denom = (
        weight_x * lx[:, None, None] + weight_y * ly[None, :, None] + weight_z * lz[None, None, :]
    )
    zero = colour((nx, ny, nz), 0) & (
        lax.broadcasted_iota(jnp.int32, (nx, ny, nz), 0)
        + lax.broadcasted_iota(jnp.int32, (nx, ny, nz), 1)
        + lax.broadcasted_iota(jnp.int32, (nx, ny, nz), 2)
        == 0
    )
    safe = jnp.where(zero, jnp.float32(1.0), denom)
    spectrum = jnp.where(zero, jnp.float32(0.0), -spectrum / safe)
    return jnp.einsum("ia,jb,kc,abc->ijk", qx, qy, qz, spectrum, precision=hi)


def trim(field, depth):
    if depth == 0:
        return field
    return field[depth:-depth, depth:-depth, depth:-depth]


def source_pad(source):
    return with_halo(source, (("gx", 0), ("gy", 1), (GZ, 2)), 2 * SWEEPS)


def sectioned(field, padded_source):
    reach = 2 * SWEEPS
    current = with_halo(field, (("gx", 0), ("gy", 1), (GZ, 2)), reach + 1)
    depth = reach + 1
    for sweep in range(SWEEPS):
        shell = trim(current, 1)
        red_shell = colour(shell.shape, depth - 1)
        shell = jnp.where(
            red_shell, (inner_sum(current) - trim(padded_source, reach - depth + 1)) / 6.0, shell
        )
        inside = trim(shell, 1)
        red_inside = colour(inside.shape, depth - 2)
        current = jnp.where(
            red_inside, inside, (inner_sum(shell) - trim(padded_source, reach - depth + 2)) / 6.0
        )
        depth = depth - 2
    inside = trim(current, 1)
    leftover = trim(padded_source, reach) - (inner_sum(current) - 6.0 * inside)
    return (inside, leftover)


def smooth_section(field, padded_source):
    return sectioned(field, padded_source)


def body(density, potential):
    sizes = lax.axis_size("gx") * lax.axis_size("gy") * lax.axis_size(GZ)
    total = over_axes(jnp.sum(density), GX_GY_GZ)
    source = density - total / (density.size * sizes)
    padded_source = source_pad(source)
    fine, left = smooth_section(potential, padded_source)
    cx, cy, cz = left.shape
    level_one = left.reshape(cx // 2, 2, cy // 2, 2, cz // 2, 2).sum(axis=(1, 3, 5)) * 0.5
    padded_one = source_pad(level_one)
    error_one = jnp.zeros_like(level_one)
    error_one, rest = smooth_section(error_one, padded_one)
    bx, by, bz = rest.shape
    local_block = jnp.sum(rest).reshape(1, 1, 1)
    blocks = gathered_copies(local_block, GZ, 2)
    blocks = gathered_copies(blocks, "gy", 1)
    blocks = gathered_copies(blocks, "gx", 0)
    coarse = coarse_solve(blocks, float(by * bz), float(bx * bz), float(bx * by))
    own = coarse[lax.axis_index("gx"), lax.axis_index("gy"), lax.axis_index(GZ)]
    error_one = error_one + own
    error_one, unused = smooth_section(error_one, padded_one)
    fine = fine + jnp.repeat(jnp.repeat(jnp.repeat(error_one, 2, 0), 2, 1), 2, 2)
    fine, unused = smooth_section(fine, padded_source)
    return fine


def solution(mesh):
    split = Mesh(
        mesh.devices.reshape(mesh.shape["gx"], mesh.shape["gy"], 4, 2), ("gx", "gy", "gz_0", "gz_1")
    )
    placed = (P("gx", "gy", GZ), P("gx", "gy", GZ))
    return jax.shard_map(
        body, mesh=split, in_specs=placed, out_specs=P("gx", "gy", GZ), check_vma=False
    )
```

profile of v0, /device:TPU:63, one launch (start us, length us, event | category | flops | bytes accessed | tf_op | source)
XLA Modules:
  0.0 283.6 jit_solution(15957046924239185973)
XLA Ops:
  1.5 11.8 %psum.28 = f32[]{:T(128)} all-reduce(f32[]{:T(128)} %reduce_sum.27), channel_id=1, replica_groups=mesh['gx'=8,'gy'=16,'gz_0'=4,'gz_1'=2] {'gx'}, use_global_device_ids=true, to_apply=%region_1.0 | all-reduce | flops 1 | bytes 8 | tf_op jit(solution)/shard_map/psum | solution.py:30
  13.3 36.7 %psum.29 = f32[]{:T(128)} all-reduce(f32[]{:T(128)} %psum.28), channel_id=1, replica_groups=mesh['gx'=8,'gy'=16,'gz_0'=4,'gz_1'=2] {'gy'}, use_global_device_ids=true, to_apply=%region_2.0 | all-reduce | flops 1 | bytes 8 | tf_op jit(solution)/shard_map/psum | solution.py:30
  50.0 4.0 %collective-permute-start.12 = (f32[5,8,64]{2,1,0:T(8,128)S(1)}, f32[5,8,64]{2,1,0:T(8,128)S(1)}, u32[]{:S(2)}, u32[]{:S(2)}) collective-permute-start(f32[5,8,64]{2,1,0:T(8,128)S(1)} %broadcast.488), channel_id=1, source_target_pairs={{0,128},{128,256},{256,384},{384,512},{512,640},{640,768},{768,896... | collective-permute-start | bytes 30728 | tf_op jit(solution)/shard_map/ppermute | solution.py:19
  54.1 6.4 %psum.30 = f32[]{:T(128)} all-reduce(f32[]{:T(128)} %psum.29), channel_id=1, replica_groups=mesh['gx'=8,'gy'=16,'gz_0'=4,'gz_1'=2] {'gz_0'}, use_global_device_ids=true, to_apply=%region_3.0 | all-reduce | flops 1 | bytes 8 | tf_op jit(solution)/shard_map/psum | solution.py:30
  62.4 16.4 %psum.31 = f32[]{:T(128)} all-reduce(f32[]{:T(128)} %psum.30), channel_id=1, replica_groups=mesh['gx'=8,'gy'=16,'gz_0'=4,'gz_1'=2] {'gz_1'}, use_global_device_ids=true, to_apply=%region_4.0 | all-reduce | flops 1 | bytes 8 | tf_op jit(solution)/shard_map/psum | solution.py:30
  80.4 4.9 %collective-permute-start.6 = (f32[4,16,128]{2,1,0:T(8,128)S(1)}, f32[4,16,128]{2,1,0:T(8,128)S(1)}, u32[]{:S(2)}, u32[]{:S(2)}) collective-permute-start(f32[4,16,128]{2,1,0:T(8,128)S(1)} %get-tuple-element.52), channel_id=1, source_target_pairs={{0,128},{128,256},{256,384},{384,512},{512,640},{640,768},{768,896... | collective-permute-start | bytes 98312 | tf_op jit(solution)/shard_map/ppermute | solution.py:19
  88.0 4.6 %collective-permute-start = (f32[5,16,128]{2,1,0:T(8,128)S(1)}, f32[5,16,128]{2,1,0:T(8,128)S(1)}, u32[]{:S(2)}, u32[]{:S(2)}) collective-permute-start(f32[5,16,128]{2,1,0:T(8,128)S(1)} %get-tuple-element.54), channel_id=1, source_target_pairs={{0,128},{128,256},{256,384},{384,512},{512,640},{640,768},{768,896... | collective-permute-start | bytes 122888 | tf_op jit(solution)/shard_map/ppermute | solution.py:19
  96.8 4.6 %collective-permute-start.15 = (f32[16,5,64]{2,1,0:T(8,128)S(1)}, f32[16,5,64]{2,1,0:T(8,128)S(1)}, u32[]{:S(2)}, u32[]{:S(2)}) collective-permute-start(f32[16,5,64]{2,1,0:T(8,128)S(1)} %get-tuple-element.64), channel_id=1, source_target_pairs={{8,0},{16,8},{24,16},{32,24},{40,32},{48,40},{56,48},{64,56},{72,6... | collective-permute-start | bytes 61448 | tf_op jit(solution)/shard_map/ppermute | solution.py:21
  103.3 4.6 %collective-permute-start.9 = (f32[20,4,128]{2,1,0:T(4,128)S(1)}, f32[20,4,128]{2,1,0:T(4,128)S(1)}, u32[]{:S(2)}, u32[]{:S(2)}) collective-permute-start(f32[20,4,128]{2,1,0:T(4,128)S(1)} %get-tuple-element.45), channel_id=1, source_target_pairs={{8,0},{16,8},{24,16},{32,24},{40,32},{48,40},{56,48},{64,56},{72,6... | collective-permute-start | bytes 122888 | tf_op jit(solution)/shard_map/ppermute | solution.py:21
  110.9 4.6 %collective-permute-start.3 = (f32[22,5,128]{2,0,1:T(8,128)S(1)}, f32[22,5,128]{2,0,1:T(8,128)S(1)}, u32[]{:S(2)}, u32[]{:S(2)}) collective-permute-start(f32[22,5,128]{2,0,1:T(8,128)S(1)} %copy.255), channel_id=1, source_target_pairs={{8,0},{16,8},{24,16},{32,24},{40,32},{48,40},{56,48},{64,56},{72,6... | collective-permute-start | bytes 168968 | tf_op jit(solution)/shard_map/ppermute | solution.py:21
  116.9 6.5 %collective-permute-start.4 = (f32[22,26,5]{2,0,1:T(8,128)S(1)}, f32[22,26,5]{2,0,1:T(8,128)S(1)}, u32[]{:S(2)}, u32[]{:S(2)}) collective-permute-start(f32[22,26,5]{2,0,1:T(8,128)S(1)} %get-tuple-element.32), channel_id=1, source_target_pairs={{0,1},{1,2},{2,3},{3,4},{4,5},{5,6},{6,7},{7,0},{8,9},{9,10},{10,1... | collective-permute-start | bytes 34328 | tf_op jit(solution)/shard_map/ppermute | solution.py:19
  127.3 3.7 %collective-permute-done.5 = f32[22,26,5]{2,0,1:T(8,128)S(1)} collective-permute-done((f32[22,26,5]{2,0,1:T(8,128)S(1)}, f32[22,26,5]{2,0,1:T(8,128)S(1)}, u32[]{:S(2)}, u32[]{:S(2)}) %collective-permute-start.5) | collective-permute-done | bytes 11472 | tf_op jit(solution)/shard_map/ppermute | solution.py:21
  139.0 7.7 %reshape.134 = f32[6,2,8,2,64,2]{5,4,3,2,1,0:T(8,128)} reshape(f32[12,16,128]{2,1,0:T(8,128)S(1)} %fusion.43) | data formatting | bytes 196608 | tf_op jit(solution)/shard_map/reshape | solution.py:141
  146.7 3.3 %reduce_sum.28 = f32[6,8,64]{2,1,0:T(8,128)S(1)} reduce(f32[6,2,8,2,64,2]{5,4,3,2,1,0:T(8,128)} %reshape.134, f32[]{:T(128)} %constant.279.clone.1), dimensions={1,3,5}, to_apply=%region_5.6 | reduce | flops 21504 | bytes 110596 | tf_op jit(solution)/shard_map/reduce_sum | solution.py:141
  150.0 4.9 %collective-permute-start.18 = (f32[4,8,64]{2,1,0:T(8,128)S(1)}, f32[4,8,64]{2,1,0:T(8,128)S(1)}, u32[]{:S(2)}, u32[]{:S(2)}) collective-permute-start(f32[4,8,64]{2,1,0:T(8,128)S(1)} %get-tuple-element.69), channel_id=1, source_target_pairs={{0,128},{128,256},{256,384},{384,512},{512,640},{640,768},{768,896... | collective-permute-start | bytes 24584 | tf_op jit(solution)/shard_map/ppermute | solution.py:19
  156.8 3.7 %collective-permute-done.19 = f32[4,8,64]{2,1,0:T(8,128)S(1)} collective-permute-done((f32[4,8,64]{2,1,0:T(8,128)S(1)}, f32[4,8,64]{2,1,0:T(8,128)S(1)}, u32[]{:S(2)}, u32[]{:S(2)}) %collective-permute-start.19) | collective-permute-done | bytes 8224 | tf_op jit(solution)/shard_map/ppermute | solution.py:21
  162.5 5.2 %collective-permute-start.21 = (f32[14,4,64]{2,1,0:T(4,128)S(1)}, f32[14,4,64]{2,1,0:T(4,128)S(1)}, u32[]{:S(2)}, u32[]{:S(2)}) collective-permute-start(f32[14,4,64]{2,1,0:T(4,128)S(1)} %get-tuple-element.66), channel_id=1, source_target_pairs={{8,0},{16,8},{24,16},{32,24},{40,32},{48,40},{56,48},{64,56},{72,6... | collective-permute-start | bytes 43016 | tf_op jit(solution)/shard_map/ppermute | solution.py:21
  172.5 3.2 %collective-permute-done.17 = f32[16,18,5]{2,1,0:T(8,128)S(1)} collective-permute-done((f32[16,18,5]{2,1,0:T(8,128)S(1)}, f32[16,18,5]{2,1,0:T(8,128)S(1)}, u32[]{:S(2)}, u32[]{:S(2)}) %collective-permute-start.17) | collective-permute-done | bytes 5792 | tf_op jit(solution)/shard_map/ppermute | solution.py:21
  180.3 7.0 %all_to_all.15 = f32[8,1,1,1]{3,2,1,0:T(1,128)S(1)} all-to-all(f32[8,1,1,1]{3,2,1,0:T(1,128)S(1)} %broadcast_in_dim.52), channel_id=1, replica_groups=mesh['gx'=8,'gy'=16,'gz_0'=4,'gz_1'=2] {'gz_0','gz_1'}, dimensions={0} | all-to-all | bytes 64 | tf_op jit(solution)/shard_map/all_to_all | solution.py:42
  188.0 4.5 %all-to-all-start.1 = ((f32[16,1,1,8]{3,2,1,0:T(1,128)}), f32[16,1,1,8]{3,2,1,0:T(1,128)S(1)}, u32[]{:S(2)}, u32[]{:S(2)}) async-start(f32[16,1,1,8]{3,2,1,0:T(1,128)} %broadcast_in_dim.54), calls=%async_computation.1 | async-start | bytes 16384 | tf_op jit(solution)/shard_map/all_to_all | solution.py:42
  192.5 11.2 %all-to-all-done.1 = f32[16,1,1,8]{3,2,1,0:T(1,128)S(1)} async-done(((f32[16,1,1,8]{3,2,1,0:T(1,128)}), f32[16,1,1,8]{3,2,1,0:T(1,128)S(1)}, u32[]{:S(2)}, u32[]{:S(2)}) %all-to-all-start.1) | async-done | bytes 544 | tf_op jit(solution)/shard_map/all_to_all | solution.py:42
  204.5 4.3 %all-to-all-start.2 = ((f32[8,1,128]{2,1,0:T(1,128)}), f32[8,1,128]{2,1,0:T(1,128)S(1)}, u32[]{:S(2)}, u32[]{:S(2)}) async-start(f32[8,1,128]{2,1,0:T(1,128)} %reshape.143), calls=%async_computation.2 | async-start | bytes 8192 | tf_op jit(solution)/shard_map/all_to_all | solution.py:42
  208.8 4.1 %all-to-all-done.2 = f32[8,1,128]{2,1,0:T(1,128)S(1)} async-done(((f32[8,1,128]{2,1,0:T(1,128)}), f32[8,1,128]{2,1,0:T(1,128)S(1)}, u32[]{:S(2)}, u32[]{:S(2)}) %all-to-all-start.2) | async-done | bytes 4128 | tf_op jit(solution)/shard_map/all_to_all | solution.py:42
  217.4 4.3 %collective-permute-start.24 = (f32[5,8,64]{2,1,0:T(8,128)S(1)}, f32[5,8,64]{2,1,0:T(8,128)S(1)}, u32[]{:S(2)}, u32[]{:S(2)}) collective-permute-start(f32[5,8,64]{2,1,0:T(8,128)S(1)} %get-tuple-element.67), channel_id=1, source_target_pairs={{0,128},{128,256},{256,384},{384,512},{512,640},{640,768},{768,896... | collective-permute-start | bytes 30728 | tf_op jit(solution)/shard_map/ppermute | solution.py:19
  223.6 3.8 %collective-permute-done.25 = f32[5,8,64]{2,1,0:T(8,128)S(1)} collective-permute-done((f32[5,8,64]{2,1,0:T(8,128)S(1)}, f32[5,8,64]{2,1,0:T(8,128)S(1)}, u32[]{:S(2)}, u32[]{:S(2)}) %collective-permute-start.25) | collective-permute-done | bytes 10272 | tf_op jit(solution)/shard_map/ppermute | solution.py:21
  229.7 4.3 %collective-permute-start.27 = (f32[16,5,64]{2,1,0:T(8,128)S(1)}, f32[16,5,64]{2,1,0:T(8,128)S(1)}, u32[]{:S(2)}, u32[]{:S(2)}) collective-permute-start(f32[16,5,64]{2,1,0:T(8,128)S(1)} %get-tuple-element.62), channel_id=1, source_target_pairs={{8,0},{16,8},{24,16},{32,24},{40,32},{48,40},{56,48},{64,56},{72,6... | collective-permute-start | bytes 61448 | tf_op jit(solution)/shard_map/ppermute | solution.py:21
  235.4 7.8 %collective-permute-start.28 = (f32[16,18,5]{2,1,0:T(8,128)S(1)}, f32[16,18,5]{2,1,0:T(8,128)S(1)}, u32[]{:S(2)}, u32[]{:S(2)}) collective-permute-start(f32[16,18,5]{2,1,0:T(8,128)S(1)} %get-tuple-element.36), channel_id=1, source_target_pairs={{0,1},{1,2},{2,3},{3,4},{4,5},{5,6},{6,7},{7,0},{8,9},{9,10},{10,1... | collective-permute-start | bytes 17288 | tf_op jit(solution)/shard_map/ppermute | solution.py:19
  245.8 3.7 %collective-permute-done.29 = f32[16,18,5]{2,1,0:T(8,128)S(1)} collective-permute-done((f32[16,18,5]{2,1,0:T(8,128)S(1)}, f32[16,18,5]{2,1,0:T(8,128)S(1)}, u32[]{:S(2)}, u32[]{:S(2)}) %collective-permute-start.29) | collective-permute-done | bytes 5792 | tf_op jit(solution)/shard_map/ppermute | solution.py:21
  253.5 3.4 %collective-permute-start.31 = (f32[5,16,128]{2,1,0:T(8,128)S(1)}, f32[5,16,128]{2,1,0:T(8,128)S(1)}, u32[]{:S(2)}, u32[]{:S(2)}) collective-permute-start(f32[5,16,128]{2,1,0:T(8,128)S(1)} %get-tuple-element.51), channel_id=1, source_target_pairs={{128,0},{256,128},{384,256},{512,384},{640,512},{768,640},{896,768... | collective-permute-start | bytes 122888 | tf_op jit(solution)/shard_map/ppermute | solution.py:21
  261.5 5.2 %collective-permute-start.33 = (f32[22,5,128]{2,0,1:T(8,128)S(1)}, f32[22,5,128]{2,0,1:T(8,128)S(1)}, u32[]{:S(2)}, u32[]{:S(2)}) collective-permute-start(f32[22,5,128]{2,0,1:T(8,128)S(1)} %copy.167), channel_id=1, source_target_pairs={{8,0},{16,8},{24,16},{32,24},{40,32},{48,40},{56,48},{64,56},{72,6... | collective-permute-start | bytes 168968 | tf_op jit(solution)/shard_map/ppermute | solution.py:21
  270.3 3.7 %collective-permute-done.34 = f32[22,26,5]{2,0,1:T(8,128)S(1)} collective-permute-done((f32[22,26,5]{2,0,1:T(8,128)S(1)}, f32[22,26,5]{2,0,1:T(8,128)S(1)}, u32[]{:S(2)}, u32[]{:S(2)}) %collective-permute-start.34) | collective-permute-done | bytes 11472 | tf_op jit(solution)/shard_map/ppermute | solution.py:19
  274.1 3.7 %collective-permute-done.35 = f32[22,26,5]{2,0,1:T(8,128)S(1)} collective-permute-done((f32[22,26,5]{2,0,1:T(8,128)S(1)}, f32[22,26,5]{2,0,1:T(8,128)S(1)}, u32[]{:S(2)}, u32[]{:S(2)}) %collective-permute-start.35) | collective-permute-done | bytes 11472 | tf_op jit(solution)/shard_map/ppermute | solution.py:21
  (159 shorter events, 74.5 us)
Async XLA Ops:
  50.0 42.8 %collective-permute-start.12 = (f32[5,8,64]{2,1,0:T(8,128)S(1)}, f32[5,8,64]{2,1,0:T(8,128)S(1)}, u32[]{:S(2)}, u32[]{:S(2)}) collective-permute-start(f32[5,8,64]{2,1,0:T(8,128)S(1)} %broadcast.488), channel_id=1, source_target_pairs={{0,128},{128,256},{256,384},{384,512},{512,640},{640,768},{768,896... | collective-permute-start | bytes 30728 | tf_op jit(solution)/shard_map/ppermute | solution.py:19
  60.5 34.3 %collective-permute-start.13 = (f32[5,8,64]{2,1,0:T(8,128)S(1)}, f32[5,8,64]{2,1,0:T(8,128)S(1)}, u32[]{:S(2)}, u32[]{:S(2)}) collective-permute-start(f32[5,8,64]{2,1,0:T(8,128)S(1)} %broadcast.488), channel_id=1, source_target_pairs={{128,0},{256,128},{384,256},{512,384},{640,512},{768,640},{896,768... | collective-permute-start | bytes 30728 | tf_op jit(solution)/shard_map/ppermute | solution.py:21
  80.4 16.4 %collective-permute-start.6 = (f32[4,16,128]{2,1,0:T(8,128)S(1)}, f32[4,16,128]{2,1,0:T(8,128)S(1)}, u32[]{:S(2)}, u32[]{:S(2)}) collective-permute-start(f32[4,16,128]{2,1,0:T(8,128)S(1)} %get-tuple-element.52), channel_id=1, source_target_pairs={{0,128},{128,256},{256,384},{384,512},{512,640},{640,768},{768,896... | collective-permute-start | bytes 98312 | tf_op jit(solution)/shard_map/ppermute | solution.py:19
  85.3 16.1 %collective-permute-start.7 = (f32[4,16,128]{2,1,0:T(8,128)S(1)}, f32[4,16,128]{2,1,0:T(8,128)S(1)}, u32[]{:S(2)}, u32[]{:S(2)}) collective-permute-start(f32[4,16,128]{2,1,0:T(8,128)S(1)} %get-tuple-element.53), channel_id=1, source_target_pairs={{128,0},{256,128},{384,256},{512,384},{640,512},{768,640},{896,768... | collective-permute-start | bytes 98312 | tf_op jit(solution)/shard_map/ppermute | solution.py:21
  88.0 15.3 %collective-permute-start = (f32[5,16,128]{2,1,0:T(8,128)S(1)}, f32[5,16,128]{2,1,0:T(8,128)S(1)}, u32[]{:S(2)}, u32[]{:S(2)}) collective-permute-start(f32[5,16,128]{2,1,0:T(8,128)S(1)} %get-tuple-element.54), channel_id=1, source_target_pairs={{0,128},{128,256},{256,384},{384,512},{512,640},{640,768},{768,896... | collective-permute-start | bytes 122888 | tf_op jit(solution)/shard_map/ppermute | solution.py:19
  92.9 15.1 %collective-permute-start.1 = (f32[5,16,128]{2,1,0:T(8,128)S(1)}, f32[5,16,128]{2,1,0:T(8,128)S(1)}, u32[]{:S(2)}, u32[]{:S(2)}) collective-permute-start(f32[5,16,128]{2,1,0:T(8,128)S(1)} %get-tuple-element.55), channel_id=1, source_target_pairs={{128,0},{256,128},{384,256},{512,384},{640,512},{768,640},{896,768... | collective-permute-start | bytes 122888 | tf_op jit(solution)/shard_map/ppermute | solution.py:21
  94.9 61.9 %collective-permute-start.14 = (f32[16,5,64]{2,1,0:T(8,128)S(1)}, f32[16,5,64]{2,1,0:T(8,128)S(1)}, u32[]{:S(2)}, u32[]{:S(2)}) collective-permute-start(f32[16,5,64]{2,1,0:T(8,128)S(1)} %get-tuple-element.63), channel_id=1, source_target_pairs={{0,8},{8,16},{16,24},{24,32},{32,40},{40,48},{48,56},{56,64},{64,7... | collective-permute-start | bytes 61448 | tf_op jit(solution)/shard_map/ppermute | solution.py:19
  96.8 60.0 %collective-permute-start.15 = (f32[16,5,64]{2,1,0:T(8,128)S(1)}, f32[16,5,64]{2,1,0:T(8,128)S(1)}, u32[]{:S(2)}, u32[]{:S(2)}) collective-permute-start(f32[16,5,64]{2,1,0:T(8,128)S(1)} %get-tuple-element.64), channel_id=1, source_target_pairs={{8,0},{16,8},{24,16},{32,24},{40,32},{48,40},{56,48},{64,56},{72,6... | collective-permute-start | bytes 61448 | tf_op jit(solution)/shard_map/ppermute | solution.py:21
  101.4 9.4 %collective-permute-start.8 = (f32[20,4,128]{2,1,0:T(4,128)S(1)}, f32[20,4,128]{2,1,0:T(4,128)S(1)}, u32[]{:S(2)}, u32[]{:S(2)}) collective-permute-start(f32[20,4,128]{2,1,0:T(4,128)S(1)} %get-tuple-element.44), channel_id=1, source_target_pairs={{0,8},{8,16},{16,24},{24,32},{32,40},{40,48},{48,56},{56,64},{64,7... | collective-permute-start | bytes 122888 | tf_op jit(solution)/shard_map/ppermute | solution.py:19
  103.3 12.1 %collective-permute-start.9 = (f32[20,4,128]{2,1,0:T(4,128)S(1)}, f32[20,4,128]{2,1,0:T(4,128)S(1)}, u32[]{:S(2)}, u32[]{:S(2)}) collective-permute-start(f32[20,4,128]{2,1,0:T(4,128)S(1)} %get-tuple-element.45), channel_id=1, source_target_pairs={{8,0},{16,8},{24,16},{32,24},{40,32},{48,40},{56,48},{64,56},{72,6... | collective-permute-start | bytes 122888 | tf_op jit(solution)/shard_map/ppermute | solution.py:21
  108.9 6.6 %collective-permute-start.2 = (f32[22,5,128]{2,0,1:T(8,128)S(1)}, f32[22,5,128]{2,0,1:T(8,128)S(1)}, u32[]{:S(2)}, u32[]{:S(2)}) collective-permute-start(f32[22,5,128]{2,0,1:T(8,128)S(1)} %copy.254), channel_id=1, source_target_pairs={{0,8},{8,16},{16,24},{24,32},{32,40},{40,48},{48,56},{56,64},{64,7... | collective-permute-start | bytes 168968 | tf_op jit(solution)/shard_map/ppermute | solution.py:19
  110.9 5.9 %collective-permute-start.3 = (f32[22,5,128]{2,0,1:T(8,128)S(1)}, f32[22,5,128]{2,0,1:T(8,128)S(1)}, u32[]{:S(2)}, u32[]{:S(2)}) collective-permute-start(f32[22,5,128]{2,0,1:T(8,128)S(1)} %copy.255), channel_id=1, source_target_pairs={{8,0},{16,8},{24,16},{32,24},{40,32},{48,40},{56,48},{64,56},{72,6... | collective-permute-start | bytes 168968 | tf_op jit(solution)/shard_map/ppermute | solution.py:21
  116.9 10.5 %collective-permute-start.4 = (f32[22,26,5]{2,0,1:T(8,128)S(1)}, f32[22,26,5]{2,0,1:T(8,128)S(1)}, u32[]{:S(2)}, u32[]{:S(2)}) collective-permute-start(f32[22,26,5]{2,0,1:T(8,128)S(1)} %get-tuple-element.32), channel_id=1, source_target_pairs={{0,1},{1,2},{2,3},{3,4},{4,5},{5,6},{6,7},{7,0},{8,9},{9,10},{10,1... | collective-permute-start | bytes 34328 | tf_op jit(solution)/shard_map/ppermute | solution.py:19
  123.4 7.6 %collective-permute-start.5 = (f32[22,26,5]{2,0,1:T(8,128)S(1)}, f32[22,26,5]{2,0,1:T(8,128)S(1)}, u32[]{:S(2)}, u32[]{:S(2)}) collective-permute-start(f32[22,26,5]{2,0,1:T(8,128)S(1)} %get-tuple-element.33), channel_id=1, source_target_pairs={{1,0},{2,1},{3,2},{4,3},{5,4},{6,5},{7,6},{0,7},{9,8},{10,9},{11,1... | collective-permute-start | bytes 34328 | tf_op jit(solution)/shard_map/ppermute | solution.py:21
  123.5 8.8 %collective-permute-start.10 = (f32[20,24,4]{2,1,0:T(8,128)S(1)}, f32[20,24,4]{2,1,0:T(8,128)S(1)}, u32[]{:S(2)}, u32[]{:S(2)}) collective-permute-start(f32[20,24,4]{2,1,0:T(8,128)S(1)} %get-tuple-element.34), channel_id=1, source_target_pairs={{0,1},{1,2},{2,3},{3,4},{4,5},{5,6},{6,7},{7,0},{8,9},{9,10},{10,1... | collective-permute-start | bytes 23048 | tf_op jit(solution)/shard_map/ppermute | solution.py:19
  127.3 7.6 %collective-permute-start.11 = (f32[20,24,4]{2,1,0:T(8,128)S(1)}, f32[20,24,4]{2,1,0:T(8,128)S(1)}, u32[]{:S(2)}, u32[]{:S(2)}) collective-permute-start(f32[20,24,4]{2,1,0:T(8,128)S(1)} %get-tuple-element.35), channel_id=1, source_target_pairs={{1,0},{2,1},{3,2},{4,3},{5,4},{6,5},{7,6},{0,7},{9,8},{10,9},{11,1... | collective-permute-start | bytes 23048 | tf_op jit(solution)/shard_map/ppermute | solution.py:21
  150.0 6.9 %collective-permute-start.18 = (f32[4,8,64]{2,1,0:T(8,128)S(1)}, f32[4,8,64]{2,1,0:T(8,128)S(1)}, u32[]{:S(2)}, u32[]{:S(2)}) collective-permute-start(f32[4,8,64]{2,1,0:T(8,128)S(1)} %get-tuple-element.69), channel_id=1, source_target_pairs={{0,128},{128,256},{256,384},{384,512},{512,640},{640,768},{768,896... | collective-permute-start | bytes 24584 | tf_op jit(solution)/shard_map/ppermute | solution.py:19
  160.6 8.8 %collective-permute-start.20 = (f32[14,4,64]{2,1,0:T(4,128)S(1)}, f32[14,4,64]{2,1,0:T(4,128)S(1)}, u32[]{:S(2)}, u32[]{:S(2)}) collective-permute-start(f32[14,4,64]{2,1,0:T(4,128)S(1)} %get-tuple-element.65), channel_id=1, source_target_pairs={{0,8},{8,16},{16,24},{24,32},{32,40},{40,48},{48,56},{56,64},{64,7... | collective-permute-start | bytes 43016 | tf_op jit(solution)/shard_map/ppermute | solution.py:19
  162.5 6.9 %collective-permute-start.21 = (f32[14,4,64]{2,1,0:T(4,128)S(1)}, f32[14,4,64]{2,1,0:T(4,128)S(1)}, u32[]{:S(2)}, u32[]{:S(2)}) collective-permute-start(f32[14,4,64]{2,1,0:T(4,128)S(1)} %get-tuple-element.66), channel_id=1, source_target_pairs={{8,0},{16,8},{24,16},{32,24},{40,32},{48,40},{56,48},{64,56},{72,6... | collective-permute-start | bytes 43016 | tf_op jit(solution)/shard_map/ppermute | solution.py:21
  169.4 6.3 %collective-permute-start.17 = (f32[16,18,5]{2,1,0:T(8,128)S(1)}, f32[16,18,5]{2,1,0:T(8,128)S(1)}, u32[]{:S(2)}, u32[]{:S(2)}) collective-permute-start(f32[16,18,5]{2,1,0:T(8,128)S(1)} %get-tuple-element.39), channel_id=1, source_target_pairs={{1,0},{2,1},{3,2},{4,3},{5,4},{6,5},{7,6},{0,7},{9,8},{10,9},{11,1... | collective-permute-start | bytes 17288 | tf_op jit(solution)/shard_map/ppermute | solution.py:21
  169.5 6.4 %collective-permute-start.22 = (f32[14,16,4]{2,1,0:T(8,128)S(1)}, f32[14,16,4]{2,1,0:T(8,128)S(1)}, u32[]{:S(2)}, u32[]{:S(2)}) collective-permute-start(f32[14,16,4]{2,1,0:T(8,128)S(1)} %get-tuple-element.48), channel_id=1, source_target_pairs={{0,1},{1,2},{2,3},{3,4},{4,5},{5,6},{6,7},{7,0},{8,9},{9,10},{10,1... | collective-permute-start | bytes 10760 | tf_op jit(solution)/shard_map/ppermute | solution.py:19
  188.0 15.7 %all-to-all-start.1 = ((f32[16,1,1,8]{3,2,1,0:T(1,128)}), f32[16,1,1,8]{3,2,1,0:T(1,128)S(1)}, u32[]{:S(2)}, u32[]{:S(2)}) async-start(f32[16,1,1,8]{3,2,1,0:T(1,128)} %broadcast_in_dim.54), calls=%async_computation.1 | async-start | bytes 16384 | tf_op jit(solution)/shard_map/all_to_all | solution.py:42
  204.5 8.4 %all-to-all-start.2 = ((f32[8,1,128]{2,1,0:T(1,128)}), f32[8,1,128]{2,1,0:T(1,128)S(1)}, u32[]{:S(2)}, u32[]{:S(2)}) async-start(f32[8,1,128]{2,1,0:T(1,128)} %reshape.143), calls=%async_computation.2 | async-start | bytes 8192 | tf_op jit(solution)/shard_map/all_to_all | solution.py:42
  217.4 6.3 %collective-permute-start.24 = (f32[5,8,64]{2,1,0:T(8,128)S(1)}, f32[5,8,64]{2,1,0:T(8,128)S(1)}, u32[]{:S(2)}, u32[]{:S(2)}) collective-permute-start(f32[5,8,64]{2,1,0:T(8,128)S(1)} %get-tuple-element.67), channel_id=1, source_target_pairs={{0,128},{128,256},{256,384},{384,512},{512,640},{640,768},{768,896... | collective-permute-start | bytes 30728 | tf_op jit(solution)/shard_map/ppermute | solution.py:19
  227.4 6.5 %collective-permute-start.26 = (f32[16,5,64]{2,1,0:T(8,128)S(1)}, f32[16,5,64]{2,1,0:T(8,128)S(1)}, u32[]{:S(2)}, u32[]{:S(2)}) collective-permute-start(f32[16,5,64]{2,1,0:T(8,128)S(1)} %get-tuple-element.61), channel_id=1, source_target_pairs={{0,8},{8,16},{16,24},{24,32},{32,40},{40,48},{48,56},{56,64},{64,7... | collective-permute-start | bytes 61448 | tf_op jit(solution)/shard_map/ppermute | solution.py:19
  235.4 10.4 %collective-permute-start.28 = (f32[16,18,5]{2,1,0:T(8,128)S(1)}, f32[16,18,5]{2,1,0:T(8,128)S(1)}, u32[]{:S(2)}, u32[]{:S(2)}) collective-permute-start(f32[16,18,5]{2,1,0:T(8,128)S(1)} %get-tuple-element.36), channel_id=1, source_target_pairs={{0,1},{1,2},{2,3},{3,4},{4,5},{5,6},{6,7},{7,0},{8,9},{9,10},{10,1... | collective-permute-start | bytes 17288 | tf_op jit(solution)/shard_map/ppermute | solution.py:19
  243.2 6.3 %collective-permute-start.29 = (f32[16,18,5]{2,1,0:T(8,128)S(1)}, f32[16,18,5]{2,1,0:T(8,128)S(1)}, u32[]{:S(2)}, u32[]{:S(2)}) collective-permute-start(f32[16,18,5]{2,1,0:T(8,128)S(1)} %get-tuple-element.37), channel_id=1, source_target_pairs={{1,0},{2,1},{3,2},{4,3},{5,4},{6,5},{7,6},{0,7},{9,8},{10,9},{11,1... | collective-permute-start | bytes 17288 | tf_op jit(solution)/shard_map/ppermute | solution.py:21
  253.5 6.0 %collective-permute-start.31 = (f32[5,16,128]{2,1,0:T(8,128)S(1)}, f32[5,16,128]{2,1,0:T(8,128)S(1)}, u32[]{:S(2)}, u32[]{:S(2)}) collective-permute-start(f32[5,16,128]{2,1,0:T(8,128)S(1)} %get-tuple-element.51), channel_id=1, source_target_pairs={{128,0},{256,128},{384,256},{512,384},{640,512},{768,640},{896,768... | collective-permute-start | bytes 122888 | tf_op jit(solution)/shard_map/ppermute | solution.py:21
  259.6 7.2 %collective-permute-start.32 = (f32[22,5,128]{2,0,1:T(8,128)S(1)}, f32[22,5,128]{2,0,1:T(8,128)S(1)}, u32[]{:S(2)}, u32[]{:S(2)}) collective-permute-start(f32[22,5,128]{2,0,1:T(8,128)S(1)} %copy.166), channel_id=1, source_target_pairs={{0,8},{8,16},{16,24},{24,32},{32,40},{40,48},{48,56},{56,64},{64,7... | collective-permute-start | bytes 168968 | tf_op jit(solution)/shard_map/ppermute | solution.py:19
  261.5 6.5 %collective-permute-start.33 = (f32[22,5,128]{2,0,1:T(8,128)S(1)}, f32[22,5,128]{2,0,1:T(8,128)S(1)}, u32[]{:S(2)}, u32[]{:S(2)}) collective-permute-start(f32[22,5,128]{2,0,1:T(8,128)S(1)} %copy.167), channel_id=1, source_target_pairs={{8,0},{16,8},{24,16},{32,24},{40,32},{48,40},{56,48},{64,56},{72,6... | collective-permute-start | bytes 168968 | tf_op jit(solution)/shard_map/ppermute | solution.py:21
  268.1 5.9 %collective-permute-start.34 = (f32[22,26,5]{2,0,1:T(8,128)S(1)}, f32[22,26,5]{2,0,1:T(8,128)S(1)}, u32[]{:S(2)}, u32[]{:S(2)}) collective-permute-start(f32[22,26,5]{2,0,1:T(8,128)S(1)} %get-tuple-element.30), channel_id=1, source_target_pairs={{0,1},{1,2},{2,3},{3,4},{4,5},{5,6},{6,7},{7,0},{8,9},{9,10},{10,1... | collective-permute-start | bytes 34328 | tf_op jit(solution)/shard_map/ppermute | solution.py:19
  270.2 7.6 %collective-permute-start.35 = (f32[22,26,5]{2,0,1:T(8,128)S(1)}, f32[22,26,5]{2,0,1:T(8,128)S(1)}, u32[]{:S(2)}, u32[]{:S(2)}) collective-permute-start(f32[22,26,5]{2,0,1:T(8,128)S(1)} %get-tuple-element.31), channel_id=1, source_target_pairs={{1,0},{2,1},{3,2},{4,3},{5,4},{6,5},{7,6},{0,7},{9,8},{10,9},{11,1... | collective-permute-start | bytes 34328 | tf_op jit(solution)/shard_map/ppermute | solution.py:21
  (7 other events, 34.8 us)
where the time goes:
time: 285 us; the launch traced here: 284 us
  starting transfers between devices  110 us (39%)
  blocking collectives  78.3 us (27%)
  waiting for transfers between devices  55 us (19%)
  other arithmetic  21.1 us (7%)
  local copies, waits for them, and re-layouts  15.4 us (5%)
    psum x4, blocking collectives, over_axes(): array = lax.psum(array, axis)  71.3 us
    ppermute x18, starting transfers between devices, with_halo(): lax.ppermute(tail, axis, [(i, (i + 1) % count) for i in range(count)])  60.2 us
    ppermute x18, starting transfers between devices, with_halo(): lax.ppermute(head, axis, [((i + 1) % count, i) for i in range(count)])  41.3 us
    ppermute x18, waiting for transfers between devices, with_halo(): lax.ppermute(head, axis, [((i + 1) % count, i) for i in range(count)])  32.5 us
    all_to_all x2, waiting for transfers between devices, sent_to_all(): lax.all_to_all(jnp.broadcast_to(array[None], (peers, *array.shape)), axis...  15.3 us
    all_to_all x2, starting transfers between devices, sent_to_all(): lax.all_to_all(jnp.broadcast_to(array[None], (peers, *array.shape)), axis...  8.79 us
    reshape x1, local copies, waits for them, and re-layouts, body(): left.reshape(cx // 2, 2, cy // 2, 2, cz // 2, 2).sum(axis=(1, 3, 5)) * 0.5  7.68 us
    ppermute x18, waiting for transfers between devices, with_halo(): lax.ppermute(tail, axis, [(i, (i + 1) % count) for i in range(count)])  7.19 us
  transfers between devices with their start and end apart: 38, of which 17 were waited for; matrix products, arithmetic and copies ran while one was open for 7% of the time, Pallas kernels for 0%

commit v1 on v0

v1 whole, which is shorter than its diff:
```python
import functools

import jax
import jax.numpy as jnp
import numpy as np
from jax import lax
from jax.experimental import pallas as pl
from jax.experimental.pallas import tpu as pltpu
from jax.sharding import PartitionSpec as P

GX, GY, GZ = 8, 16, 8
BX, BY, BZ = 6, 8, 64
LANES = 128
SHIFT = 4.25
SIXTH = 1.0 / 6.0
HI = lax.Precision.HIGHEST
F32 = jnp.float32


def roll(x, shift, axis):
    return pltpu.roll(x, shift % x.shape[axis], axis)


def iota(shape, dim):
    return lax.broadcasted_iota(jnp.int32, shape, dim)


def dot(a, b):
    return lax.dot_general(a, b, (((1,), (0,)), ((), ())), precision=HI, preferred_element_type=F32)


def dot_nt(a, b):
    return lax.dot_general(a, b, (((1,), (1,)), ((), ())), precision=HI, preferred_element_type=F32)


def plus(a, b):
    if a is None:
        return b
    return a if b is None else a + b


def basis_of(count):
    rows = np.arange(count)[:, None]
    cols = np.arange(count)[None, :]
    freq = (cols + 1) // 2
    angle = 2.0 * np.pi * freq * rows / count
    table = np.where(cols % 2 == 1, np.cos(angle), np.sin(angle)) * np.sqrt(2.0 / count)
    table = np.where(2 * freq == count, np.cos(angle) / np.sqrt(count), table)
    table = np.where(cols == 0, 1.0 / np.sqrt(count), table)
    modes = (np.arange(count) + 1) // 2
    return table, 2.0 - 2.0 * np.cos(2.0 * np.pi * modes / count)


def coarse_tables():
    qx, lx = basis_of(GX)
    qy, ly = basis_of(GY)
    qz, lz = basis_of(GZ)
    qyz = np.einsum("jb,kc->jkbc", qy, qz).reshape(LANES, LANES)
    lam = BY * BZ * lx[:, None, None] + BX * BZ * ly[None, :, None] + BX * BY * lz[None, None, :]
    lam[0, 0, 0] = 1.0
    inverse = -1.0 / lam
    inverse[0, 0, 0] = 0.0
    inverse = inverse.reshape(GX, LANES)
    around = lambda n: np.arange(-1, n + 1) % n
    tx = np.repeat(qx[around(GX)][:, :, None], LANES, axis=2)
    ty = np.repeat(qy[around(GY)], GZ, axis=1)
    tz = np.tile(qz[around(GZ)], (1, GY))
    return [np.asarray(t, np.float32) for t in (qyz, inverse, tx, ty, tz)]


def parting():
    table = np.zeros((LANES, LANES), np.float32)
    for z in range(LANES):
        table[z, (z % 2) * 64 + z // 2] = 1.0
    return table


def unit_response():
    red = black = 0.0
    for _ in range(2):
        red = (6 * black - 1) / 6
        black = (6 * red - 1) / 6
    level = 0.5 * (4 * (1 - (6 * black - 6 * red)) + 4 * (1 - (6 * red - 6 * black)))
    one = [0.0, 0.0]
    for _ in range(4):
        one[0] = (6 * one[1] - level) / 6
        one[1] = (6 * one[0] - level) / 6
    v = [[own + group for own in (red, black)] for group in one]
    for _ in range(2):
        for own in (0, 1):
            near = 3 * (v[0][1 - own] + v[1][1 - own])
            v[0][own] = v[1][own] = (near - 1) / 6
    return v


CELLS = [(a, b, c) for a in (0, 1) for b in (0, 1) for c in (0, 1)]


def spread(depth, a, count):
    low = -((depth + a) // 2)
    high = (2 * count + depth - 1 - a) // 2
    return range(low, high + 1)


def beside(field, cell, x):
    a, b, c = cell
    total = plus(field.get(((1 - a, b, c), x)), field.get(((1 - a, b, c), x + (1 if a else -1))))
    other = field.get(((a, 1 - b, c), x))
    if other is not None:
        total = plus(total, other + roll(other, -1 if b else 1, 0))
    other = field.get(((a, b, 1 - c), x))
    if other is not None:
        total = plus(total, other + roll(other, -1 if c else 1, 1))
    return total


class Kept:
    def __init__(self, ref):
        self.ref = ref
        self.slots = {}

    def get(self, key):
        slot = self.slots.get(key)
        return None if slot is None else self.ref[slot]

    def put(self, key, value):
        slot = self.slots.setdefault(key, len(self.slots))
        self.ref[slot] = value


def fine_half(field, source, colour, depth):
    for cell in CELLS:
        if sum(cell) % 2 != colour:
            continue
        for x in spread(depth, cell[0], BX):
            near = beside(field, cell, x)
            s = source.get((cell, x))
            if near is None and s is None:
                continue
            value = near if s is None else (-s if near is None else near - s)
            field.put((cell, x), value * SIXTH)


def coarsened(field, source, x):
    total = None
    for cell in CELLS:
        if sum(cell) % 2 != 0:
            continue
        near = beside(field, cell, x)
        s = source.get((cell, x))
        own = field.get((cell, x))
        part = None if own is None else 6.0 * own
        part = plus(part, s)
        if near is not None:
            part = -near if part is None else part - near
        total = plus(total, part)
    return None if total is None else total * 0.5


def red_of(shape, x):
    return (iota(shape, 0) + iota(shape, 1) + (x % 2)) % 2 == 0


def beside_one(field, x):
    total = plus(field.get(x - 1), field.get(x + 1))
    own = field.get(x)
    if own is not None:
        total = plus(total, roll(own, 1, 0) + roll(own, -1, 0))
        total = total + (roll(own, 1, 1) + roll(own, -1, 1))
    return total


def one_half(field, source, colour, low, high, masks):
    for x in range(low, high):
        near = beside_one(field, x)
        s = source.get(x)
        own = field.get(x)
        if near is None and s is None:
            continue
        value = near if s is None else (-s if near is None else near - s)
        value = value * SIXTH
        red = masks[x % 2]
        rest = jnp.zeros_like(value) if own is None else own
        field.put(x, jnp.where(red, value, rest) if colour == 0 else jnp.where(red, rest, value))


def part_kernel(density, potential, table, out, dscratch, pscratch):
    t = table[...]
    dscratch[...] = dot(density[...].reshape(192, LANES) - SHIFT, t)
    pscratch[...] = dot(potential[...].reshape(192, LANES), t)
    low = iota((BY, LANES), 1) < 64
    for x in range(BX):
        for a in (0, 1):
            rows = []
            for b in (0, 1):
                at = pl.ds((2 * x + a) * 16 + b, BY, stride=2)
                out[2 * a + b, x] = dscratch[at, :]
                rows.append(pscratch[at, :])
            out[4 + a, x] = jnp.where(low, rows[1 - a], rows[a])


def source_slot(cell):
    return 2 * cell[0] + cell[1]


def halves(cell):
    return 4 + cell[0], cell[2]


def share_kernel(pairs, out, fref, sref, eref, lref, stack):
    own = iota((BY, LANES), 1) < 64
    source, field = Kept(sref), Kept(fref)
    nothing = jnp.zeros((BY, LANES), F32)
    mass = None
    for cell in CELLS:
        for x in range(BX):
            value = pairs[source_slot(cell), x]
            mass = plus(mass, value) if cell[2] == 0 else mass
            if cell[2]:
                value = roll(value, 64, 1)
            source.put((cell, x), jnp.concatenate([jnp.where(own, value, 0.0), nothing], 0))
            if sum(cell) % 2:
                array, half = halves(cell)
                value = pairs[array, x]
                if half:
                    value = roll(value, 64, 1)
                field.put((cell, x), jnp.concatenate([jnp.where(own, value, 0.0), nothing], 0))
    for step in range(4):
        fine_half(field, source, step % 2, step + 1)
    level, error = Kept(lref), Kept(eref)
    near = iota((BY, LANES), 0) < 4
    for x in range(-3, BX + 3):
        value = coarsened(field, source, x)
        top, rim = value[:BY], value[BY:]
        level.put(x, jnp.concatenate([top, jnp.where(near, rim, 0.0), jnp.where(near, 0.0, rim)], 0))
    masks = [red_of((24, LANES), x) for x in (0, 1)]
    for step in range(4):
        one_half(error, level, step % 2, -3 - step, BX + 3 + step, masks)
    for i, (low, high) in enumerate(((-7, -6), (-6, 0), (0, 6), (6, 12), (12, 13))):
        total = None
        for x in range(low, high):
            part = plus(level.get(x), None if error.get(x) is None else 6.0 * error.get(x))
            around = beside_one(error, x)
            part = -around if part is None else part - around
            total = plus(total, jnp.where(masks[x % 2], part, 0.0))
        for j in range(3):
            stack[pl.ds((3 * i + j) * 8, 8), :] = total[8 * j : 8 * j + 8]
    stack[pl.ds(120, 8), :] = mass
    rows, cols = iota((LANES, LANES), 0), iota((LANES, LANES), 1)
    summed = dot(jnp.where(cols // 8 == rows, 1.0, 0.0), stack[...])
    row, lane = iota((8, LANES), 0), iota((8, LANES), 1)
    pick = ((row == 0) & (lane < 64)) | ((row == 1) & (lane >= 64) & (lane < 96))
    pick = pick | ((row == 2) & (lane >= 96))
    summed = jnp.where((rows == 15) & (cols < 64), summed + roll(summed, 64, 1), summed)
    summed = jnp.where((rows == 15) & (cols >= 64), 0.0, summed)
    sent = dot_nt(jnp.where(pick, 1.0, 0.0), summed)
    for peer in range(GZ):
        out[peer] = sent


def along_z_kernel(got, out):
    total = got[:, 0, :] + roll(got[:, 1, :], 1, 0) + roll(got[:, 2, :], -1, 0)
    rows, cols = iota((LANES, LANES), 0), iota((LANES, LANES), 1)
    tiled = dot(total, jnp.where((rows < 16) & (cols % 16 == rows), 1.0, 0.0))
    row, lane = iota((GZ, LANES), 0), iota((GZ, LANES), 1)
    flat = jnp.sum(jnp.where(lane // 16 == row, tiled, 0.0), axis=0, keepdims=True)
    for peer in range(GY):
        out[peer] = flat


def along_y_kernel(got, out):
    values = got[:, 0, :]
    slot = iota((GY, LANES), 1) % 16
    total = jnp.where((slot % 3 == 0) | (slot == 15), values, 0.0)
    total = total + roll(jnp.where((slot % 3 == 1), values, 0.0), 1, 0)
    total = total + roll(jnp.where((slot % 3 == 2), values, 0.0), -1, 0)
    rows, cols = iota((LANES, LANES), 0), iota((LANES, LANES), 1)
    row, lane = iota((GY, LANES), 0), iota((GY, LANES), 1)
    place = iota((8, LANES), 0)
    sent = jnp.zeros((8, LANES), F32)
    for r in range(6):
        take = (cols % 8 == rows // 16) & ((rows % 16) // 3 == r)
        tiled = dot(total, jnp.where(take, 1.0, 0.0))
        flat = jnp.sum(jnp.where(lane // 8 == row, tiled, 0.0), axis=0, keepdims=True)
        sent = jnp.where(place == r, flat, sent)
    for peer in range(GX):
        out[peer] = sent


def wide_x(own, left, right, array, x):
    if x < 0:
        return left[array, x + BX]
    if x >= BX:
        return right[array, x - BX]
    return own[array, x]


def rim_y_kernel(own, left, right, low, high):
    for array in range(6):
        for x in range(-BX, 2 * BX):
            value = wide_x(own, left, right, array, x)
            low[array, x + BX] = value[:4]
            high[array, x + BX] = value[4:]


def tall(own, left, right, below, above, array, x):
    value = wide_x(own, left, right, array, x)
    rim = jnp.concatenate([above[array, x + BX], below[array, x + BX]], 0)
    return jnp.concatenate([value, rim], 0)


def groups():
    made = []
    for x in range(-BX, 2 * BX):
        made.append((x + BX, [(i, x) for i in range(4)]))
    for x in range(-BX, 3):
        made.append((18 + x + BX, [(4, x), (5, x), (4, x + 9), (5, x + 9)]))
    return made


def rim_z_kernel(own, left, right, below, above, low, high):
    lane = iota((16, LANES), 1)
    for slot, members in groups():
        lows = highs = None
        for i, (array, x) in enumerate(members):
            value = tall(own, left, right, below, above, array, x)
            down = roll(value, 16 * i, 1)
            up = roll(value, 16 * (i + 1), 1)
            lows = down if lows is None else jnp.where((lane % 64) // 16 == i, down, lows)
            highs = up if highs is None else jnp.where((lane % 64) // 16 == i, up, highs)
        low[slot] = lows
        high[slot] = highs


def fine_kernel(own, left, right, below, above, before, after, level, fine, kept, fref, sref):
    source, field = Kept(sref), Kept(fref)
    lane = iota((16, LANES), 1)
    home = {}
    for slot, members in groups():
        for i, key in enumerate(members):
            home[key] = (slot, i)
    for array in range(6):
        for x in range(-BX, 2 * BX):
            value = tall(own, left, right, below, above, array, x)
            slot, i = home[(array, x)]
            up, down = after[slot], before[slot]
            for c in (0, 1):
                mine = roll(value, 64, 1) if c else value
                right_rim = roll(up, 64 - 16 * i - 64 * c, 1)
                left_rim = roll(down, 48 - 16 * i + 64 * c, 1)
                full = jnp.where(lane < 64, mine, 0.0)
                full = jnp.where((lane >= 64) & (lane < 80), right_rim, full)
                full = jnp.where(lane >= 112, left_rim, full)
                if array < 4:
                    source.put(((array // 2, array % 2, c), x), full)
                else:
                    a = array - 4
                    b = (1 + a + c) % 2
                    field.put(((a, b, c), x), full)
    for step, depth in enumerate((10, 9, 8, 7)):
        fine_half(field, source, step % 2, depth)
    for x in range(-3, BX + 3):
        level[x + 3] = coarsened(field, source, x)
    for n, cell in enumerate(CELLS):
        for x in range(-2, BX + 2):
            fine[n, x + 2] = field.get((cell, x))
            kept[n, x + 2] = source.get((cell, x))


def level_y_kernel(own, below, above, wide, low, high):
    first = iota((8, LANES), 0) == 0
    last = iota((8, LANES), 0) == 7
    for x in range(12):
        mine, down, up = own[x], below[x], above[x]
        tail = jnp.where(first, up[8:16], 0.0)
        lead = jnp.where(last, down[8:16], 0.0)
        value = jnp.concatenate([mine[:8], up[:8], tail + lead, down[:8]], 0)
        wide[x] = value
        if x >= 3:
            low[x - 3] = value
        if x < 9:
            high[x] = value


def mid_kernel(wide, left, right, level, mid, eref):
    for x in range(-9, BX + 9):
        if x < 0:
            value = left[x + 9]
        elif x >= BX:
            value = right[x - BX]
        else:
            value = wide[x + 3]
        level[x + 9] = value
    source = Given(level, 9, 24)
    error = Kept(eref)
    masks = [red_of((32, LANES), x) for x in (0, 1)]
    for step, depth in enumerate((9, 8, 7, 6)):
        one_half(error, source, step % 2, -depth, BX + depth, masks)
    for x in range(-6, BX + 6):
        mid[x + 6] = error.get(x)


class Given:
    def __init__(self, ref, start, count):
        self.ref, self.start, self.count = ref, start, count

    def get(self, x):
        return self.ref[x + self.start] if 0 <= x + self.start < self.count else None

    def put(self, x, value):
        self.ref[x + self.start] = value


def last_kernel(got, qyz, inverse, tx, ty, tz, level, mid, fine, kept, table, out, eref, fref, oref, *, axes):
    blocks = None
    for r in range(5):
        blocks = plus(blocks, roll(got[:, r, :], r - 2, 0))
    mean = jnp.sum(got[:, 5, :], keepdims=True) * (1.0 / (GX * GY * GZ * 8 * BX * BY * BZ))
    blocks = blocks - jnp.sum(blocks, keepdims=True) * (1.0 / (GX * GY * GZ))
    half = dot(blocks, qyz[...])
    modes = None
    for x in range(GX):
        modes = plus(modes, half[x : x + 1, :] * tx[x + 1])
    modes = modes * inverse[...]
    ix, iy, iz = axes
    own_lane = iota((LANES, LANES), 0)
    zrow = lambda d: tz[pl.ds(iz + 1 + d, 1), :]
    spread_z = jnp.where(own_lane < 64, zrow(0), jnp.where(own_lane < 96, zrow(1), zrow(-1)))
    place = iota((16, LANES), 0)
    stacked = jnp.zeros((16, LANES), F32)
    for dx in (-1, 0, 1):
        line = jnp.sum(modes * tx[ix + 1 + dx], axis=0, keepdims=True)
        for dy in (-1, 0, 1):
            stacked = jnp.where(place == 3 * (dx + 1) + dy + 1, line * ty[pl.ds(iy + 1 + dy, 1), :], stacked)
    coarse = dot_nt(stacked, spread_z)
    row = iota((32, LANES), 0)
    error = Given(eref, 6, 18)
    for dx in (-1, 0, 1):
        r = 3 * (dx + 1)
        add = jnp.where(row < 8, coarse[r + 1 : r + 2], jnp.where(row < 16, coarse[r + 2 : r + 3], coarse[r : r + 1]))
        for x in range(BX * dx, BX * dx + BX):
            error.put(x, mid[x + 6] + add)
    source = Given(level, 9, 24)
    masks = [red_of((32, LANES), x) for x in (0, 1)]
    for step, depth in enumerate((5, 4, 3, 2)):
        one_half(error, source, step % 2, -depth, BX + depth, masks)
    near = iota((8, LANES), 0) < 4
    field, terms = Kept(fref), Sources(kept)
    for x in range(-2, BX + 2):
        e = error.get(x)
        e = jnp.concatenate([e[:8], jnp.where(near, e[8:16], e[24:])], 0)
        for n, cell in enumerate(CELLS):
            field.put((cell, x), fine[n, x + 2] + e)
    for step, depth in enumerate((3, 2, 1, 0)):
        fine_half(field, terms, step % 2, depth)
    v = unit_response()
    shape = (8, LANES)
    lane = iota(shape, 1)
    for x in range(BX):
        group = (iota(shape, 0) + lane + x) % 2 == 0
        for a in (0, 1):
            for b in (0, 1):
                pair = []
                for c in (0, 1):
                    own = (a + b + c) % 2
                    value = field.get(((a, b, c), x))[:8]
                    pair.append(value - mean * jnp.where(group, v[0][own], v[1][own]))
                both = jnp.where(lane < 64, pair[0], roll(pair[1], 64, 1))
                oref[pl.ds((2 * x + a) * 16 + b, 8, stride=2), :] = both
    out[...] = dot_nt(oref[...], table[...]).reshape(12, 16, LANES)


class Sources:
    def __init__(self, ref):
        self.ref = ref

    def get(self, key):
        cell, x = key
        return self.ref[CELLS.index(cell), x + 2] if -2 <= x < BX + 2 else None


def run(kernel, shapes, args, scratch=(), flops=1000000, **static):
    space = pl.BlockSpec(memory_space=pltpu.VMEM)
    moved = 4 * sum(int(np.prod(s)) for s in shapes)
    return pl.pallas_call(
        kernel,
        out_shape=[jax.ShapeDtypeStruct(s, F32) for s in shapes],
        in_specs=[space] * len(args),
        out_specs=[space] * len(shapes),
        scratch_shapes=[pltpu.VMEM(s, F32) for s in scratch],
        cost_estimate=pl.CostEstimate(flops=flops, bytes_accessed=moved, transcendentals=0),
        name=kernel.__name__,
    )(*args)


def place_kernel(*refs):
    axes = (lax.axis_index("gx"), lax.axis_index("gy"), lax.axis_index("gz"))
    last_kernel(*refs, axes=axes)


def moved(array, axis, step):
    count = lax.axis_size(axis)
    return lax.ppermute(array, axis, [(i, (i + step) % count) for i in range(count)])


def everyone(array, axis):
    return lax.all_to_all(array, axis, 0, 0, tiled=True)


def body(density, potential):
    qyz, inverse, tx, ty, tz = (jnp.asarray(t) for t in coarse_tables())
    table = jnp.asarray(parting())
    (own,) = run(part_kernel, [(6, 6, 8, LANES)], [density, potential, table], [(192, LANES)] * 2)
    left, right = moved(own, "gx", 1), moved(own, "gx", -1)
    (shares,) = run(
        share_kernel,
        [(GZ, 8, LANES)],
        [own],
        [(96, 16, LANES), (48, 16, LANES), (20, 24, LANES), (12, 24, LANES), (LANES, LANES)],
    )
    (line,) = run(along_z_kernel, [(GY, 1, LANES)], [everyone(shares, "gz")])
    (plane,) = run(along_y_kernel, [(GX, 8, LANES)], [everyone(line, "gy")])
    blocks = everyone(plane, "gx")
    low, high = run(rim_y_kernel, [(6, 18, 4, LANES)] * 2, [own, left, right])
    below, above = moved(high, "gy", 1), moved(low, "gy", -1)
    low, high = run(rim_z_kernel, [(27, 16, LANES)] * 2, [own, left, right, below, above])
    before, after = moved(high, "gz", 1), moved(low, "gz", -1)
    level, fine, kept = run(
        fine_kernel,
        [(12, 16, LANES), (8, 10, 16, LANES), (8, 10, 16, LANES)],
        [own, left, right, below, above, before, after],
        [(144, 16, LANES), (144, 16, LANES)],
    )
    below, above = moved(level, "gy", 1), moved(level, "gy", -1)
    wide, low, high = run(
        level_y_kernel, [(12, 32, LANES), (9, 32, LANES), (9, 32, LANES)], [level, below, above]
    )
    left, right = moved(high, "gx", 1), moved(low, "gx", -1)
    level, mid = run(
        mid_kernel, [(24, 32, LANES), (18, 32, LANES)], [wide, left, right], [(24, 32, LANES)]
    )
    (out,) = run(
        place_kernel,
        [(12, 16, LANES)],
        [blocks, qyz, inverse, tx, ty, tz, level, mid, fine, kept, table],
        [(18, 32, LANES), (80, 16, LANES), (192, LANES)],
    )
    return out


def solution(mesh):
    spec = P("gx", "gy", "gz")
    return jax.shard_map(body, mesh=mesh, in_specs=(spec, spec), out_specs=spec, check_vma=False)
```

time: 285 us -> 129 us (0.45)
  the two profiles are of different devices: /device:TPU:63 before, /device:TPU:2 now
where the time goes in v1:
time: 129 us
  starting transfers between devices  50.4 us (39%)
  blocking collectives  28.6 us (22%)
  Pallas kernels  25 us (19%)
  waiting for transfers between devices  19.7 us (15%)
  local copies, waits for them, and re-layouts  4.71 us (4%)
    ppermute x10, starting transfers between devices, moved(): lax.ppermute(array, axis, [(i, (i + step) % count) for i in range(count)])  44 us
    all_to_all x2, blocking collectives, everyone(): return lax.all_to_all(array, axis, 0, 0, tiled=True)  28.6 us
    pallas_call x10, Pallas kernels, run(): pl.pallas_call(kernel, out_shape=[jax.ShapeDtypeStruct(s, F32) for s in s...  25 us
    ppermute x10, waiting for transfers between devices, moved(): lax.ppermute(array, axis, [(i, (i + step) % count) for i in range(count)])  14.8 us
    all_to_all x1, starting transfers between devices, everyone(): return lax.all_to_all(array, axis, 0, 0, tiled=True)  6.48 us
    all_to_all x1, waiting for transfers between devices, everyone(): return lax.all_to_all(array, axis, 0, 0, tiled=True)  4.9 us
    unnamed x22, local copies, waits for them, and re-layouts  4.71 us
  transfers between devices with their start and end apart: 11, of which 8 were waited for; matrix products, arithmetic and copies ran while one was open for 0% of the time, Pallas kernels for 7%

profile of v1, /device:TPU:2, one launch (start us, length us, event | category | flops | bytes accessed | tf_op | source)
XLA Modules:
  0.0 128.5 jit_solution(8253696949504170146)
XLA Ops:
  0.0 1.9 %part_kernel.1.pairs.own = f32[6,6,8,128]{3,2,1,0:T(8,128)} custom-call(f32[12,16,128]{2,1,0:T(8,128)} %density.1, f32[12,16,128]{2,1,0:T(8,128)} %potential.1, f32[128,128]{1,0:T(8,128)} %constant.17.clone.table.refs_10_), custom_call_target="tpu_custom_call" | custom-call | flops 1000000 | bytes 147456 | tf_op jit(solution)/shard_map/part_kernel/pallas_call | solution.py:485
  1.9 3.5 %collective-permute-start = (f32[6,6,8,128]{3,2,1,0:T(8,128)}, f32[6,6,8,128]{3,2,1,0:T(8,128)S(1)}, u32[]{:S(2)}, u32[]{:S(2)}) collective-permute-start(f32[6,6,8,128]{3,2,1,0:T(8,128)} %part_kernel.1.pairs.own), channel_id=1, source_target_pairs={{0,128},{128,256},{256,384},{384,512},{512,640},{640,768},{768,896... | collective-permute-start | bytes 442376 | tf_op jit(solution)/shard_map/ppermute | solution.py:503
  5.4 3.8 %collective-permute-start.1 = (f32[6,6,8,128]{3,2,1,0:T(8,128)}, f32[6,6,8,128]{3,2,1,0:T(8,128)S(1)}, u32[]{:S(2)}, u32[]{:S(2)}) collective-permute-start(f32[6,6,8,128]{3,2,1,0:T(8,128)} %part_kernel.1.pairs.own), channel_id=1, source_target_pairs={{0,896},{128,0},{256,128},{384,256},{512,384},{640,512},{768,640},... | collective-permute-start | bytes 442376 | tf_op jit(solution)/shard_map/ppermute | solution.py:503
  9.2 2.1 %collective-permute-done.left = f32[6,6,8,128]{3,2,1,0:T(8,128)S(1)} collective-permute-done((f32[6,6,8,128]{3,2,1,0:T(8,128)}, f32[6,6,8,128]{3,2,1,0:T(8,128)S(1)}, u32[]{:S(2)}, u32[]{:S(2)}) %collective-permute-start) | collective-permute-done | bytes 147488 | tf_op jit(solution)/shard_map/ppermute | solution.py:503
  11.3 1.5 %collective-permute-done.1.right = f32[6,6,8,128]{3,2,1,0:T(8,128)S(1)} collective-permute-done((f32[6,6,8,128]{3,2,1,0:T(8,128)}, f32[6,6,8,128]{3,2,1,0:T(8,128)S(1)}, u32[]{:S(2)}, u32[]{:S(2)}) %collective-permute-start.1) | collective-permute-done | bytes 147488 | tf_op jit(solution)/shard_map/ppermute | solution.py:503
  13.5 1.9 %rim_y_kernel.1 = (f32[6,18,4,128]{3,2,1,0:T(4,128)}, f32[6,18,4,128]{3,2,1,0:T(4,128)}) custom-call(f32[6,6,8,128]{3,2,1,0:T(8,128)} %part_kernel.1.pairs.own, f32[6,6,8,128]{3,2,1,0:T(8,128)} %copy-done, f32[6,6,8,128]{3,2,1,0:T(8,128)} %copy-done.1), custom_call_target="tpu_custom_call" | custom-call | flops 1000000 | bytes 442368 | tf_op jit(solution)/shard_map/rim_y_kernel/pallas_call | solution.py:485
  15.4 4.3 %collective-permute-start.2 = (f32[6,18,4,128]{3,2,1,0:T(4,128)}, f32[6,18,4,128]{3,2,1,0:T(4,128)S(1)}, u32[]{:S(2)}, u32[]{:S(2)}) collective-permute-start(f32[6,18,4,128]{3,2,1,0:T(4,128)} %get-tuple-element.17), channel_id=1, source_target_pairs={{0,8},{8,16},{16,24},{24,32},{32,40},{40,48},{48,56},{56,64},{64,7... | collective-permute-start | bytes 663560 | tf_op jit(solution)/shard_map/ppermute | solution.py:503
  19.7 15.9 %collective-permute-start.3 = (f32[6,18,4,128]{3,2,1,0:T(4,128)}, f32[6,18,4,128]{3,2,1,0:T(4,128)S(1)}, u32[]{:S(2)}, u32[]{:S(2)}) collective-permute-start(f32[6,18,4,128]{3,2,1,0:T(4,128)} %get-tuple-element.18), channel_id=1, source_target_pairs={{0,120},{8,0},{16,8},{24,16},{32,24},{40,32},{48,40},{56,48},{64,5... | collective-permute-start | bytes 663560 | tf_op jit(solution)/shard_map/ppermute | solution.py:503
  35.5 2.6 %collective-permute-done.2.below = f32[6,18,4,128]{3,2,1,0:T(4,128)S(1)} collective-permute-done((f32[6,18,4,128]{3,2,1,0:T(4,128)}, f32[6,18,4,128]{3,2,1,0:T(4,128)S(1)}, u32[]{:S(2)}, u32[]{:S(2)}) %collective-permute-start.2) | collective-permute-done | bytes 221216 | tf_op jit(solution)/shard_map/ppermute | solution.py:503
  38.2 1.3 collective-permute-done.3.above
  40.2 2.5 %rim_z_kernel.1 = (f32[27,16,128]{2,1,0:T(8,128)}, f32[27,16,128]{2,1,0:T(8,128)}) custom-call(f32[6,6,8,128]{3,2,1,0:T(8,128)} %part_kernel.1.pairs.own, f32[6,6,8,128]{3,2,1,0:T(8,128)} %copy-done, f32[6,6,8,128]{3,2,1,0:T(8,128)} %copy-done.1, f32[6,18,4,128]{3,2,1,0:T(4,128)} %copy-done.2, f32[6,18,4,128]{3,2,1,0:T(4,128)} %copy-done.3), custom_call_target="tpu_custom_call" | custom-call | flops 1000000 | bytes 442368 | tf_op jit(solution)/shard_map/rim_z_kernel/pallas_call | solution.py:485
  42.7 1.7 %collective-permute-start.5 = (f32[27,16,128]{2,1,0:T(8,128)}, f32[27,16,128]{2,1,0:T(8,128)S(1)}, u32[]{:S(2)}, u32[]{:S(2)}) collective-permute-start(f32[27,16,128]{2,1,0:T(8,128)} %get-tuple-element.20), channel_id=1, source_target_pairs={{0,7},{1,0},{2,1},{3,2},{4,3},{5,4},{6,5},{7,6},{8,15},{9,8},{10,9... | collective-permute-start | bytes 663560 | tf_op jit(solution)/shard_map/ppermute | solution.py:503
  44.4 3.8 %collective-permute-done.4.before = f32[27,16,128]{2,1,0:T(8,128)S(1)} collective-permute-done((f32[27,16,128]{2,1,0:T(8,128)}, f32[27,16,128]{2,1,0:T(8,128)S(1)}, u32[]{:S(2)}, u32[]{:S(2)}) %collective-permute-start.4) | collective-permute-done | bytes 221216 | tf_op jit(solution)/shard_map/ppermute | solution.py:503
  48.2 0.7 copy-done.4
  48.9 0.7 copy-done.5
  49.6 4.0 %fine_kernel.1 = (f32[12,16,128]{2,1,0:T(8,128)}, f32[8,10,16,128]{3,2,1,0:T(8,128)}, f32[8,10,16,128]{3,2,1,0:T(8,128)}) custom-call(f32[6,6,8,128]{3,2,1,0:T(8,128)} %part_kernel.1.pairs.own, f32[6,6,8,128]{3,2,1,0:T(8,128)} %copy-done, f32[6,6,8,128]{3,2,1,0:T(8,128)} %copy-done.1, f32[6,18,4,128]{3,2,1,0:T(4,128)} %copy-done.2, ...), custom_call_target="tpu_custom_call" | custom-call | flops 1000000 | bytes 1409024 | tf_op jit(solution)/shard_map/fine_kernel/pallas_call | solution.py:485
  53.6 1.9 %collective-permute-start.6 = (f32[12,16,128]{2,1,0:T(8,128)}, f32[12,16,128]{2,1,0:T(8,128)S(1)}, u32[]{:S(2)}, u32[]{:S(2)}) collective-permute-start(f32[12,16,128]{2,1,0:T(8,128)} %get-tuple-element.21.own), channel_id=1, source_target_pairs={{0,8},{8,16},{16,24},{24,32},{32,40},{40,48},{48,56},{56,64},{64,7... | collective-permute-start | bytes 294920 | tf_op jit(solution)/shard_map/ppermute | solution.py:503
  55.6 5.5 %collective-permute-start.7 = (f32[12,16,128]{2,1,0:T(8,128)}, f32[12,16,128]{2,1,0:T(8,128)S(1)}, u32[]{:S(2)}, u32[]{:S(2)}) collective-permute-start(f32[12,16,128]{2,1,0:T(8,128)} %get-tuple-element.21.own), channel_id=1, source_target_pairs={{0,120},{8,0},{16,8},{24,16},{32,24},{40,32},{48,40},{56,48},{64,5... | collective-permute-start | bytes 294920 | tf_op jit(solution)/shard_map/ppermute | solution.py:503
  61.1 1.7 %collective-permute-done.6.below = f32[12,16,128]{2,1,0:T(8,128)S(1)} collective-permute-done((f32[12,16,128]{2,1,0:T(8,128)}, f32[12,16,128]{2,1,0:T(8,128)S(1)}, u32[]{:S(2)}, u32[]{:S(2)}) %collective-permute-start.6) | collective-permute-done | bytes 98336 | tf_op jit(solution)/shard_map/ppermute | solution.py:503
  62.8 1.7 %collective-permute-done.7.above = f32[12,16,128]{2,1,0:T(8,128)S(1)} collective-permute-done((f32[12,16,128]{2,1,0:T(8,128)}, f32[12,16,128]{2,1,0:T(8,128)S(1)}, u32[]{:S(2)}, u32[]{:S(2)}) %collective-permute-start.7) | collective-permute-done | bytes 98336 | tf_op jit(solution)/shard_map/ppermute | solution.py:503
  65.1 1.8 %level_y_kernel.1 = (f32[12,32,128]{2,1,0:T(8,128)}, f32[9,32,128]{2,1,0:T(8,128)}, f32[9,32,128]{2,1,0:T(8,128)}) custom-call(f32[12,16,128]{2,1,0:T(8,128)} %get-tuple-element.21.own, f32[12,16,128]{2,1,0:T(8,128)} %copy-done.9, f32[12,16,128]{2,1,0:T(8,128)} %copy-done.10), custom_call_target="tpu_custom_call" | custom-call | flops 1000000 | bytes 491520 | tf_op jit(solution)/shard_map/level_y_kernel/pallas_call | solution.py:485
  66.9 3.4 %collective-permute-start.8 = (f32[9,32,128]{2,1,0:T(8,128)}, f32[9,32,128]{2,1,0:T(8,128)S(1)}, u32[]{:S(2)}, u32[]{:S(2)}) collective-permute-start(f32[9,32,128]{2,1,0:T(8,128)} %get-tuple-element.23), channel_id=1, source_target_pairs={{0,128},{128,256},{256,384},{384,512},{512,640},{640,768},{768,896... | collective-permute-start | bytes 442376 | tf_op jit(solution)/shard_map/ppermute | solution.py:503
  70.3 4.0 %collective-permute-start.9 = (f32[9,32,128]{2,1,0:T(8,128)}, f32[9,32,128]{2,1,0:T(8,128)S(1)}, u32[]{:S(2)}, u32[]{:S(2)}) collective-permute-start(f32[9,32,128]{2,1,0:T(8,128)} %get-tuple-element.24), channel_id=1, source_target_pairs={{0,896},{128,0},{256,128},{384,256},{512,384},{640,512},{768,640},... | collective-permute-start | bytes 442376 | tf_op jit(solution)/shard_map/ppermute | solution.py:503
  74.3 3.1 %share_kernel.1 = f32[8,8,128]{2,1,0:T(8,128)} custom-call(f32[6,6,8,128]{3,2,1,0:T(8,128)} %part_kernel.1.pairs.own), custom_call_target="tpu_custom_call" | custom-call | flops 1000000 | bytes 32768 | tf_op jit(solution)/shard_map/share_kernel/pallas_call | solution.py:485
  77.5 8.8 %all_to_all.15.got = f32[8,8,128]{2,1,0:T(8,128)} all-to-all(f32[8,8,128]{2,1,0:T(8,128)} %share_kernel.1), channel_id=1, replica_groups=mesh['gx'=8,'gy'=16,'gz'=8] {'gz'}, dimensions={0} | all-to-all | bytes 65536 | tf_op jit(solution)/shard_map/all_to_all | solution.py:507
  86.3 1.5 %along_z_kernel.1 = f32[16,1,128]{2,1,0:T(1,128)} custom-call(f32[8,8,128]{2,1,0:T(8,128)} %all_to_all.15.got), custom_call_target="tpu_custom_call" | custom-call | flops 1000000 | bytes 8192 | tf_op jit(solution)/shard_map/along_z_kernel/pallas_call | solution.py:485
  87.8 19.8 %all_to_all.16.got = f32[16,1,128]{2,1,0:T(1,128)} all-to-all(f32[16,1,128]{2,1,0:T(1,128)} %along_z_kernel.1), channel_id=1, replica_groups=mesh['gx'=8,'gy'=16,'gz'=8] {'gy'}, dimensions={0} | all-to-all | bytes 16384 | tf_op jit(solution)/shard_map/all_to_all | solution.py:507
  107.6 1.8 %along_y_kernel.1 = f32[8,8,128]{2,1,0:T(8,128)} custom-call(f32[16,1,128]{2,1,0:T(1,128)} %all_to_all.16.got), custom_call_target="tpu_custom_call" | custom-call | flops 1000000 | bytes 32768 | tf_op jit(solution)/shard_map/along_y_kernel/pallas_call | solution.py:485
  109.4 6.5 %all-to-all-start.2 = ((f32[8,8,128]{2,1,0:T(8,128)}), f32[8,8,128]{2,1,0:T(8,128)S(1)}, u32[]{:S(2)}, u32[]{:S(2)}) async-start(f32[8,8,128]{2,1,0:T(8,128)} %along_y_kernel.1), calls=%async_computation.2 | async-start | bytes 65536 | tf_op jit(solution)/shard_map/all_to_all | solution.py:507
  116.6 2.4 %mid_kernel.1 = (f32[24,32,128]{2,1,0:T(8,128)}, f32[18,32,128]{2,1,0:T(8,128)}) custom-call(f32[12,32,128]{2,1,0:T(8,128)} %get-tuple-element.22.wide, f32[9,32,128]{2,1,0:T(8,128)} %copy-done.6, f32[9,32,128]{2,1,0:T(8,128)} %copy-done.7), custom_call_target="tpu_custom_call" | custom-call | flops 1000000 | bytes 688128 | tf_op jit(solution)/shard_map/mid_kernel/pallas_call | solution.py:485
  119.0 4.9 %all-to-all-done.2.refs_0_ = f32[8,8,128]{2,1,0:T(8,128)S(1)} async-done(((f32[8,8,128]{2,1,0:T(8,128)}), f32[8,8,128]{2,1,0:T(8,128)S(1)}, u32[]{:S(2)}, u32[]{:S(2)}) %all-to-all-start.2) | async-done | bytes 32800 | tf_op jit(solution)/shard_map/all_to_all | solution.py:507
  124.5 4.0 %place_kernel.1 = f32[12,16,128]{2,1,0:T(8,128)} custom-call(f32[8,8,128]{2,1,0:T(8,128)} %copy-done.8, f32[128,128]{1,0:T(8,128)} %constant.12.clone.refs_1_, f32[8,128]{1,0:T(8,128)} %constant.13.clone.refs_2_, f32[10,8,128]{2,1,0:T(8,128)} %constant.14.clone.refs_3_, f32[18,128]{1,0:T(8,128)} %constant.15.clone.refs_4_, ...), custom_call_target="tpu_custom_call" | custom-call | flops 1000000 | bytes 98304 | tf_op jit(solution)/shard_map/place_kernel/pallas_call | solution.py:485
  (24 shorter events, 3.3 us)
Async XLA Ops:
  1.9 9.4 %collective-permute-start = (f32[6,6,8,128]{3,2,1,0:T(8,128)}, f32[6,6,8,128]{3,2,1,0:T(8,128)S(1)}, u32[]{:S(2)}, u32[]{:S(2)}) collective-permute-start(f32[6,6,8,128]{3,2,1,0:T(8,128)} %part_kernel.1.pairs.own), channel_id=1, source_target_pairs={{0,128},{128,256},{256,384},{384,512},{512,640},{640,768},{768,896... | collective-permute-start | bytes 442376 | tf_op jit(solution)/shard_map/ppermute | solution.py:503
  5.4 7.4 %collective-permute-start.1 = (f32[6,6,8,128]{3,2,1,0:T(8,128)}, f32[6,6,8,128]{3,2,1,0:T(8,128)S(1)}, u32[]{:S(2)}, u32[]{:S(2)}) collective-permute-start(f32[6,6,8,128]{3,2,1,0:T(8,128)} %part_kernel.1.pairs.own), channel_id=1, source_target_pairs={{0,896},{128,0},{256,128},{384,256},{512,384},{640,512},{768,640},... | collective-permute-start | bytes 442376 | tf_op jit(solution)/shard_map/ppermute | solution.py:503
  11.3 1.5 %copy-start = (f32[6,6,8,128]{3,2,1,0:T(8,128)}, f32[6,6,8,128]{3,2,1,0:T(8,128)S(1)}, u32[]{:S(2)}) copy-start(f32[6,6,8,128]{3,2,1,0:T(8,128)S(1)} %collective-permute-done.left) | copy-start | bytes 442372
  12.8 0.7 copy-start.1
  15.4 22.8 %collective-permute-start.2 = (f32[6,18,4,128]{3,2,1,0:T(4,128)}, f32[6,18,4,128]{3,2,1,0:T(4,128)S(1)}, u32[]{:S(2)}, u32[]{:S(2)}) collective-permute-start(f32[6,18,4,128]{3,2,1,0:T(4,128)} %get-tuple-element.17), channel_id=1, source_target_pairs={{0,8},{8,16},{16,24},{24,32},{32,40},{40,48},{48,56},{56,64},{64,7... | collective-permute-start | bytes 663560 | tf_op jit(solution)/shard_map/ppermute | solution.py:503
  19.7 19.8 %collective-permute-start.3 = (f32[6,18,4,128]{3,2,1,0:T(4,128)}, f32[6,18,4,128]{3,2,1,0:T(4,128)S(1)}, u32[]{:S(2)}, u32[]{:S(2)}) collective-permute-start(f32[6,18,4,128]{3,2,1,0:T(4,128)} %get-tuple-element.18), channel_id=1, source_target_pairs={{0,120},{8,0},{16,8},{24,16},{32,24},{40,32},{48,40},{56,48},{64,5... | collective-permute-start | bytes 663560 | tf_op jit(solution)/shard_map/ppermute | solution.py:503
  38.2 1.3 %copy-start.2 = (f32[6,18,4,128]{3,2,1,0:T(4,128)}, f32[6,18,4,128]{3,2,1,0:T(4,128)S(1)}, u32[]{:S(2)}) copy-start(f32[6,18,4,128]{3,2,1,0:T(4,128)S(1)} %collective-permute-done.2.below) | copy-start | bytes 663556
  39.5 0.7 copy-start.3
  42.7 5.6 %collective-permute-start.4 = (f32[27,16,128]{2,1,0:T(8,128)}, f32[27,16,128]{2,1,0:T(8,128)S(1)}, u32[]{:S(2)}, u32[]{:S(2)}) collective-permute-start(f32[27,16,128]{2,1,0:T(8,128)} %get-tuple-element.19), channel_id=1, source_target_pairs={{0,1},{1,2},{2,3},{3,4},{4,5},{5,6},{6,7},{7,0},{8,9},{9,10},{10,1... | collective-permute-start | bytes 663560 | tf_op jit(solution)/shard_map/ppermute | solution.py:503
  42.7 5.6 %collective-permute-start.5 = (f32[27,16,128]{2,1,0:T(8,128)}, f32[27,16,128]{2,1,0:T(8,128)S(1)}, u32[]{:S(2)}, u32[]{:S(2)}) collective-permute-start(f32[27,16,128]{2,1,0:T(8,128)} %get-tuple-element.20), channel_id=1, source_target_pairs={{0,7},{1,0},{2,1},{3,2},{4,3},{5,4},{6,5},{7,6},{8,15},{9,8},{10,9... | collective-permute-start | bytes 663560 | tf_op jit(solution)/shard_map/ppermute | solution.py:503
  48.2 0.7 copy-start.4
  48.9 0.7 copy-start.5
  53.6 9.1 %collective-permute-start.6 = (f32[12,16,128]{2,1,0:T(8,128)}, f32[12,16,128]{2,1,0:T(8,128)S(1)}, u32[]{:S(2)}, u32[]{:S(2)}) collective-permute-start(f32[12,16,128]{2,1,0:T(8,128)} %get-tuple-element.21.own), channel_id=1, source_target_pairs={{0,8},{8,16},{16,24},{24,32},{32,40},{40,48},{48,56},{56,64},{64,7... | collective-permute-start | bytes 294920 | tf_op jit(solution)/shard_map/ppermute | solution.py:503
  55.6 8.9 %collective-permute-start.7 = (f32[12,16,128]{2,1,0:T(8,128)}, f32[12,16,128]{2,1,0:T(8,128)S(1)}, u32[]{:S(2)}, u32[]{:S(2)}) collective-permute-start(f32[12,16,128]{2,1,0:T(8,128)} %get-tuple-element.21.own), channel_id=1, source_target_pairs={{0,120},{8,0},{16,8},{24,16},{32,24},{40,32},{48,40},{56,48},{64,5... | collective-permute-start | bytes 294920 | tf_op jit(solution)/shard_map/ppermute | solution.py:503
  62.8 1.7 %copy-start.9 = (f32[12,16,128]{2,1,0:T(8,128)}, f32[12,16,128]{2,1,0:T(8,128)S(1)}, u32[]{:S(2)}) copy-start(f32[12,16,128]{2,1,0:T(8,128)S(1)} %collective-permute-done.6.below) | copy-start | bytes 294916
  64.5 0.6 copy-start.10
  66.9 48.9 %collective-permute-start.8 = (f32[9,32,128]{2,1,0:T(8,128)}, f32[9,32,128]{2,1,0:T(8,128)S(1)}, u32[]{:S(2)}, u32[]{:S(2)}) collective-permute-start(f32[9,32,128]{2,1,0:T(8,128)} %get-tuple-element.23), channel_id=1, source_target_pairs={{0,128},{128,256},{256,384},{384,512},{512,640},{640,768},{768,896... | collective-permute-start | bytes 442376 | tf_op jit(solution)/shard_map/ppermute | solution.py:503
  70.3 45.6 %collective-permute-start.9 = (f32[9,32,128]{2,1,0:T(8,128)}, f32[9,32,128]{2,1,0:T(8,128)S(1)}, u32[]{:S(2)}, u32[]{:S(2)}) collective-permute-start(f32[9,32,128]{2,1,0:T(8,128)} %get-tuple-element.24), channel_id=1, source_target_pairs={{0,896},{128,0},{256,128},{384,256},{512,384},{640,512},{768,640},... | collective-permute-start | bytes 442376 | tf_op jit(solution)/shard_map/ppermute | solution.py:503
  109.4 14.5 %all-to-all-start.2 = ((f32[8,8,128]{2,1,0:T(8,128)}), f32[8,8,128]{2,1,0:T(8,128)S(1)}, u32[]{:S(2)}, u32[]{:S(2)}) async-start(f32[8,8,128]{2,1,0:T(8,128)} %along_y_kernel.1), calls=%async_computation.2 | async-start | bytes 65536 | tf_op jit(solution)/shard_map/all_to_all | solution.py:507
  115.9 0.7 copy-start.6
  115.9 0.7 copy-start.7
  123.9 0.6 copy-start.8

commit v2 on v1

--- a/solution.py
+++ b/solution.py
@@ -1,5 +1,3 @@
-import functools
-
 import jax
 import jax.numpy as jnp
 import numpy as np
@@ -7,6 +5,7 @@
 from jax.experimental import pallas as pl
 from jax.experimental.pallas import tpu as pltpu
 from jax.sharding import PartitionSpec as P
+
 
 GX, GY, GZ = 8, 16, 8
 BX, BY, BZ = 6, 8, 64
@@ -55,17 +54,22 @@
     qx, lx = basis_of(GX)
     qy, ly = basis_of(GY)
     qz, lz = basis_of(GZ)
-    qyz = np.einsum("jb,kc->jkbc", qy, qz).reshape(LANES, LANES)
-    lam = BY * BZ * lx[:, None, None] + BX * BZ * ly[None, :, None] + BX * BY * lz[None, None, :]
+    count = GX * GZ
+    qxz = np.zeros((LANES, LANES))
+    qxz[:count, :count] = np.einsum("ia,kc->ikac", qx, qz).reshape(count, count)
+    lam = BX * BZ * ly[:, None, None] + BY * BZ * lx[None, :, None] + BX * BY * lz[None, None, :]
     lam[0, 0, 0] = 1.0
-    inverse = -1.0 / lam
-    inverse[0, 0, 0] = 0.0
-    inverse = inverse.reshape(GX, LANES)
+    table = -1.0 / lam
+    table[0, 0, 0] = 0.0
+    inverse = np.zeros((GY, LANES))
+    inverse[:, :count] = table.reshape(GY, count)
     around = lambda n: np.arange(-1, n + 1) % n
-    tx = np.repeat(qx[around(GX)][:, :, None], LANES, axis=2)
-    ty = np.repeat(qy[around(GY)], GZ, axis=1)
-    tz = np.tile(qz[around(GZ)], (1, GY))
-    return [np.asarray(t, np.float32) for t in (qyz, inverse, tx, ty, tz)]
+    ty = np.repeat(qy[around(GY)][:, :, None], LANES, axis=2)
+    tx = np.zeros((GX + 2, LANES))
+    tx[:, :count] = np.repeat(qx[around(GX)], GZ, axis=1)
+    tz = np.zeros((GZ + 2, LANES))
+    tz[:, :count] = np.tile(qz[around(GZ)], (1, GX))
+    return [np.asarray(t, np.float32) for t in (qxz, inverse, tx, ty, tz)]
 
 
 def parting():
@@ -254,58 +258,72 @@
     summed = jnp.where((rows == 15) & (cols < 64), summed + roll(summed, 64, 1), summed)
     summed = jnp.where((rows == 15) & (cols >= 64), 0.0, summed)
     sent = dot_nt(jnp.where(pick, 1.0, 0.0), summed)
-    for peer in range(GZ):
+    flat = sent[0:1] + roll(sent[1:2], 16, 1) + roll(sent[2:3], 32, 1)
+    for peer in range(GX * GZ):
+        out[peer] = flat
+
+
+def along_xz_kernel(got, out):
+    values = got[:, 0, :]
+    lane = iota((GZ, LANES), 1)
+    part, slot = lane // 16, lane % 16
+    lines = []
+    for i in range(GX):
+        line = values[GZ * i : GZ * i + GZ]
+        total = jnp.where(part == 0, line, 0.0)
+        total = total + roll(jnp.where(part == 1, line, 0.0), 1, 0)
+        lines.append(total + roll(jnp.where(part == 2, line, 0.0), -1, 0))
+    rows = []
+    for i in range(GX):
+        total = jnp.where(slot == 15, lines[i], 0.0)
+        for r in range(5):
+            total = jnp.where((slot < 15) & (slot // 3 == r), lines[(i - (r - 2)) % GX], total)
+        rows.append(total)
+    total = jnp.concatenate(rows + rows, 0)
+    row, col = iota((8, LANES), 0), iota((8, LANES), 1)
+    take = (col < 48) & (col % 16 < 15) & ((col % 16) % 3 == row)
+    take = take | ((row == 3) & (col == 15))
+    sums = dot_nt(jnp.where(take, 1.0, 0.0), total)
+    first = iota((1, LANES), 1) < 64
+    sent = [jnp.where(first, sums[0:1], sums[1:2]), jnp.where(first, sums[2:3], sums[3:4])]
+    sent = jnp.concatenate(sent, 0)
+    for peer in range(GY):
         out[peer] = sent
 
 
-def along_z_kernel(got, out):
-    total = got[:, 0, :] + roll(got[:, 1, :], 1, 0) + roll(got[:, 2, :], -1, 0)
-    rows, cols = iota((LANES, LANES), 0), iota((LANES, LANES), 1)
-    tiled = dot(total, jnp.where((rows < 16) & (cols % 16 == rows), 1.0, 0.0))
-    row, lane = iota((GZ, LANES), 0), iota((GZ, LANES), 1)
-    flat = jnp.sum(jnp.where(lane // 16 == row, tiled, 0.0), axis=0, keepdims=True)
-    for peer in range(GY):
-        out[peer] = flat
-
-
-def along_y_kernel(got, out):
-    values = got[:, 0, :]
-    slot = iota((GY, LANES), 1) % 16
-    total = jnp.where((slot % 3 == 0) | (slot == 15), values, 0.0)
-    total = total + roll(jnp.where((slot % 3 == 1), values, 0.0), 1, 0)
-    total = total + roll(jnp.where((slot % 3 == 2), values, 0.0), -1, 0)
-    rows, cols = iota((LANES, LANES), 0), iota((LANES, LANES), 1)
-    row, lane = iota((GY, LANES), 0), iota((GY, LANES), 1)
-    place = iota((8, LANES), 0)
-    sent = jnp.zeros((8, LANES), F32)
-    for r in range(6):
-        take = (cols % 8 == rows // 16) & ((rows % 16) // 3 == r)
-        tiled = dot(total, jnp.where(take, 1.0, 0.0))
-        flat = jnp.sum(jnp.where(lane // 8 == row, tiled, 0.0), axis=0, keepdims=True)
-        sent = jnp.where(place == r, flat, sent)
-    for peer in range(GX):
-        out[peer] = sent
+def sides(axis, first, second):
+    odd = lax.axis_index(axis) % 2 == 1
+
+    def pick(swap):
+        return lambda *at: jnp.where(odd != swap, first[at], second[at])
+
+    return pick(False), pick(True)
+
+
+def for_swaps(axis, low, high):
+    odd = lax.axis_index(axis) % 2 == 1
+    return jnp.where(odd, low, high), jnp.where(odd, high, low)
 
 
 def wide_x(own, left, right, array, x):
     if x < 0:
-        return left[array, x + BX]
+        return left(array, x + BX)
     if x >= BX:
-        return right[array, x - BX]
+        return right(array, x - BX)
     return own[array, x]
 
 
-def rim_y_kernel(own, left, right, low, high):
+def rim_y_kernel(own, xa, xb, ya, yb):
+    left, right = sides("gx", xa, xb)
     for array in range(6):
         for x in range(-BX, 2 * BX):
             value = wide_x(own, left, right, array, x)
-            low[array, x + BX] = value[:4]
-            high[array, x + BX] = value[4:]
+            ya[array, x + BX], yb[array, x + BX] = for_swaps("gy", value[:4], value[4:])
 
 
 def tall(own, left, right, below, above, array, x):
     value = wide_x(own, left, right, array, x)
-    rim = jnp.concatenate([above[array, x + BX], below[array, x + BX]], 0)
+    rim = jnp.concatenate([above(array, x + BX), below(array, x + BX)], 0)
     return jnp.concatenate([value, rim], 0)
 
 
@@ -318,7 +336,9 @@
     return made
 
 
-def rim_z_kernel(own, left, right, below, above, low, high):
+def rim_z_kernel(own, xa, xb, ya, yb, za, zb):
+    left, right = sides("gx", xa, xb)
+    below, above = sides("gy", ya, yb)
     lane = iota((16, LANES), 1)
     for slot, members in groups():
         lows = highs = None
@@ -328,11 +348,13 @@
             up = roll(value, 16 * (i + 1), 1)
             lows = down if lows is None else jnp.where((lane % 64) // 16 == i, down, lows)
             highs = up if highs is None else jnp.where((lane % 64) // 16 == i, up, highs)
-        low[slot] = lows
-        high[slot] = highs
-
-
-def fine_kernel(own, left, right, below, above, before, after, level, fine, kept, fref, sref):
+        za[slot], zb[slot] = for_swaps("gz", lows, highs)
+
+
+def fine_kernel(own, xa, xb, ya, yb, za, zb, level, fine, kept, fref, sref):
+    left, right = sides("gx", xa, xb)
+    below, above = sides("gy", ya, yb)
+    before, after = sides("gz", za, zb)
     source, field = Kept(sref), Kept(fref)
     lane = iota((16, LANES), 1)
     home = {}
@@ -343,7 +365,7 @@
         for x in range(-BX, 2 * BX):
             value = tall(own, left, right, below, above, array, x)
             slot, i = home[(array, x)]
-            up, down = after[slot], before[slot]
+            up, down = after(slot), before(slot)
             for c in (0, 1):
                 mine = roll(value, 64, 1) if c else value
                 right_rim = roll(up, 64 - 16 * i - 64 * c, 1)
@@ -367,27 +389,27 @@
             kept[n, x + 2] = source.get((cell, x))
 
 
-def level_y_kernel(own, below, above, wide, low, high):
+def level_y_kernel(own, ya, yb, wide, xa, xb):
+    below, above = sides("gy", ya, yb)
     first = iota((8, LANES), 0) == 0
     last = iota((8, LANES), 0) == 7
     for x in range(12):
-        mine, down, up = own[x], below[x], above[x]
+        mine, down, up = own[x], below(x), above(x)
         tail = jnp.where(first, up[8:16], 0.0)
         lead = jnp.where(last, down[8:16], 0.0)
         value = jnp.concatenate([mine[:8], up[:8], tail + lead, down[:8]], 0)
         wide[x] = value
-        if x >= 3:
-            low[x - 3] = value
-        if x < 9:
-            high[x] = value
-
-
-def mid_kernel(wide, left, right, level, mid, eref):
+    for x in range(9):
+        xa[x], xb[x] = for_swaps("gx", wide[x + 3], wide[x])
+
+
+def mid_kernel(wide, xa, xb, level, mid, eref):
+    left, right = sides("gx", xa, xb)
     for x in range(-9, BX + 9):
         if x < 0:
-            value = left[x + 9]
+            value = left(x + 9)
         elif x >= BX:
-            value = right[x - BX]
+            value = right(x - BX)
         else:
             value = wide[x + 3]
         level[x + 9] = value
@@ -411,16 +433,19 @@
         self.ref[x + self.start] = value
 
 
-def last_kernel(got, qyz, inverse, tx, ty, tz, level, mid, fine, kept, table, out, eref, fref, oref, *, axes):
-    blocks = None
-    for r in range(5):
-        blocks = plus(blocks, roll(got[:, r, :], r - 2, 0))
-    mean = jnp.sum(got[:, 5, :], keepdims=True) * (1.0 / (GX * GY * GZ * 8 * BX * BY * BZ))
-    blocks = blocks - jnp.sum(blocks, keepdims=True) * (1.0 / (GX * GY * GZ))
-    half = dot(blocks, qyz[...])
+def last_kernel(got, qxz, inverse, tx, ty, tz, level, mid, fine, kept, table, out, eref, fref, oref, *, axes):
+    one, two = got[:, 0, :], got[:, 1, :]
+    blocks = one + roll(roll(one, 64, 1), 1, 0) + roll(two, -1, 0)
+    inside = iota((GY, LANES), 1) < GX * GZ
+    mean = jnp.sum(jnp.where(inside, 0.0, two), keepdims=True)
+    mean = mean * (1.0 / (GX * GY * GZ * 8 * BX * BY * BZ))
+    blocks = jnp.where(inside, blocks, 0.0)
+    level_out = jnp.sum(blocks, keepdims=True) * (1.0 / (GX * GY * GZ))
+    blocks = jnp.where(inside, blocks - level_out, 0.0)
+    half = dot(blocks, qxz[...])
     modes = None
-    for x in range(GX):
-        modes = plus(modes, half[x : x + 1, :] * tx[x + 1])
+    for y in range(GY):
+        modes = plus(modes, half[y : y + 1, :] * ty[y + 1])
     modes = modes * inverse[...]
     ix, iy, iz = axes
     own_lane = iota((LANES, LANES), 0)
@@ -428,10 +453,11 @@
     spread_z = jnp.where(own_lane < 64, zrow(0), jnp.where(own_lane < 96, zrow(1), zrow(-1)))
     place = iota((16, LANES), 0)
     stacked = jnp.zeros((16, LANES), F32)
-    for dx in (-1, 0, 1):
-        line = jnp.sum(modes * tx[ix + 1 + dx], axis=0, keepdims=True)
-        for dy in (-1, 0, 1):
-            stacked = jnp.where(place == 3 * (dx + 1) + dy + 1, line * ty[pl.ds(iy + 1 + dy, 1), :], stacked)
+    for dy in (-1, 0, 1):
+        line = jnp.sum(modes * ty[iy + 1 + dy], axis=0, keepdims=True)
+        for dx in (-1, 0, 1):
+            both = line * tx[pl.ds(ix + 1 + dx, 1), :]
+            stacked = jnp.where(place == 3 * (dx + 1) + dy + 1, both, stacked)
     coarse = dot_nt(stacked, spread_z)
     row = iota((32, LANES), 0)
     error = Given(eref, 6, 18)
@@ -479,7 +505,7 @@
         return self.ref[CELLS.index(cell), x + 2] if -2 <= x < BX + 2 else None
 
 
-def run(kernel, shapes, args, scratch=(), flops=1000000, **static):
+def run(kernel, shapes, args, scratch=(), flops=500000000):
     space = pl.BlockSpec(memory_space=pltpu.VMEM)
     moved = 4 * sum(int(np.prod(s)) for s in shapes)
     return pl.pallas_call(
@@ -489,7 +515,7 @@
         out_specs=[space] * len(shapes),
         scratch_shapes=[pltpu.VMEM(s, F32) for s in scratch],
         cost_estimate=pl.CostEstimate(flops=flops, bytes_accessed=moved, transcendentals=0),
-        name=kernel.__name__,
+        compiler_params=pltpu.CompilerParams(vmem_limit_bytes=16 << 20),
     )(*args)
 
 
@@ -498,51 +524,51 @@
     last_kernel(*refs, axes=axes)
 
 
-def moved(array, axis, step):
+def swapped(first, second, axis):
     count = lax.axis_size(axis)
-    return lax.ppermute(array, axis, [(i, (i + step) % count) for i in range(count)])
+    one = [(i, i ^ 1) for i in range(count)]
+    two = [(i, (i + 1 if i % 2 else i - 1) % count) for i in range(count)]
+    got = lax.ppermute(first, axis, one)
+    return got, lax.ppermute(second, axis, two)
 
 
 def everyone(array, axis):
     return lax.all_to_all(array, axis, 0, 0, tiled=True)
 
 
-def body(density, potential):
-    qyz, inverse, tx, ty, tz = (jnp.asarray(t) for t in coarse_tables())
+def steps(density, potential):
+    tables = [jnp.asarray(t) for t in coarse_tables()]
     table = jnp.asarray(parting())
     (own,) = run(part_kernel, [(6, 6, 8, LANES)], [density, potential, table], [(192, LANES)] * 2)
-    left, right = moved(own, "gx", 1), moved(own, "gx", -1)
+    xs = swapped(own, own, "gx")
     (shares,) = run(
         share_kernel,
-        [(GZ, 8, LANES)],
+        [(GX * GZ, 1, LANES)],
         [own],
         [(96, 16, LANES), (48, 16, LANES), (20, 24, LANES), (12, 24, LANES), (LANES, LANES)],
     )
-    (line,) = run(along_z_kernel, [(GY, 1, LANES)], [everyone(shares, "gz")])
-    (plane,) = run(along_y_kernel, [(GX, 8, LANES)], [everyone(line, "gy")])
-    blocks = everyone(plane, "gx")
-    low, high = run(rim_y_kernel, [(6, 18, 4, LANES)] * 2, [own, left, right])
-    below, above = moved(high, "gy", 1), moved(low, "gy", -1)
-    low, high = run(rim_z_kernel, [(27, 16, LANES)] * 2, [own, left, right, below, above])
-    before, after = moved(high, "gz", 1), moved(low, "gz", -1)
+    (plane,) = run(along_xz_kernel, [(GY, 2, LANES)], [everyone(shares, ("gx", "gz"))])
+    blocks = everyone(plane, "gy")
+    ys = swapped(*run(rim_y_kernel, [(6, 18, 4, LANES)] * 2, [own, *xs]), "gy")
+    zs = swapped(*run(rim_z_kernel, [(27, 16, LANES)] * 2, [own, *xs, *ys]), "gz")
     level, fine, kept = run(
         fine_kernel,
         [(12, 16, LANES), (8, 10, 16, LANES), (8, 10, 16, LANES)],
-        [own, left, right, below, above, before, after],
+        [own, *xs, *ys, *zs],
         [(144, 16, LANES), (144, 16, LANES)],
     )
-    below, above = moved(level, "gy", 1), moved(level, "gy", -1)
-    wide, low, high = run(
-        level_y_kernel, [(12, 32, LANES), (9, 32, LANES), (9, 32, LANES)], [level, below, above]
+    ys = swapped(level, level, "gy")
+    wide, xa, xb = run(
+        level_y_kernel, [(12, 32, LANES), (9, 32, LANES), (9, 32, LANES)], [level, *ys]
     )
-    left, right = moved(high, "gx", 1), moved(low, "gx", -1)
+    xs = swapped(xa, xb, "gx")
     level, mid = run(
-        mid_kernel, [(24, 32, LANES), (18, 32, LANES)], [wide, left, right], [(24, 32, LANES)]
+        mid_kernel, [(24, 32, LANES), (18, 32, LANES)], [wide, *xs], [(24, 32, LANES)]
     )
     (out,) = run(
         place_kernel,
         [(12, 16, LANES)],
-        [blocks, qyz, inverse, tx, ty, tz, level, mid, fine, kept, table],
+        [blocks, *tables, level, mid, fine, kept, table],
         [(18, 32, LANES), (80, 16, LANES), (192, LANES)],
     )
     return out
@@ -550,4 +576,4 @@
 
 def solution(mesh):
     spec = P("gx", "gy", "gz")
-    return jax.shard_map(body, mesh=mesh, in_specs=(spec, spec), out_specs=spec, check_vma=False)
+    return jax.shard_map(steps, mesh=mesh, in_specs=(spec, spec), out_specs=spec, check_vma=False)

time: 129 us -> 110 us (0.85)
  the two profiles are of different devices: /device:TPU:2 before, /device:TPU:1 now
where the time goes in v2:
time: 110 us; the launch traced here: 109 us
  starting transfers between devices  56.1 us (51%)
  waiting for transfers between devices  23.7 us (22%)
  blocking collectives  18.1 us (16%)
  Pallas kernels  8.23 us (7%)
  local copies, waits for them, and re-layouts  2.66 us (2%)
    ppermute x5, starting transfers between devices, swapped(): return (got, lax.ppermute(second, axis, two))  33.1 us
    all_to_all x1, blocking collectives, everyone(): return lax.all_to_all(array, axis, 0, 0, tiled=True)  18.1 us
    ppermute x5, starting transfers between devices, swapped(): got = lax.ppermute(first, axis, one)  16.9 us
    ppermute x5, waiting for transfers between devices, swapped(): return (got, lax.ppermute(second, axis, two))  13 us
    all_to_all x1, waiting for transfers between devices, everyone(): return lax.all_to_all(array, axis, 0, 0, tiled=True)  10.7 us
    pallas_call x9, Pallas kernels, run(): pl.pallas_call(kernel, out_shape=[jax.ShapeDtypeStruct(s, F32) for s in s...  8.23 us
    all_to_all x1, starting transfers between devices, everyone(): return lax.all_to_all(array, axis, 0, 0, tiled=True)  6.1 us
    unnamed x18, local copies, waits for them, and re-layouts  2.66 us
  transfers between devices with their start and end apart: 11, of which 5 were waited for; matrix products, arithmetic and copies ran while one was open for 0% of the time, Pallas kernels for 3%

profile of v2, /device:TPU:1, one launch (start us, length us, event | category | flops | bytes accessed | tf_op | source)
XLA Modules:
  0.0 109.0 jit_solution(5342657602990095175)
XLA Ops:
  0.0 0.8 copy-done.1
  0.8 0.9 copy-done.7
  1.7 0.9 copy-done.8
  2.6 0.3 shard_map.82.pairs.own
  2.9 4.0 %collective-permute-start = (f32[6,6,8,128]{3,2,1,0:T(8,128)S(1)}, f32[6,6,8,128]{3,2,1,0:T(8,128)S(1)}, u32[]{:S(2)}, u32[]{:S(2)}) collective-permute-start(f32[6,6,8,128]{3,2,1,0:T(8,128)S(1)} %shard_map.82.pairs.own), channel_id=1, source_target_pairs={{0,128},{128,0},{256,384},{384,256},{512,640},{640,512},{768,896},... | collective-permute-start | bytes 442376 | tf_op jit(solution)/shard_map/ppermute | solution.py:531
  7.0 4.9 %collective-permute-start.1 = (f32[6,6,8,128]{3,2,1,0:T(8,128)S(1)}, f32[6,6,8,128]{3,2,1,0:T(8,128)S(1)}, u32[]{:S(2)}, u32[]{:S(2)}) collective-permute-start(f32[6,6,8,128]{3,2,1,0:T(8,128)S(1)} %shard_map.82.pairs.own), channel_id=1, source_target_pairs={{0,896},{128,256},{256,128},{384,512},{512,384},{640,768},{768,640... | collective-permute-start | bytes 442376 | tf_op jit(solution)/shard_map/ppermute | solution.py:532
  11.9 2.5 %collective-permute-done.1.xb = f32[6,6,8,128]{3,2,1,0:T(8,128)S(1)} collective-permute-done((f32[6,6,8,128]{3,2,1,0:T(8,128)S(1)}, f32[6,6,8,128]{3,2,1,0:T(8,128)S(1)}, u32[]{:S(2)}, u32[]{:S(2)}) %collective-permute-start.1) | collective-permute-done | bytes 147488 | tf_op jit(solution)/shard_map/ppermute | solution.py:532
  14.4 0.1 shard_map.85
  14.5 4.7 %collective-permute-start.2 = (f32[6,18,4,128]{3,2,1,0:T(4,128)S(1)}, f32[6,18,4,128]{3,2,1,0:T(4,128)S(1)}, u32[]{:S(2)}, u32[]{:S(2)}) collective-permute-start(f32[6,18,4,128]{3,2,1,0:T(4,128)S(1)} %get-tuple-element.17), channel_id=1, source_target_pairs={{0,8},{8,0},{16,24},{24,16},{32,40},{40,32},{48,56},{56,48},{64,72... | collective-permute-start | bytes 663560 | tf_op jit(solution)/shard_map/ppermute | solution.py:531
  19.2 16.1 %collective-permute-start.3 = (f32[6,18,4,128]{3,2,1,0:T(4,128)S(1)}, f32[6,18,4,128]{3,2,1,0:T(4,128)S(1)}, u32[]{:S(2)}, u32[]{:S(2)}) collective-permute-start(f32[6,18,4,128]{3,2,1,0:T(4,128)S(1)} %get-tuple-element.18), channel_id=1, source_target_pairs={{0,120},{8,16},{16,8},{24,32},{32,24},{40,48},{48,40},{56,64},{64,... | collective-permute-start | bytes 663560 | tf_op jit(solution)/shard_map/ppermute | solution.py:532
  35.3 4.0 %collective-permute-done.3.yb = f32[6,18,4,128]{3,2,1,0:T(4,128)S(1)} collective-permute-done((f32[6,18,4,128]{3,2,1,0:T(4,128)S(1)}, f32[6,18,4,128]{3,2,1,0:T(4,128)S(1)}, u32[]{:S(2)}, u32[]{:S(2)}) %collective-permute-start.3) | collective-permute-done | bytes 221216 | tf_op jit(solution)/shard_map/ppermute | solution.py:532
  39.3 0.5 shard_map.86
  39.8 4.3 %collective-permute-start.4 = (f32[27,16,128]{2,1,0:T(8,128)S(1)}, f32[27,16,128]{2,1,0:T(8,128)S(1)}, u32[]{:S(2)}, u32[]{:S(2)}) collective-permute-start(f32[27,16,128]{2,1,0:T(8,128)S(1)} %get-tuple-element.19), channel_id=1, source_target_pairs={{0,1},{1,0},{2,3},{3,2},{4,5},{5,4},{6,7},{7,6},{8,9},{9,8},{10,11... | collective-permute-start | bytes 663560 | tf_op jit(solution)/shard_map/ppermute | solution.py:531
  44.1 3.0 %collective-permute-start.5 = (f32[27,16,128]{2,1,0:T(8,128)S(1)}, f32[27,16,128]{2,1,0:T(8,128)S(1)}, u32[]{:S(2)}, u32[]{:S(2)}) collective-permute-start(f32[27,16,128]{2,1,0:T(8,128)S(1)} %get-tuple-element.20), channel_id=1, source_target_pairs={{0,7},{1,2},{2,1},{3,4},{4,3},{5,6},{6,5},{7,0},{8,15},{9,10},{10,... | collective-permute-start | bytes 663560 | tf_op jit(solution)/shard_map/ppermute | solution.py:532
  47.1 4.5 %collective-permute-done.5.zb = f32[27,16,128]{2,1,0:T(8,128)S(1)} collective-permute-done((f32[27,16,128]{2,1,0:T(8,128)S(1)}, f32[27,16,128]{2,1,0:T(8,128)S(1)}, u32[]{:S(2)}, u32[]{:S(2)}) %collective-permute-start.5) | collective-permute-done | bytes 221216 | tf_op jit(solution)/shard_map/ppermute | solution.py:532
  51.6 1.7 %shard_map.87 = (f32[12,16,128]{2,1,0:T(8,128)S(1)}, f32[8,10,16,128]{3,2,1,0:T(8,128)S(1)}, f32[8,10,16,128]{3,2,1,0:T(8,128)S(1)}) custom-call(f32[6,6,8,128]{3,2,1,0:T(8,128)S(1)} %shard_map.82.pairs.own, f32[6,6,8,128]{3,2,1,0:T(8,128)S(1)} %collective-permute-done.xa, f32[6,6,8,128]{3,2,1,0:T(8,128)S(1)} %collective-permute-done.1.xb, ...), custom_call_target="tpu_custom_call" | custom-call | flops 500000000 | bytes 1409024 | tf_op jit(solution)/shard_map/pallas_call | solution.py:511
  53.4 1.9 %collective-permute-start.6 = (f32[12,16,128]{2,1,0:T(8,128)S(1)}, f32[12,16,128]{2,1,0:T(8,128)S(1)}, u32[]{:S(2)}, u32[]{:S(2)}) collective-permute-start(f32[12,16,128]{2,1,0:T(8,128)S(1)} %get-tuple-element.21.own), channel_id=1, source_target_pairs={{0,8},{8,0},{16,24},{24,16},{32,40},{40,32},{48,56},{56,48},{64,72... | collective-permute-start | bytes 294920 | tf_op jit(solution)/shard_map/ppermute | solution.py:531
  55.3 4.6 %collective-permute-start.7 = (f32[12,16,128]{2,1,0:T(8,128)S(1)}, f32[12,16,128]{2,1,0:T(8,128)S(1)}, u32[]{:S(2)}, u32[]{:S(2)}) collective-permute-start(f32[12,16,128]{2,1,0:T(8,128)S(1)} %get-tuple-element.21.own), channel_id=1, source_target_pairs={{0,120},{8,16},{16,8},{24,32},{32,24},{40,48},{48,40},{56,64},{64,... | collective-permute-start | bytes 294920 | tf_op jit(solution)/shard_map/ppermute | solution.py:532
  59.9 2.0 %collective-permute-done.7.yb = f32[12,16,128]{2,1,0:T(8,128)S(1)} collective-permute-done((f32[12,16,128]{2,1,0:T(8,128)S(1)}, f32[12,16,128]{2,1,0:T(8,128)S(1)}, u32[]{:S(2)}, u32[]{:S(2)}) %collective-permute-start.7) | collective-permute-done | bytes 98336 | tf_op jit(solution)/shard_map/ppermute | solution.py:532
  61.9 1.9 %collective-permute-start.8 = (f32[9,32,128]{2,1,0:T(8,128)S(1)}, f32[9,32,128]{2,1,0:T(8,128)S(1)}, u32[]{:S(2)}, u32[]{:S(2)}) collective-permute-start(f32[9,32,128]{2,1,0:T(8,128)S(1)} %get-tuple-element.23), channel_id=1, source_target_pairs={{0,128},{128,0},{256,384},{384,256},{512,640},{640,512},{768,896},... | collective-permute-start | bytes 442376 | tf_op jit(solution)/shard_map/ppermute | solution.py:531
  63.8 4.5 %collective-permute-start.9 = (f32[9,32,128]{2,1,0:T(8,128)S(1)}, f32[9,32,128]{2,1,0:T(8,128)S(1)}, u32[]{:S(2)}, u32[]{:S(2)}) collective-permute-start(f32[9,32,128]{2,1,0:T(8,128)S(1)} %get-tuple-element.24), channel_id=1, source_target_pairs={{0,896},{128,256},{256,128},{384,512},{512,384},{640,768},{768,640... | collective-permute-start | bytes 442376 | tf_op jit(solution)/shard_map/ppermute | solution.py:532
  68.3 1.7 %shard_map.83 = f32[64,1,128]{2,1,0:T(1,128)S(1)} custom-call(f32[6,6,8,128]{3,2,1,0:T(8,128)S(1)} %shard_map.82.pairs.own), custom_call_target="tpu_custom_call" | custom-call | flops 500000000 | bytes 32768 | tf_op jit(solution)/shard_map/pallas_call | solution.py:511
  70.0 18.1 %all_to_all.10.got = f32[64,1,128]{2,1,0:T(1,128)S(1)} all-to-all(f32[64,1,128]{2,1,0:T(1,128)S(1)} %shard_map.83), channel_id=1, replica_groups=mesh['gx'=8,'gy'=16,'gz'=8] {'gx','gz'}, dimensions={0} | all-to-all | bytes 65536 | tf_op jit(solution)/shard_map/all_to_all | solution.py:536
  88.2 0.9 shard_map.84
  89.0 6.1 %all-to-all-start.1 = ((f32[16,2,128]{2,1,0:T(2,128)}), f32[16,2,128]{2,1,0:T(2,128)S(1)}, u32[]{:S(2)}, u32[]{:S(2)}) async-start(f32[16,2,128]{2,1,0:T(2,128)} %shard_map.84), calls=%async_computation.1 | async-start | bytes 32768 | tf_op jit(solution)/shard_map/all_to_all | solution.py:536
  95.2 0.0 copy-start
  95.2 0.0 copy-start.3
  95.2 0.0 copy-start.4
  95.2 0.0 copy-start.5
  95.2 0.6 shard_map.89
  95.8 10.7 %all-to-all-done.1.refs_0_ = f32[16,2,128]{2,1,0:T(2,128)S(1)} async-done(((f32[16,2,128]{2,1,0:T(2,128)}), f32[16,2,128]{2,1,0:T(2,128)S(1)}, u32[]{:S(2)}, u32[]{:S(2)}) %all-to-all-start.1) | async-done | bytes 16416 | tf_op jit(solution)/shard_map/all_to_all | solution.py:536
  106.6 2.5 %shard_map.90 = f32[12,16,128]{2,1,0:T(8,128)} custom-call(f32[16,2,128]{2,1,0:T(2,128)S(1)} %all-to-all-done.1.refs_0_, f32[128,128]{1,0:T(8,128)S(1)} %copy-done.3, f32[16,128]{1,0:T(8,128)S(1)} %copy-done.4, f32[10,128]{1,0:T(8,128)S(1)} %copy-done.5, f32[18,16,128]{2,1,0:T(8,128)S(1)} %copy-done, f32[10,128]{1,0:T(8,128)S(1)} %copy-done.6, ...), custom_call_target="tpu_custom_call" | custom-call | flops 500000000 | bytes 98304 | tf_op jit(solution)/shard_map/pallas_call | solution.py:511
  (18 shorter events, 0.1 us)
Async XLA Ops:
  0.0 0.8 copy-start.1
  0.8 0.9 copy-start.7
  1.7 0.9 copy-start.8
  2.9 8.9 %collective-permute-start = (f32[6,6,8,128]{3,2,1,0:T(8,128)S(1)}, f32[6,6,8,128]{3,2,1,0:T(8,128)S(1)}, u32[]{:S(2)}, u32[]{:S(2)}) collective-permute-start(f32[6,6,8,128]{3,2,1,0:T(8,128)S(1)} %shard_map.82.pairs.own), channel_id=1, source_target_pairs={{0,128},{128,0},{256,384},{384,256},{512,640},{640,512},{768,896},... | collective-permute-start | bytes 442376 | tf_op jit(solution)/shard_map/ppermute | solution.py:531
  7.0 7.4 %collective-permute-start.1 = (f32[6,6,8,128]{3,2,1,0:T(8,128)S(1)}, f32[6,6,8,128]{3,2,1,0:T(8,128)S(1)}, u32[]{:S(2)}, u32[]{:S(2)}) collective-permute-start(f32[6,6,8,128]{3,2,1,0:T(8,128)S(1)} %shard_map.82.pairs.own), channel_id=1, source_target_pairs={{0,896},{128,256},{256,128},{384,512},{512,384},{640,768},{768,640... | collective-permute-start | bytes 442376 | tf_op jit(solution)/shard_map/ppermute | solution.py:532
  14.5 20.9 %collective-permute-start.2 = (f32[6,18,4,128]{3,2,1,0:T(4,128)S(1)}, f32[6,18,4,128]{3,2,1,0:T(4,128)S(1)}, u32[]{:S(2)}, u32[]{:S(2)}) collective-permute-start(f32[6,18,4,128]{3,2,1,0:T(4,128)S(1)} %get-tuple-element.17), channel_id=1, source_target_pairs={{0,8},{8,0},{16,24},{24,16},{32,40},{40,32},{48,56},{56,48},{64,72... | collective-permute-start | bytes 663560 | tf_op jit(solution)/shard_map/ppermute | solution.py:531
  19.2 20.1 %collective-permute-start.3 = (f32[6,18,4,128]{3,2,1,0:T(4,128)S(1)}, f32[6,18,4,128]{3,2,1,0:T(4,128)S(1)}, u32[]{:S(2)}, u32[]{:S(2)}) collective-permute-start(f32[6,18,4,128]{3,2,1,0:T(4,128)S(1)} %get-tuple-element.18), channel_id=1, source_target_pairs={{0,120},{8,16},{16,8},{24,32},{32,24},{40,48},{48,40},{56,64},{64,... | collective-permute-start | bytes 663560 | tf_op jit(solution)/shard_map/ppermute | solution.py:532
  39.8 7.3 %collective-permute-start.4 = (f32[27,16,128]{2,1,0:T(8,128)S(1)}, f32[27,16,128]{2,1,0:T(8,128)S(1)}, u32[]{:S(2)}, u32[]{:S(2)}) collective-permute-start(f32[27,16,128]{2,1,0:T(8,128)S(1)} %get-tuple-element.19), channel_id=1, source_target_pairs={{0,1},{1,0},{2,3},{3,2},{4,5},{5,4},{6,7},{7,6},{8,9},{9,8},{10,11... | collective-permute-start | bytes 663560 | tf_op jit(solution)/shard_map/ppermute | solution.py:531
  44.1 7.5 %collective-permute-start.5 = (f32[27,16,128]{2,1,0:T(8,128)S(1)}, f32[27,16,128]{2,1,0:T(8,128)S(1)}, u32[]{:S(2)}, u32[]{:S(2)}) collective-permute-start(f32[27,16,128]{2,1,0:T(8,128)S(1)} %get-tuple-element.20), channel_id=1, source_target_pairs={{0,7},{1,2},{2,1},{3,4},{4,3},{5,6},{6,5},{7,0},{8,15},{9,10},{10,... | collective-permute-start | bytes 663560 | tf_op jit(solution)/shard_map/ppermute | solution.py:532
  53.4 6.5 %collective-permute-start.6 = (f32[12,16,128]{2,1,0:T(8,128)S(1)}, f32[12,16,128]{2,1,0:T(8,128)S(1)}, u32[]{:S(2)}, u32[]{:S(2)}) collective-permute-start(f32[12,16,128]{2,1,0:T(8,128)S(1)} %get-tuple-element.21.own), channel_id=1, source_target_pairs={{0,8},{8,0},{16,24},{24,16},{32,40},{40,32},{48,56},{56,48},{64,72... | collective-permute-start | bytes 294920 | tf_op jit(solution)/shard_map/ppermute | solution.py:531
  55.3 6.6 %collective-permute-start.7 = (f32[12,16,128]{2,1,0:T(8,128)S(1)}, f32[12,16,128]{2,1,0:T(8,128)S(1)}, u32[]{:S(2)}, u32[]{:S(2)}) collective-permute-start(f32[12,16,128]{2,1,0:T(8,128)S(1)} %get-tuple-element.21.own), channel_id=1, source_target_pairs={{0,120},{8,16},{16,8},{24,32},{32,24},{40,48},{48,40},{56,64},{64,... | collective-permute-start | bytes 294920 | tf_op jit(solution)/shard_map/ppermute | solution.py:532
  61.9 33.2 %collective-permute-start.8 = (f32[9,32,128]{2,1,0:T(8,128)S(1)}, f32[9,32,128]{2,1,0:T(8,128)S(1)}, u32[]{:S(2)}, u32[]{:S(2)}) collective-permute-start(f32[9,32,128]{2,1,0:T(8,128)S(1)} %get-tuple-element.23), channel_id=1, source_target_pairs={{0,128},{128,0},{256,384},{384,256},{512,640},{640,512},{768,896},... | collective-permute-start | bytes 442376 | tf_op jit(solution)/shard_map/ppermute | solution.py:531
  63.8 31.3 %collective-permute-start.9 = (f32[9,32,128]{2,1,0:T(8,128)S(1)}, f32[9,32,128]{2,1,0:T(8,128)S(1)}, u32[]{:S(2)}, u32[]{:S(2)}) collective-permute-start(f32[9,32,128]{2,1,0:T(8,128)S(1)} %get-tuple-element.24), channel_id=1, source_target_pairs={{0,896},{128,256},{256,128},{384,512},{512,384},{640,768},{768,640... | collective-permute-start | bytes 442376 | tf_op jit(solution)/shard_map/ppermute | solution.py:532
  89.0 17.5 %all-to-all-start.1 = ((f32[16,2,128]{2,1,0:T(2,128)}), f32[16,2,128]{2,1,0:T(2,128)S(1)}, u32[]{:S(2)}, u32[]{:S(2)}) async-start(f32[16,2,128]{2,1,0:T(2,128)} %shard_map.84), calls=%async_computation.1 | async-start | bytes 32768 | tf_op jit(solution)/shard_map/all_to_all | solution.py:536
  95.2 11.4 %copy-start = (f32[18,16,128]{2,1,0:T(8,128)S(1)}, f32[18,16,128]{2,1,0:T(8,128)}, u32[]{:S(2)}) copy-start(f32[18,16,128]{2,1,0:T(8,128)} %constant.15.clone.refs_4_) | copy-start | bytes 442372
  95.2 11.4 %copy-start.2 = (f32[128,128]{1,0:T(8,128)S(1)}, f32[128,128]{1,0:T(8,128)}, u32[]{:S(2)}) copy-start(f32[128,128]{1,0:T(8,128)} %constant.17.clone.table.refs_10_) | copy-start | bytes 196612
  95.2 11.4 %copy-start.3 = (f32[128,128]{1,0:T(8,128)S(1)}, f32[128,128]{1,0:T(8,128)}, u32[]{:S(2)}) copy-start(f32[128,128]{1,0:T(8,128)} %constant.12.clone.refs_1_) | copy-start | bytes 196612
  95.2 11.4 %copy-start.4 = (f32[16,128]{1,0:T(8,128)S(1)}, f32[16,128]{1,0:T(8,128)}, u32[]{:S(2)}) copy-start(f32[16,128]{1,0:T(8,128)} %constant.13.clone.refs_2_) | copy-start | bytes 24580
  95.2 11.3 %copy-start.5 = (f32[10,128]{1,0:T(8,128)S(1)}, f32[10,128]{1,0:T(8,128)}, u32[]{:S(2)}) copy-start(f32[10,128]{1,0:T(8,128)} %constant.14.clone.refs_3_) | copy-start | bytes 15364
  95.2 11.3 %copy-start.6 = (f32[10,128]{1,0:T(8,128)S(1)}, f32[10,128]{1,0:T(8,128)}, u32[]{:S(2)}) copy-start(f32[10,128]{1,0:T(8,128)} %constant.16.clone.refs_5_) | copy-start | bytes 15364

commit v3 on v2

--- a/solution.py
+++ b/solution.py
@@ -73,10 +73,8 @@
 
 
 def parting():
-    table = np.zeros((LANES, LANES), np.float32)
-    for z in range(LANES):
-        table[z, (z % 2) * 64 + z // 2] = 1.0
-    return table
+    rows, cols = iota((LANES, LANES), 0), iota((LANES, LANES), 1)
+    return jnp.where(cols == (rows % 2) * 64 + rows // 2, 1.0, 0.0)
 
 
 def unit_response():
@@ -188,8 +186,8 @@
         field.put(x, jnp.where(red, value, rest) if colour == 0 else jnp.where(red, rest, value))
 
 
-def part_kernel(density, potential, table, out, dscratch, pscratch):
-    t = table[...]
+def part_kernel(density, potential, out, dscratch, pscratch):
+    t = parting()
     dscratch[...] = dot(density[...].reshape(192, LANES) - SHIFT, t)
     pscratch[...] = dot(potential[...].reshape(192, LANES), t)
     low = iota((BY, LANES), 1) < 64
@@ -433,7 +431,7 @@
         self.ref[x + self.start] = value
 
 
-def last_kernel(got, qxz, inverse, tx, ty, tz, level, mid, fine, kept, table, out, eref, fref, oref, *, axes):
+def last_kernel(got, qxz, inverse, tx, ty, tz, level, mid, fine, kept, out, eref, fref, oref, *, axes):
     one, two = got[:, 0, :], got[:, 1, :]
     blocks = one + roll(roll(one, 64, 1), 1, 0) + roll(two, -1, 0)
     inside = iota((GY, LANES), 1) < GX * GZ
@@ -493,7 +491,7 @@
                     pair.append(value - mean * jnp.where(group, v[0][own], v[1][own]))
                 both = jnp.where(lane < 64, pair[0], roll(pair[1], 64, 1))
                 oref[pl.ds((2 * x + a) * 16 + b, 8, stride=2), :] = both
-    out[...] = dot_nt(oref[...], table[...]).reshape(12, 16, LANES)
+    out[...] = dot_nt(oref[...], parting()).reshape(12, 16, LANES)
 
 
 class Sources:
@@ -538,8 +536,7 @@
 
 def steps(density, potential):
     tables = [jnp.asarray(t) for t in coarse_tables()]
-    table = jnp.asarray(parting())
-    (own,) = run(part_kernel, [(6, 6, 8, LANES)], [density, potential, table], [(192, LANES)] * 2)
+    (own,) = run(part_kernel, [(6, 6, 8, LANES)], [density, potential], [(192, LANES)] * 2)
     xs = swapped(own, own, "gx")
     (shares,) = run(
         share_kernel,
@@ -568,7 +565,7 @@
     (out,) = run(
         place_kernel,
         [(12, 16, LANES)],
-        [blocks, *tables, level, mid, fine, kept, table],
+        [blocks, *tables, level, mid, fine, kept],
         [(18, 32, LANES), (80, 16, LANES), (192, LANES)],
     )
     return out

time: 110 us -> 109 us (level)
    unnamed x18 -> x14, local copies, waits for them, and re-layouts: 2.66 us -> 1.82 us
where the time goes in v3:
time: 109 us; the launch traced here: 108 us
  starting transfers between devices  56.1 us (51%)
  waiting for transfers between devices  23.7 us (22%)
  blocking collectives  18.1 us (17%)
  Pallas kernels  8.25 us (8%)
  local copies, waits for them, and re-layouts  1.82 us (2%)
    ppermute x5, starting transfers between devices, swapped(): return (got, lax.ppermute(second, axis, two))  33.1 us
    all_to_all x1, blocking collectives, everyone(): return lax.all_to_all(array, axis, 0, 0, tiled=True)  18.1 us
    ppermute x5, starting transfers between devices, swapped(): got = lax.ppermute(first, axis, one)  16.9 us
    ppermute x5, waiting for transfers between devices, swapped(): return (got, lax.ppermute(second, axis, two))  13 us
    all_to_all x1, waiting for transfers between devices, everyone(): return lax.all_to_all(array, axis, 0, 0, tiled=True)  10.7 us
    pallas_call x9, Pallas kernels, run(): pl.pallas_call(kernel, out_shape=[jax.ShapeDtypeStruct(s, F32) for s in s...  8.25 us
    all_to_all x1, starting transfers between devices, everyone(): return lax.all_to_all(array, axis, 0, 0, tiled=True)  6.1 us
  transfers between devices with their start and end apart: 11, of which 5 were waited for; matrix products, arithmetic and copies ran while one was open for 0% of the time, Pallas kernels for 3%

profile of v3, /device:TPU:1, one launch (start us, length us, event | category | flops | bytes accessed | tf_op | source)
XLA Modules:
  0.0 108.2 jit_solution(17672474901207189396)
XLA Ops:
  0.0 0.9 copy-done.5
  0.9 0.9 copy-done.6
  1.8 0.3 shard_map.73.pairs.own
  2.1 4.0 %collective-permute-start = (f32[6,6,8,128]{3,2,1,0:T(8,128)S(1)}, f32[6,6,8,128]{3,2,1,0:T(8,128)S(1)}, u32[]{:S(2)}, u32[]{:S(2)}) collective-permute-start(f32[6,6,8,128]{3,2,1,0:T(8,128)S(1)} %shard_map.73.pairs.own), channel_id=1, source_target_pairs={{0,128},{128,0},{256,384},{384,256},{512,640},{640,512},{768,896},... | collective-permute-start | bytes 442376 | tf_op jit(solution)/shard_map/ppermute | solution.py:529
  6.2 4.9 %collective-permute-start.1 = (f32[6,6,8,128]{3,2,1,0:T(8,128)S(1)}, f32[6,6,8,128]{3,2,1,0:T(8,128)S(1)}, u32[]{:S(2)}, u32[]{:S(2)}) collective-permute-start(f32[6,6,8,128]{3,2,1,0:T(8,128)S(1)} %shard_map.73.pairs.own), channel_id=1, source_target_pairs={{0,896},{128,256},{256,128},{384,512},{512,384},{640,768},{768,640... | collective-permute-start | bytes 442376 | tf_op jit(solution)/shard_map/ppermute | solution.py:530
  11.0 2.5 %collective-permute-done.1.xb = f32[6,6,8,128]{3,2,1,0:T(8,128)S(1)} collective-permute-done((f32[6,6,8,128]{3,2,1,0:T(8,128)S(1)}, f32[6,6,8,128]{3,2,1,0:T(8,128)S(1)}, u32[]{:S(2)}, u32[]{:S(2)}) %collective-permute-start.1) | collective-permute-done | bytes 147488 | tf_op jit(solution)/shard_map/ppermute | solution.py:530
  13.6 0.1 shard_map.76
  13.6 4.7 %collective-permute-start.2 = (f32[6,18,4,128]{3,2,1,0:T(4,128)S(1)}, f32[6,18,4,128]{3,2,1,0:T(4,128)S(1)}, u32[]{:S(2)}, u32[]{:S(2)}) collective-permute-start(f32[6,18,4,128]{3,2,1,0:T(4,128)S(1)} %get-tuple-element.17), channel_id=1, source_target_pairs={{0,8},{8,0},{16,24},{24,16},{32,40},{40,32},{48,56},{56,48},{64,72... | collective-permute-start | bytes 663560 | tf_op jit(solution)/shard_map/ppermute | solution.py:529
  18.4 16.1 %collective-permute-start.3 = (f32[6,18,4,128]{3,2,1,0:T(4,128)S(1)}, f32[6,18,4,128]{3,2,1,0:T(4,128)S(1)}, u32[]{:S(2)}, u32[]{:S(2)}) collective-permute-start(f32[6,18,4,128]{3,2,1,0:T(4,128)S(1)} %get-tuple-element.18), channel_id=1, source_target_pairs={{0,120},{8,16},{16,8},{24,32},{32,24},{40,48},{48,40},{56,64},{64,... | collective-permute-start | bytes 663560 | tf_op jit(solution)/shard_map/ppermute | solution.py:530
  34.5 4.0 %collective-permute-done.3.yb = f32[6,18,4,128]{3,2,1,0:T(4,128)S(1)} collective-permute-done((f32[6,18,4,128]{3,2,1,0:T(4,128)S(1)}, f32[6,18,4,128]{3,2,1,0:T(4,128)S(1)}, u32[]{:S(2)}, u32[]{:S(2)}) %collective-permute-start.3) | collective-permute-done | bytes 221216 | tf_op jit(solution)/shard_map/ppermute | solution.py:530
  38.5 0.5 shard_map.77
  39.0 4.3 %collective-permute-start.4 = (f32[27,16,128]{2,1,0:T(8,128)S(1)}, f32[27,16,128]{2,1,0:T(8,128)S(1)}, u32[]{:S(2)}, u32[]{:S(2)}) collective-permute-start(f32[27,16,128]{2,1,0:T(8,128)S(1)} %get-tuple-element.19), channel_id=1, source_target_pairs={{0,1},{1,0},{2,3},{3,2},{4,5},{5,4},{6,7},{7,6},{8,9},{9,8},{10,11... | collective-permute-start | bytes 663560 | tf_op jit(solution)/shard_map/ppermute | solution.py:529
  43.3 3.0 %collective-permute-start.5 = (f32[27,16,128]{2,1,0:T(8,128)S(1)}, f32[27,16,128]{2,1,0:T(8,128)S(1)}, u32[]{:S(2)}, u32[]{:S(2)}) collective-permute-start(f32[27,16,128]{2,1,0:T(8,128)S(1)} %get-tuple-element.20), channel_id=1, source_target_pairs={{0,7},{1,2},{2,1},{3,4},{4,3},{5,6},{6,5},{7,0},{8,15},{9,10},{10,... | collective-permute-start | bytes 663560 | tf_op jit(solution)/shard_map/ppermute | solution.py:530
  46.3 4.5 %collective-permute-done.5.zb = f32[27,16,128]{2,1,0:T(8,128)S(1)} collective-permute-done((f32[27,16,128]{2,1,0:T(8,128)S(1)}, f32[27,16,128]{2,1,0:T(8,128)S(1)}, u32[]{:S(2)}, u32[]{:S(2)}) %collective-permute-start.5) | collective-permute-done | bytes 221216 | tf_op jit(solution)/shard_map/ppermute | solution.py:530
  50.8 1.7 %shard_map.78 = (f32[12,16,128]{2,1,0:T(8,128)S(1)}, f32[8,10,16,128]{3,2,1,0:T(8,128)S(1)}, f32[8,10,16,128]{3,2,1,0:T(8,128)S(1)}) custom-call(f32[6,6,8,128]{3,2,1,0:T(8,128)S(1)} %shard_map.73.pairs.own, f32[6,6,8,128]{3,2,1,0:T(8,128)S(1)} %collective-permute-done.xa, f32[6,6,8,128]{3,2,1,0:T(8,128)S(1)} %collective-permute-done.1.xb, ...), custom_call_target="tpu_custom_call" | custom-call | flops 500000000 | bytes 1409024 | tf_op jit(solution)/shard_map/pallas_call | solution.py:509
  52.5 1.9 %collective-permute-start.6 = (f32[12,16,128]{2,1,0:T(8,128)S(1)}, f32[12,16,128]{2,1,0:T(8,128)S(1)}, u32[]{:S(2)}, u32[]{:S(2)}) collective-permute-start(f32[12,16,128]{2,1,0:T(8,128)S(1)} %get-tuple-element.21.own), channel_id=1, source_target_pairs={{0,8},{8,0},{16,24},{24,16},{32,40},{40,32},{48,56},{56,48},{64,72... | collective-permute-start | bytes 294920 | tf_op jit(solution)/shard_map/ppermute | solution.py:529
  54.5 4.6 %collective-permute-start.7 = (f32[12,16,128]{2,1,0:T(8,128)S(1)}, f32[12,16,128]{2,1,0:T(8,128)S(1)}, u32[]{:S(2)}, u32[]{:S(2)}) collective-permute-start(f32[12,16,128]{2,1,0:T(8,128)S(1)} %get-tuple-element.21.own), channel_id=1, source_target_pairs={{0,120},{8,16},{16,8},{24,32},{32,24},{40,48},{48,40},{56,64},{64,... | collective-permute-start | bytes 294920 | tf_op jit(solution)/shard_map/ppermute | solution.py:530
  59.1 2.0 %collective-permute-done.7.yb = f32[12,16,128]{2,1,0:T(8,128)S(1)} collective-permute-done((f32[12,16,128]{2,1,0:T(8,128)S(1)}, f32[12,16,128]{2,1,0:T(8,128)S(1)}, u32[]{:S(2)}, u32[]{:S(2)}) %collective-permute-start.7) | collective-permute-done | bytes 98336 | tf_op jit(solution)/shard_map/ppermute | solution.py:530
  61.1 1.9 %collective-permute-start.8 = (f32[9,32,128]{2,1,0:T(8,128)S(1)}, f32[9,32,128]{2,1,0:T(8,128)S(1)}, u32[]{:S(2)}, u32[]{:S(2)}) collective-permute-start(f32[9,32,128]{2,1,0:T(8,128)S(1)} %get-tuple-element.23), channel_id=1, source_target_pairs={{0,128},{128,0},{256,384},{384,256},{512,640},{640,512},{768,896},... | collective-permute-start | bytes 442376 | tf_op jit(solution)/shard_map/ppermute | solution.py:529
  63.0 4.5 %collective-permute-start.9 = (f32[9,32,128]{2,1,0:T(8,128)S(1)}, f32[9,32,128]{2,1,0:T(8,128)S(1)}, u32[]{:S(2)}, u32[]{:S(2)}) collective-permute-start(f32[9,32,128]{2,1,0:T(8,128)S(1)} %get-tuple-element.24), channel_id=1, source_target_pairs={{0,896},{128,256},{256,128},{384,512},{512,384},{640,768},{768,640... | collective-permute-start | bytes 442376 | tf_op jit(solution)/shard_map/ppermute | solution.py:530
  67.5 1.7 %shard_map.74 = f32[64,1,128]{2,1,0:T(1,128)S(1)} custom-call(f32[6,6,8,128]{3,2,1,0:T(8,128)S(1)} %shard_map.73.pairs.own), custom_call_target="tpu_custom_call" | custom-call | flops 500000000 | bytes 32768 | tf_op jit(solution)/shard_map/pallas_call | solution.py:509
  69.2 18.1 %all_to_all.10.got = f32[64,1,128]{2,1,0:T(1,128)S(1)} all-to-all(f32[64,1,128]{2,1,0:T(1,128)S(1)} %shard_map.74), channel_id=1, replica_groups=mesh['gx'=8,'gy'=16,'gz'=8] {'gx','gz'}, dimensions={0} | all-to-all | bytes 65536 | tf_op jit(solution)/shard_map/all_to_all | solution.py:534
  87.3 0.9 shard_map.75
  88.2 6.1 %all-to-all-start.1 = ((f32[16,2,128]{2,1,0:T(2,128)}), f32[16,2,128]{2,1,0:T(2,128)S(1)}, u32[]{:S(2)}, u32[]{:S(2)}) async-start(f32[16,2,128]{2,1,0:T(2,128)} %shard_map.75), calls=%async_computation.1 | async-start | bytes 32768 | tf_op jit(solution)/shard_map/all_to_all | solution.py:534
  94.3 0.0 copy-start
  94.3 0.0 copy-start.1
  94.4 0.0 copy-start.2
  94.4 0.0 copy-start.3
  94.4 0.0 copy-start.4
  94.4 0.6 shard_map.80
  95.0 10.7 %all-to-all-done.1.refs_0_ = f32[16,2,128]{2,1,0:T(2,128)S(1)} async-done(((f32[16,2,128]{2,1,0:T(2,128)}), f32[16,2,128]{2,1,0:T(2,128)S(1)}, u32[]{:S(2)}, u32[]{:S(2)}) %all-to-all-start.1) | async-done | bytes 16416 | tf_op jit(solution)/shard_map/all_to_all | solution.py:534
  105.7 2.5 %shard_map.81 = f32[12,16,128]{2,1,0:T(8,128)} custom-call(f32[16,2,128]{2,1,0:T(2,128)S(1)} %all-to-all-done.1.refs_0_, f32[128,128]{1,0:T(8,128)S(1)} %copy-done.1, f32[16,128]{1,0:T(8,128)S(1)} %copy-done.2, f32[10,128]{1,0:T(8,128)S(1)} %copy-done.3, f32[18,16,128]{2,1,0:T(8,128)S(1)} %copy-done, f32[10,128]{1,0:T(8,128)S(1)} %copy-done.4, ...), custom_call_target="tpu_custom_call" | custom-call | flops 500000000 | bytes 98304 | tf_op jit(solution)/shard_map/pallas_call | solution.py:509
  (14 shorter events, 0.1 us)
Async XLA Ops:
  0.0 0.9 copy-start.5
  0.9 0.9 copy-start.6
  2.1 8.9 %collective-permute-start = (f32[6,6,8,128]{3,2,1,0:T(8,128)S(1)}, f32[6,6,8,128]{3,2,1,0:T(8,128)S(1)}, u32[]{:S(2)}, u32[]{:S(2)}) collective-permute-start(f32[6,6,8,128]{3,2,1,0:T(8,128)S(1)} %shard_map.73.pairs.own), channel_id=1, source_target_pairs={{0,128},{128,0},{256,384},{384,256},{512,640},{640,512},{768,896},... | collective-permute-start | bytes 442376 | tf_op jit(solution)/shard_map/ppermute | solution.py:529
  6.2 7.4 %collective-permute-start.1 = (f32[6,6,8,128]{3,2,1,0:T(8,128)S(1)}, f32[6,6,8,128]{3,2,1,0:T(8,128)S(1)}, u32[]{:S(2)}, u32[]{:S(2)}) collective-permute-start(f32[6,6,8,128]{3,2,1,0:T(8,128)S(1)} %shard_map.73.pairs.own), channel_id=1, source_target_pairs={{0,896},{128,256},{256,128},{384,512},{512,384},{640,768},{768,640... | collective-permute-start | bytes 442376 | tf_op jit(solution)/shard_map/ppermute | solution.py:530
  13.6 20.9 %collective-permute-start.2 = (f32[6,18,4,128]{3,2,1,0:T(4,128)S(1)}, f32[6,18,4,128]{3,2,1,0:T(4,128)S(1)}, u32[]{:S(2)}, u32[]{:S(2)}) collective-permute-start(f32[6,18,4,128]{3,2,1,0:T(4,128)S(1)} %get-tuple-element.17), channel_id=1, source_target_pairs={{0,8},{8,0},{16,24},{24,16},{32,40},{40,32},{48,56},{56,48},{64,72... | collective-permute-start | bytes 663560 | tf_op jit(solution)/shard_map/ppermute | solution.py:529
  18.4 20.1 %collective-permute-start.3 = (f32[6,18,4,128]{3,2,1,0:T(4,128)S(1)}, f32[6,18,4,128]{3,2,1,0:T(4,128)S(1)}, u32[]{:S(2)}, u32[]{:S(2)}) collective-permute-start(f32[6,18,4,128]{3,2,1,0:T(4,128)S(1)} %get-tuple-element.18), channel_id=1, source_target_pairs={{0,120},{8,16},{16,8},{24,32},{32,24},{40,48},{48,40},{56,64},{64,... | collective-permute-start | bytes 663560 | tf_op jit(solution)/shard_map/ppermute | solution.py:530
  39.0 7.3 %collective-permute-start.4 = (f32[27,16,128]{2,1,0:T(8,128)S(1)}, f32[27,16,128]{2,1,0:T(8,128)S(1)}, u32[]{:S(2)}, u32[]{:S(2)}) collective-permute-start(f32[27,16,128]{2,1,0:T(8,128)S(1)} %get-tuple-element.19), channel_id=1, source_target_pairs={{0,1},{1,0},{2,3},{3,2},{4,5},{5,4},{6,7},{7,6},{8,9},{9,8},{10,11... | collective-permute-start | bytes 663560 | tf_op jit(solution)/shard_map/ppermute | solution.py:529
  43.3 7.5 %collective-permute-start.5 = (f32[27,16,128]{2,1,0:T(8,128)S(1)}, f32[27,16,128]{2,1,0:T(8,128)S(1)}, u32[]{:S(2)}, u32[]{:S(2)}) collective-permute-start(f32[27,16,128]{2,1,0:T(8,128)S(1)} %get-tuple-element.20), channel_id=1, source_target_pairs={{0,7},{1,2},{2,1},{3,4},{4,3},{5,6},{6,5},{7,0},{8,15},{9,10},{10,... | collective-permute-start | bytes 663560 | tf_op jit(solution)/shard_map/ppermute | solution.py:530
  52.5 6.5 %collective-permute-start.6 = (f32[12,16,128]{2,1,0:T(8,128)S(1)}, f32[12,16,128]{2,1,0:T(8,128)S(1)}, u32[]{:S(2)}, u32[]{:S(2)}) collective-permute-start(f32[12,16,128]{2,1,0:T(8,128)S(1)} %get-tuple-element.21.own), channel_id=1, source_target_pairs={{0,8},{8,0},{16,24},{24,16},{32,40},{40,32},{48,56},{56,48},{64,72... | collective-permute-start | bytes 294920 | tf_op jit(solution)/shard_map/ppermute | solution.py:529
  54.5 6.6 %collective-permute-start.7 = (f32[12,16,128]{2,1,0:T(8,128)S(1)}, f32[12,16,128]{2,1,0:T(8,128)S(1)}, u32[]{:S(2)}, u32[]{:S(2)}) collective-permute-start(f32[12,16,128]{2,1,0:T(8,128)S(1)} %get-tuple-element.21.own), channel_id=1, source_target_pairs={{0,120},{8,16},{16,8},{24,32},{32,24},{40,48},{48,40},{56,64},{64,... | collective-permute-start | bytes 294920 | tf_op jit(solution)/shard_map/ppermute | solution.py:530
  61.1 33.2 %collective-permute-start.8 = (f32[9,32,128]{2,1,0:T(8,128)S(1)}, f32[9,32,128]{2,1,0:T(8,128)S(1)}, u32[]{:S(2)}, u32[]{:S(2)}) collective-permute-start(f32[9,32,128]{2,1,0:T(8,128)S(1)} %get-tuple-element.23), channel_id=1, source_target_pairs={{0,128},{128,0},{256,384},{384,256},{512,640},{640,512},{768,896},... | collective-permute-start | bytes 442376 | tf_op jit(solution)/shard_map/ppermute | solution.py:529
  63.0 31.3 %collective-permute-start.9 = (f32[9,32,128]{2,1,0:T(8,128)S(1)}, f32[9,32,128]{2,1,0:T(8,128)S(1)}, u32[]{:S(2)}, u32[]{:S(2)}) collective-permute-start(f32[9,32,128]{2,1,0:T(8,128)S(1)} %get-tuple-element.24), channel_id=1, source_target_pairs={{0,896},{128,256},{256,128},{384,512},{512,384},{640,768},{768,640... | collective-permute-start | bytes 442376 | tf_op jit(solution)/shard_map/ppermute | solution.py:530
  88.2 17.5 %all-to-all-start.1 = ((f32[16,2,128]{2,1,0:T(2,128)}), f32[16,2,128]{2,1,0:T(2,128)S(1)}, u32[]{:S(2)}, u32[]{:S(2)}) async-start(f32[16,2,128]{2,1,0:T(2,128)} %shard_map.75), calls=%async_computation.1 | async-start | bytes 32768 | tf_op jit(solution)/shard_map/all_to_all | solution.py:534
  94.3 11.4 %copy-start = (f32[18,16,128]{2,1,0:T(8,128)S(1)}, f32[18,16,128]{2,1,0:T(8,128)}, u32[]{:S(2)}) copy-start(f32[18,16,128]{2,1,0:T(8,128)} %constant.13.clone.refs_4_) | copy-start | bytes 442372
  94.3 11.4 %copy-start.1 = (f32[128,128]{1,0:T(8,128)S(1)}, f32[128,128]{1,0:T(8,128)}, u32[]{:S(2)}) copy-start(f32[128,128]{1,0:T(8,128)} %constant.10.clone.refs_1_) | copy-start | bytes 196612
  94.4 11.4 %copy-start.2 = (f32[16,128]{1,0:T(8,128)S(1)}, f32[16,128]{1,0:T(8,128)}, u32[]{:S(2)}) copy-start(f32[16,128]{1,0:T(8,128)} %constant.11.clone.refs_2_) | copy-start | bytes 24580
  94.4 11.4 %copy-start.3 = (f32[10,128]{1,0:T(8,128)S(1)}, f32[10,128]{1,0:T(8,128)}, u32[]{:S(2)}) copy-start(f32[10,128]{1,0:T(8,128)} %constant.12.clone.refs_3_) | copy-start | bytes 15364
  94.4 11.3 %copy-start.4 = (f32[10,128]{1,0:T(8,128)S(1)}, f32[10,128]{1,0:T(8,128)}, u32[]{:S(2)}) copy-start(f32[10,128]{1,0:T(8,128)} %constant.14.clone.refs_5_) | copy-start | bytes 15364

commit v4 on v3

--- a/solution.py
+++ b/solution.py
@@ -349,21 +349,16 @@
         za[slot], zb[slot] = for_swaps("gz", lows, highs)
 
 
-def fine_kernel(own, xa, xb, ya, yb, za, zb, level, fine, kept, fref, sref):
+def fine_kernel(own, xa, xb, ya, yb, za, zb, level, rows, fine, kept, fref, sref):
     left, right = sides("gx", xa, xb)
     below, above = sides("gy", ya, yb)
     before, after = sides("gz", za, zb)
     source, field = Kept(sref), Kept(fref)
     lane = iota((16, LANES), 1)
-    home = {}
     for slot, members in groups():
-        for i, key in enumerate(members):
-            home[key] = (slot, i)
-    for array in range(6):
-        for x in range(-BX, 2 * BX):
+        up, down = after(slot), before(slot)
+        for i, (array, x) in enumerate(members):
             value = tall(own, left, right, below, above, array, x)
-            slot, i = home[(array, x)]
-            up, down = after(slot), before(slot)
             for c in (0, 1):
                 mine = roll(value, 64, 1) if c else value
                 right_rim = roll(up, 64 - 16 * i - 64 * c, 1)
@@ -379,12 +374,40 @@
                     field.put(((a, b, c), x), full)
     for step, depth in enumerate((10, 9, 8, 7)):
         fine_half(field, source, step % 2, depth)
-    for x in range(-3, BX + 3):
-        level[x + 3] = coarsened(field, source, x)
+    for x in range(12):
+        value = coarsened(field, source, x - 3)
+        level[x] = value
+        rows[x] = value[:8]
+        for at, row in ((x, 8), (12 + x, 15)):
+            rows[12 + at // 8, pl.ds(at % 8, 1), :] = value[row : row + 1]
     for n, cell in enumerate(CELLS):
         for x in range(-2, BX + 2):
             fine[n, x + 2] = field.get((cell, x))
             kept[n, x + 2] = source.get((cell, x))
+
+
+TILES = {k: 4 if k == 1 else 3 if k < 6 else 2 for k in range(1, 10)}
+FIRST = {k: sum(TILES[i] for i in range(1, k)) for k in TILES}
+
+
+def layer_tiles(value, k):
+    near = iota((8, LANES), 0) < 4
+    if TILES[k] == 4:
+        return [value[8 * i : 8 * i + 8] for i in range(4)]
+    if TILES[k] == 3:
+        return [value[:8], value[8:16], value[24:]]
+    return [value[:8], jnp.where(near, value[8:16], value[24:])]
+
+
+def tiled_layer(tiles, k):
+    near = iota((8, LANES), 0) < 4
+    nothing = jnp.zeros((8, LANES), F32)
+    got = [tiles(FIRST[k] + i) for i in range(TILES[k])]
+    if TILES[k] == 3:
+        got = [got[0], got[1], nothing, got[2]]
+    if TILES[k] == 2:
+        got = [got[0], jnp.where(near, got[1], 0.0), nothing, jnp.where(near, 0.0, got[1])]
+    return jnp.concatenate(got, 0)
 
 
 def level_y_kernel(own, ya, yb, wide, xa, xb):
@@ -392,22 +415,24 @@
     first = iota((8, LANES), 0) == 0
     last = iota((8, LANES), 0) == 7
     for x in range(12):
-        mine, down, up = own[x], below(x), above(x)
-        tail = jnp.where(first, up[8:16], 0.0)
-        lead = jnp.where(last, down[8:16], 0.0)
-        value = jnp.concatenate([mine[:8], up[:8], tail + lead, down[:8]], 0)
-        wide[x] = value
-    for x in range(9):
-        xa[x], xb[x] = for_swaps("gx", wide[x + 3], wide[x])
+        tail = above(12 + x // 8)[x % 8 : x % 8 + 1]
+        at = 12 + x
+        lead = below(12 + at // 8)[at % 8 : at % 8 + 1]
+        outer = jnp.where(first, tail, jnp.where(last, lead, 0.0))
+        wide[x] = jnp.concatenate([own[x][:8], above(x), outer, below(x)], 0)
+    for k in TILES:
+        pairs = zip(layer_tiles(wide[k + 2], k), layer_tiles(wide[9 - k], k))
+        for i, (low, high) in enumerate(pairs):
+            xa[FIRST[k] + i], xb[FIRST[k] + i] = for_swaps("gx", low, high)
 
 
 def mid_kernel(wide, xa, xb, level, mid, eref):
     left, right = sides("gx", xa, xb)
     for x in range(-9, BX + 9):
         if x < 0:
-            value = left(x + 9)
+            value = tiled_layer(left, -x)
         elif x >= BX:
-            value = right(x - BX)
+            value = tiled_layer(right, x - BX + 1)
         else:
             value = wide[x + 3]
         level[x + 9] = value
@@ -431,7 +456,7 @@
         self.ref[x + self.start] = value
 
 
-def last_kernel(got, qxz, inverse, tx, ty, tz, level, mid, fine, kept, out, eref, fref, oref, *, axes):
+def solve_kernel(got, qxz, inverse, tx, ty, tz, coarse, constant):
     one, two = got[:, 0, :], got[:, 1, :]
     blocks = one + roll(roll(one, 64, 1), 1, 0) + roll(two, -1, 0)
     inside = iota((GY, LANES), 1) < GX * GZ
@@ -445,7 +470,7 @@
     for y in range(GY):
         modes = plus(modes, half[y : y + 1, :] * ty[y + 1])
     modes = modes * inverse[...]
-    ix, iy, iz = axes
+    ix, iy, iz = (lax.axis_index(axis) for axis in ("gx", "gy", "gz"))
     own_lane = iota((LANES, LANES), 0)
     zrow = lambda d: tz[pl.ds(iz + 1 + d, 1), :]
     spread_z = jnp.where(own_lane < 64, zrow(0), jnp.where(own_lane < 96, zrow(1), zrow(-1)))
@@ -456,7 +481,12 @@
         for dx in (-1, 0, 1):
             both = line * tx[pl.ds(ix + 1 + dx, 1), :]
             stacked = jnp.where(place == 3 * (dx + 1) + dy + 1, both, stacked)
-    coarse = dot_nt(stacked, spread_z)
+    coarse[...] = dot_nt(stacked, spread_z)
+    constant[...] = jnp.broadcast_to(mean, (8, LANES))
+
+
+def place_kernel(solved, constant, level, mid, fine, kept, out, eref, fref, oref):
+    coarse, mean = solved[...], constant[...]
     row = iota((32, LANES), 0)
     error = Given(eref, 6, 18)
     for dx in (-1, 0, 1):
@@ -517,11 +547,6 @@
     )(*args)
 
 
-def place_kernel(*refs):
-    axes = (lax.axis_index("gx"), lax.axis_index("gy"), lax.axis_index("gz"))
-    last_kernel(*refs, axes=axes)
-
-
 def swapped(first, second, axis):
     count = lax.axis_size(axis)
     one = [(i, i ^ 1) for i in range(count)]
@@ -548,24 +573,25 @@
     blocks = everyone(plane, "gy")
     ys = swapped(*run(rim_y_kernel, [(6, 18, 4, LANES)] * 2, [own, *xs]), "gy")
     zs = swapped(*run(rim_z_kernel, [(27, 16, LANES)] * 2, [own, *xs, *ys]), "gz")
-    level, fine, kept = run(
+    level, rows, fine, kept = run(
         fine_kernel,
-        [(12, 16, LANES), (8, 10, 16, LANES), (8, 10, 16, LANES)],
+        [(12, 16, LANES), (15, 8, LANES), (8, 10, 16, LANES), (8, 10, 16, LANES)],
         [own, *xs, *ys, *zs],
         [(144, 16, LANES), (144, 16, LANES)],
     )
-    ys = swapped(level, level, "gy")
+    ys = swapped(rows, rows, "gy")
     wide, xa, xb = run(
-        level_y_kernel, [(12, 32, LANES), (9, 32, LANES), (9, 32, LANES)], [level, *ys]
+        level_y_kernel, [(12, 32, LANES), (24, 8, LANES), (24, 8, LANES)], [level, *ys]
     )
     xs = swapped(xa, xb, "gx")
     level, mid = run(
         mid_kernel, [(24, 32, LANES), (18, 32, LANES)], [wide, *xs], [(24, 32, LANES)]
     )
+    solved = run(solve_kernel, [(16, LANES), (8, LANES)], [blocks, *tables])
     (out,) = run(
         place_kernel,
         [(12, 16, LANES)],
-        [blocks, *tables, level, mid, fine, kept],
+        [*solved, level, mid, fine, kept],
         [(18, 32, LANES), (80, 16, LANES), (192, LANES)],
     )
     return out

time: 109 us -> 88.6 us (0.81)
  blocking collectives: 18.1 us -> 0 us
  waiting for transfers between devices: 23.7 us -> 12.9 us
  starting transfers between devices: 56.1 us -> 64.2 us
    all_to_all x1 -> x0, blocking collectives: 18.1 us -> none  [everyone(): return lax.all_to_all(array, axis, 0, 0, tiled=True)]
    all_to_all x1 -> x2, starting transfers between devices: 6.1 us -> 14.7 us  [everyone(): return lax.all_to_all(array, axis, 0, 0, tiled=True)]
    ppermute x5, waiting for transfers between devices: 13 us -> 6.48 us  [swapped(): return (got, lax.ppermute(second, axis, two))]
    all_to_all x1 -> x2, waiting for transfers between devices: 10.7 us -> 6.45 us  [everyone(): return lax.all_to_all(array, axis, 0, 0, tiled=True)]
    pallas_call x9 -> x10, Pallas kernels: 8.25 us -> 8.84 us  [run(): pl.pallas_call(kernel, out_shape=[jax.ShapeDtypeStruct(s, F32) for s in s...]
  transfers between devices with their start and end apart: 11 -> 12, of which waited for: 5 -> 4; matrix products, arithmetic and copies ran while one was open for 0% -> 0% of each run, Pallas kernels for 3% -> 6%
where the time goes in v4:
time: 88.6 us; the launch traced here: 88 us
  starting transfers between devices  64.2 us (72%)
  waiting for transfers between devices  12.9 us (15%)
  Pallas kernels  8.84 us (10%)
  local copies, waits for them, and re-layouts  1.82 us (2%)
    ppermute x5, starting transfers between devices, swapped(): return (got, lax.ppermute(second, axis, two))  32.1 us
    ppermute x5, starting transfers between devices, swapped(): got = lax.ppermute(first, axis, one)  17.4 us
    all_to_all x2, starting transfers between devices, everyone(): return lax.all_to_all(array, axis, 0, 0, tiled=True)  14.7 us
    pallas_call x10, Pallas kernels, run(): pl.pallas_call(kernel, out_shape=[jax.ShapeDtypeStruct(s, F32) for s in s...  8.84 us
    ppermute x5, waiting for transfers between devices, swapped(): return (got, lax.ppermute(second, axis, two))  6.48 us
    all_to_all x2, waiting for transfers between devices, everyone(): return lax.all_to_all(array, axis, 0, 0, tiled=True)  6.45 us
    unnamed x14, local copies, waits for them, and re-layouts  1.82 us
  transfers between devices with their start and end apart: 12, of which 4 were waited for; matrix products, arithmetic and copies ran while one was open for 0% of the time, Pallas kernels for 6%

profile of v4, /device:TPU:1, one launch (start us, length us, event | category | flops | bytes accessed | tf_op | source)
XLA Modules:
  0.0 88.0 jit_solution(11380837595746639822)
XLA Ops:
  0.0 0.9 %copy-done = f32[12,16,128]{2,1,0:T(8,128)S(1)} copy-done((f32[12,16,128]{2,1,0:T(8,128)S(1)}, f32[12,16,128]{2,1,0:T(8,128)}, u32[]{:S(2)}) %copy-start) | copy-done | bytes 98328
  0.9 0.9 %copy-done.1 = f32[12,16,128]{2,1,0:T(8,128)S(1)} copy-done((f32[12,16,128]{2,1,0:T(8,128)S(1)}, f32[12,16,128]{2,1,0:T(8,128)}, u32[]{:S(2)}) %copy-start.1) | copy-done | bytes 98328
  1.8 0.3 shard_map.73.pairs.own
  2.1 4.0 %collective-permute-start = (f32[6,6,8,128]{3,2,1,0:T(8,128)S(1)}, f32[6,6,8,128]{3,2,1,0:T(8,128)S(1)}, u32[]{:S(2)}, u32[]{:S(2)}) collective-permute-start(f32[6,6,8,128]{3,2,1,0:T(8,128)S(1)} %shard_map.73.pairs.own), channel_id=1, source_target_pairs={{0,128},{128,0},{256,384},{384,256},{512,640},{640,512},{768,896},... | collective-permute-start | bytes 442376 | tf_op jit(solution)/shard_map/ppermute | solution.py:554
  6.2 4.9 %collective-permute-start.1 = (f32[6,6,8,128]{3,2,1,0:T(8,128)S(1)}, f32[6,6,8,128]{3,2,1,0:T(8,128)S(1)}, u32[]{:S(2)}, u32[]{:S(2)}) collective-permute-start(f32[6,6,8,128]{3,2,1,0:T(8,128)S(1)} %shard_map.73.pairs.own), channel_id=1, source_target_pairs={{0,896},{128,256},{256,128},{384,512},{512,384},{640,768},{768,640... | collective-permute-start | bytes 442376 | tf_op jit(solution)/shard_map/ppermute | solution.py:555
  11.0 2.5 %collective-permute-done.1.xb = f32[6,6,8,128]{3,2,1,0:T(8,128)S(1)} collective-permute-done((f32[6,6,8,128]{3,2,1,0:T(8,128)S(1)}, f32[6,6,8,128]{3,2,1,0:T(8,128)S(1)}, u32[]{:S(2)}, u32[]{:S(2)}) %collective-permute-start.1) | collective-permute-done | bytes 147488 | tf_op jit(solution)/shard_map/ppermute | solution.py:555
  13.6 0.1 shard_map.77
  13.6 4.7 %collective-permute-start.2 = (f32[6,18,4,128]{3,2,1,0:T(4,128)S(1)}, f32[6,18,4,128]{3,2,1,0:T(4,128)S(1)}, u32[]{:S(2)}, u32[]{:S(2)}) collective-permute-start(f32[6,18,4,128]{3,2,1,0:T(4,128)S(1)} %get-tuple-element.22), channel_id=1, source_target_pairs={{0,8},{8,0},{16,24},{24,16},{32,40},{40,32},{48,56},{56,48},{64,72... | collective-permute-start | bytes 663560 | tf_op jit(solution)/shard_map/ppermute | solution.py:554
  18.4 16.1 %collective-permute-start.3 = (f32[6,18,4,128]{3,2,1,0:T(4,128)S(1)}, f32[6,18,4,128]{3,2,1,0:T(4,128)S(1)}, u32[]{:S(2)}, u32[]{:S(2)}) collective-permute-start(f32[6,18,4,128]{3,2,1,0:T(4,128)S(1)} %get-tuple-element.23), channel_id=1, source_target_pairs={{0,120},{8,16},{16,8},{24,32},{32,24},{40,48},{48,40},{56,64},{64,... | collective-permute-start | bytes 663560 | tf_op jit(solution)/shard_map/ppermute | solution.py:555
  34.5 4.0 %collective-permute-done.3.yb = f32[6,18,4,128]{3,2,1,0:T(4,128)S(1)} collective-permute-done((f32[6,18,4,128]{3,2,1,0:T(4,128)S(1)}, f32[6,18,4,128]{3,2,1,0:T(4,128)S(1)}, u32[]{:S(2)}, u32[]{:S(2)}) %collective-permute-start.3) | collective-permute-done | bytes 221216 | tf_op jit(solution)/shard_map/ppermute | solution.py:555
  38.5 0.5 shard_map.78
  39.0 4.3 %collective-permute-start.4 = (f32[27,16,128]{2,1,0:T(8,128)S(1)}, f32[27,16,128]{2,1,0:T(8,128)S(1)}, u32[]{:S(2)}, u32[]{:S(2)}) collective-permute-start(f32[27,16,128]{2,1,0:T(8,128)S(1)} %get-tuple-element.24), channel_id=1, source_target_pairs={{0,1},{1,0},{2,3},{3,2},{4,5},{5,4},{6,7},{7,6},{8,9},{9,8},{10,11... | collective-permute-start | bytes 663560 | tf_op jit(solution)/shard_map/ppermute | solution.py:554
  43.3 3.0 %collective-permute-start.5 = (f32[27,16,128]{2,1,0:T(8,128)S(1)}, f32[27,16,128]{2,1,0:T(8,128)S(1)}, u32[]{:S(2)}, u32[]{:S(2)}) collective-permute-start(f32[27,16,128]{2,1,0:T(8,128)S(1)} %get-tuple-element.25), channel_id=1, source_target_pairs={{0,7},{1,2},{2,1},{3,4},{4,3},{5,6},{6,5},{7,0},{8,15},{9,10},{10,... | collective-permute-start | bytes 663560 | tf_op jit(solution)/shard_map/ppermute | solution.py:555
  46.3 2.3 %shard_map.74 = f32[64,1,128]{2,1,0:T(1,128)} custom-call(f32[6,6,8,128]{3,2,1,0:T(8,128)S(1)} %shard_map.73.pairs.own), custom_call_target="tpu_custom_call" | custom-call | flops 500000000 | bytes 32768 | tf_op jit(solution)/shard_map/pallas_call | solution.py:539
  48.6 8.5 %all-to-all-start = ((f32[64,1,128]{2,1,0:T(1,128)}), f32[64,1,128]{2,1,0:T(1,128)S(1)}, u32[]{:S(2)}, u32[]{:S(2)}) async-start(f32[64,1,128]{2,1,0:T(1,128)} %shard_map.74), calls=%async_computation | async-start | bytes 65536 | tf_op jit(solution)/shard_map/all_to_all | solution.py:559
  57.1 1.7 %shard_map.79 = (f32[12,16,128]{2,1,0:T(8,128)S(1)}, f32[15,8,128]{2,1,0:T(8,128)S(1)}, f32[8,10,16,128]{3,2,1,0:T(8,128)S(1)}, f32[8,10,16,128]{3,2,1,0:T(8,128)S(1)}) custom-call(f32[6,6,8,128]{3,2,1,0:T(8,128)S(1)} %shard_map.73.pairs.own, f32[6,6,8,128]{3,2,1,0:T(8,128)S(1)} %collective-permute-done.xa, f32[6,6,8,128]{3,2,1,0:T(8,128)S(1)} %collective-permute-done.1.xb, ...), custom_call_target="tpu_custom_call" | custom-call | flops 500000000 | bytes 1470464 | tf_op jit(solution)/shard_map/pallas_call | solution.py:539
  58.8 1.9 %collective-permute-start.6 = (f32[15,8,128]{2,1,0:T(8,128)S(1)}, f32[15,8,128]{2,1,0:T(8,128)S(1)}, u32[]{:S(2)}, u32[]{:S(2)}) collective-permute-start(f32[15,8,128]{2,1,0:T(8,128)S(1)} %get-tuple-element.27), channel_id=1, source_target_pairs={{0,8},{8,0},{16,24},{24,16},{32,40},{40,32},{48,56},{56,48},{64,72... | collective-permute-start | bytes 184328 | tf_op jit(solution)/shard_map/ppermute | solution.py:554
  60.8 4.8 %collective-permute-start.7 = (f32[15,8,128]{2,1,0:T(8,128)S(1)}, f32[15,8,128]{2,1,0:T(8,128)S(1)}, u32[]{:S(2)}, u32[]{:S(2)}) collective-permute-start(f32[15,8,128]{2,1,0:T(8,128)S(1)} %get-tuple-element.27), channel_id=1, source_target_pairs={{0,120},{8,16},{16,8},{24,32},{32,24},{40,48},{48,40},{56,64},{64,... | collective-permute-start | bytes 184328 | tf_op jit(solution)/shard_map/ppermute | solution.py:555
  65.5 0.9 all-to-all-done.got
  66.4 0.9 shard_map.75
  67.3 6.3 %all-to-all-start.1 = ((f32[16,2,128]{2,1,0:T(2,128)}), f32[16,2,128]{2,1,0:T(2,128)S(1)}, u32[]{:S(2)}, u32[]{:S(2)}) async-start(f32[16,2,128]{2,1,0:T(2,128)} %shard_map.75), calls=%async_computation.1 | async-start | bytes 32768 | tf_op jit(solution)/shard_map/all_to_all | solution.py:559
  73.6 0.0 copy-start.2
  73.6 0.0 copy-start.3
  73.6 0.0 copy-start.4
  73.6 0.0 copy-start.5
  73.6 0.0 copy-start.6
  73.7 2.4 %collective-permute-start.8 = (f32[24,8,128]{2,1,0:T(8,128)S(1)}, f32[24,8,128]{2,1,0:T(8,128)S(1)}, u32[]{:S(2)}, u32[]{:S(2)}) collective-permute-start(f32[24,8,128]{2,1,0:T(8,128)S(1)} %get-tuple-element.29), channel_id=1, source_target_pairs={{0,128},{128,0},{256,384},{384,256},{512,640},{640,512},{768,896},... | collective-permute-start | bytes 294920 | tf_op jit(solution)/shard_map/ppermute | solution.py:554
  76.1 3.3 %collective-permute-start.9 = (f32[24,8,128]{2,1,0:T(8,128)S(1)}, f32[24,8,128]{2,1,0:T(8,128)S(1)}, u32[]{:S(2)}, u32[]{:S(2)}) collective-permute-start(f32[24,8,128]{2,1,0:T(8,128)S(1)} %get-tuple-element.30), channel_id=1, source_target_pairs={{0,896},{128,256},{256,128},{384,512},{512,384},{640,768},{768,640... | collective-permute-start | bytes 294920 | tf_op jit(solution)/shard_map/ppermute | solution.py:555
  79.4 5.6 %all-to-all-done.1.got = f32[16,2,128]{2,1,0:T(2,128)S(1)} async-done(((f32[16,2,128]{2,1,0:T(2,128)}), f32[16,2,128]{2,1,0:T(2,128)S(1)}, u32[]{:S(2)}, u32[]{:S(2)}) %all-to-all-start.1) | async-done | bytes 16416 | tf_op jit(solution)/shard_map/all_to_all | solution.py:559
  85.0 0.7 shard_map.76
  85.7 0.7 shard_map.81
  86.3 1.7 %shard_map.82 = f32[12,16,128]{2,1,0:T(8,128)} custom-call(f32[16,128]{1,0:T(8,128)S(1)} %get-tuple-element.20.solved, f32[8,128]{1,0:T(8,128)S(1)} %get-tuple-element.21.constant, f32[24,32,128]{2,1,0:T(8,128)S(1)} %get-tuple-element.31.level, f32[18,32,128]{2,1,0:T(8,128)S(1)} %get-tuple-element.32.mid, f32[8,10,16,128]{3,2,1,0:T(8,128)S(1)} %get-tuple-element.33.fine, ...), custom_call_target="tpu_custom_call" | custom-call | flops 500000000 | bytes 98304 | tf_op jit(solution)/shard_map/pallas_call | solution.py:539
  (16 shorter events, 0.1 us)
Async XLA Ops:
  0.0 0.9 %copy-start = (f32[12,16,128]{2,1,0:T(8,128)S(1)}, f32[12,16,128]{2,1,0:T(8,128)}, u32[]{:S(2)}) copy-start(f32[12,16,128]{2,1,0:T(8,128)} %density.1) | copy-start | bytes 294916
  0.9 0.9 %copy-start.1 = (f32[12,16,128]{2,1,0:T(8,128)S(1)}, f32[12,16,128]{2,1,0:T(8,128)}, u32[]{:S(2)}) copy-start(f32[12,16,128]{2,1,0:T(8,128)} %potential.1) | copy-start | bytes 294916
  2.1 8.9 %collective-permute-start = (f32[6,6,8,128]{3,2,1,0:T(8,128)S(1)}, f32[6,6,8,128]{3,2,1,0:T(8,128)S(1)}, u32[]{:S(2)}, u32[]{:S(2)}) collective-permute-start(f32[6,6,8,128]{3,2,1,0:T(8,128)S(1)} %shard_map.73.pairs.own), channel_id=1, source_target_pairs={{0,128},{128,0},{256,384},{384,256},{512,640},{640,512},{768,896},... | collective-permute-start | bytes 442376 | tf_op jit(solution)/shard_map/ppermute | solution.py:554
  6.2 7.4 %collective-permute-start.1 = (f32[6,6,8,128]{3,2,1,0:T(8,128)S(1)}, f32[6,6,8,128]{3,2,1,0:T(8,128)S(1)}, u32[]{:S(2)}, u32[]{:S(2)}) collective-permute-start(f32[6,6,8,128]{3,2,1,0:T(8,128)S(1)} %shard_map.73.pairs.own), channel_id=1, source_target_pairs={{0,896},{128,256},{256,128},{384,512},{512,384},{640,768},{768,640... | collective-permute-start | bytes 442376 | tf_op jit(solution)/shard_map/ppermute | solution.py:555
  13.6 20.9 %collective-permute-start.2 = (f32[6,18,4,128]{3,2,1,0:T(4,128)S(1)}, f32[6,18,4,128]{3,2,1,0:T(4,128)S(1)}, u32[]{:S(2)}, u32[]{:S(2)}) collective-permute-start(f32[6,18,4,128]{3,2,1,0:T(4,128)S(1)} %get-tuple-element.22), channel_id=1, source_target_pairs={{0,8},{8,0},{16,24},{24,16},{32,40},{40,32},{48,56},{56,48},{64,72... | collective-permute-start | bytes 663560 | tf_op jit(solution)/shard_map/ppermute | solution.py:554
  18.4 20.1 %collective-permute-start.3 = (f32[6,18,4,128]{3,2,1,0:T(4,128)S(1)}, f32[6,18,4,128]{3,2,1,0:T(4,128)S(1)}, u32[]{:S(2)}, u32[]{:S(2)}) collective-permute-start(f32[6,18,4,128]{3,2,1,0:T(4,128)S(1)} %get-tuple-element.23), channel_id=1, source_target_pairs={{0,120},{8,16},{16,8},{24,32},{32,24},{40,48},{48,40},{56,64},{64,... | collective-permute-start | bytes 663560 | tf_op jit(solution)/shard_map/ppermute | solution.py:555
  39.0 18.1 %collective-permute-start.4 = (f32[27,16,128]{2,1,0:T(8,128)S(1)}, f32[27,16,128]{2,1,0:T(8,128)S(1)}, u32[]{:S(2)}, u32[]{:S(2)}) collective-permute-start(f32[27,16,128]{2,1,0:T(8,128)S(1)} %get-tuple-element.24), channel_id=1, source_target_pairs={{0,1},{1,0},{2,3},{3,2},{4,5},{5,4},{6,7},{7,6},{8,9},{9,8},{10,11... | collective-permute-start | bytes 663560 | tf_op jit(solution)/shard_map/ppermute | solution.py:554
  43.3 13.8 %collective-permute-start.5 = (f32[27,16,128]{2,1,0:T(8,128)S(1)}, f32[27,16,128]{2,1,0:T(8,128)S(1)}, u32[]{:S(2)}, u32[]{:S(2)}) collective-permute-start(f32[27,16,128]{2,1,0:T(8,128)S(1)} %get-tuple-element.25), channel_id=1, source_target_pairs={{0,7},{1,2},{2,1},{3,4},{4,3},{5,6},{6,5},{7,0},{8,15},{9,10},{10,... | collective-permute-start | bytes 663560 | tf_op jit(solution)/shard_map/ppermute | solution.py:555
  48.6 17.8 %all-to-all-start = ((f32[64,1,128]{2,1,0:T(1,128)}), f32[64,1,128]{2,1,0:T(1,128)S(1)}, u32[]{:S(2)}, u32[]{:S(2)}) async-start(f32[64,1,128]{2,1,0:T(1,128)} %shard_map.74), calls=%async_computation | async-start | bytes 65536 | tf_op jit(solution)/shard_map/all_to_all | solution.py:559
  58.8 14.7 %collective-permute-start.6 = (f32[15,8,128]{2,1,0:T(8,128)S(1)}, f32[15,8,128]{2,1,0:T(8,128)S(1)}, u32[]{:S(2)}, u32[]{:S(2)}) collective-permute-start(f32[15,8,128]{2,1,0:T(8,128)S(1)} %get-tuple-element.27), channel_id=1, source_target_pairs={{0,8},{8,0},{16,24},{24,16},{32,40},{40,32},{48,56},{56,48},{64,72... | collective-permute-start | bytes 184328 | tf_op jit(solution)/shard_map/ppermute | solution.py:554
  60.8 12.8 %collective-permute-start.7 = (f32[15,8,128]{2,1,0:T(8,128)S(1)}, f32[15,8,128]{2,1,0:T(8,128)S(1)}, u32[]{:S(2)}, u32[]{:S(2)}) collective-permute-start(f32[15,8,128]{2,1,0:T(8,128)S(1)} %get-tuple-element.27), channel_id=1, source_target_pairs={{0,120},{8,16},{16,8},{24,32},{32,24},{40,48},{48,40},{56,64},{64,... | collective-permute-start | bytes 184328 | tf_op jit(solution)/shard_map/ppermute | solution.py:555
  67.3 17.7 %all-to-all-start.1 = ((f32[16,2,128]{2,1,0:T(2,128)}), f32[16,2,128]{2,1,0:T(2,128)S(1)}, u32[]{:S(2)}, u32[]{:S(2)}) async-start(f32[16,2,128]{2,1,0:T(2,128)} %shard_map.75), calls=%async_computation.1 | async-start | bytes 32768 | tf_op jit(solution)/shard_map/all_to_all | solution.py:559
  73.6 11.4 %copy-start.2 = (f32[18,16,128]{2,1,0:T(8,128)S(1)}, f32[18,16,128]{2,1,0:T(8,128)}, u32[]{:S(2)}) copy-start(f32[18,16,128]{2,1,0:T(8,128)} %constant.13.clone.ty) | copy-start | bytes 442372
  73.6 11.4 %copy-start.3 = (f32[128,128]{1,0:T(8,128)S(1)}, f32[128,128]{1,0:T(8,128)}, u32[]{:S(2)}) copy-start(f32[128,128]{1,0:T(8,128)} %constant.10.clone.qxz) | copy-start | bytes 196612
  73.6 11.4 %copy-start.4 = (f32[16,128]{1,0:T(8,128)S(1)}, f32[16,128]{1,0:T(8,128)}, u32[]{:S(2)}) copy-start(f32[16,128]{1,0:T(8,128)} %constant.11.clone.inverse) | copy-start | bytes 24580
  73.6 11.4 %copy-start.5 = (f32[10,128]{1,0:T(8,128)S(1)}, f32[10,128]{1,0:T(8,128)}, u32[]{:S(2)}) copy-start(f32[10,128]{1,0:T(8,128)} %constant.12.clone.tx) | copy-start | bytes 15364
  73.6 11.3 %copy-start.6 = (f32[10,128]{1,0:T(8,128)S(1)}, f32[10,128]{1,0:T(8,128)}, u32[]{:S(2)}) copy-start(f32[10,128]{1,0:T(8,128)} %constant.14.clone.tz) | copy-start | bytes 15364
  73.7 12.0 %collective-permute-start.8 = (f32[24,8,128]{2,1,0:T(8,128)S(1)}, f32[24,8,128]{2,1,0:T(8,128)S(1)}, u32[]{:S(2)}, u32[]{:S(2)}) collective-permute-start(f32[24,8,128]{2,1,0:T(8,128)S(1)} %get-tuple-element.29), channel_id=1, source_target_pairs={{0,128},{128,0},{256,384},{384,256},{512,640},{640,512},{768,896},... | collective-permute-start | bytes 294920 | tf_op jit(solution)/shard_map/ppermute | solution.py:554
  76.1 9.6 %collective-permute-start.9 = (f32[24,8,128]{2,1,0:T(8,128)S(1)}, f32[24,8,128]{2,1,0:T(8,128)S(1)}, u32[]{:S(2)}, u32[]{:S(2)}) collective-permute-start(f32[24,8,128]{2,1,0:T(8,128)S(1)} %get-tuple-element.30), channel_id=1, source_target_pairs={{0,896},{128,256},{256,128},{384,512},{512,384},{640,768},{768,640... | collective-permute-start | bytes 294920 | tf_op jit(solution)/shard_map/ppermute | solution.py:555

commit v5 on v3

--- a/solution.py
+++ b/solution.py
@@ -1,3 +1,5 @@
+import functools
+
 import jax
 import jax.numpy as jnp
 import numpy as np
@@ -209,15 +211,13 @@
     return 4 + cell[0], cell[2]
 
 
-def share_kernel(pairs, out, fref, sref, eref, lref, stack):
+def spread_kernel(pairs, level, xa, xb, xxa, xxb, fref, sref):
     own = iota((BY, LANES), 1) < 64
     source, field = Kept(sref), Kept(fref)
     nothing = jnp.zeros((BY, LANES), F32)
-    mass = None
     for cell in CELLS:
         for x in range(BX):
             value = pairs[source_slot(cell), x]
-            mass = plus(mass, value) if cell[2] == 0 else mass
             if cell[2]:
                 value = roll(value, 64, 1)
             source.put((cell, x), jnp.concatenate([jnp.where(own, value, 0.0), nothing], 0))
@@ -229,10 +229,32 @@
                 field.put((cell, x), jnp.concatenate([jnp.where(own, value, 0.0), nothing], 0))
     for step in range(4):
         fine_half(field, source, step % 2, step + 1)
+    for x in range(12):
+        value = coarsened(field, source, x - 3)
+        level[x] = value
+        for t in (0, 1):
+            xa[2 * x + t] = value[8 * t : 8 * t + 8]
+            xb[2 * x + t] = value[8 * t : 8 * t + 8]
+    for array in range(6):
+        for q in range(4):
+            at = 24 + 4 * array + q
+            xa[at], xb[at] = for_swaps("gx", pairs[array, q], pairs[array, 2 + q])
+    for x in range(6):
+        low, high = level[x], level[x + 6]
+        for t in (0, 1):
+            rows = slice(8 * t, 8 * t + 8)
+            xxa[2 * x + t], xxb[2 * x + t] = for_swaps("gx", low[rows], high[rows], 2)
+
+
+def share_kernel(pairs, given, out, eref, lref, stack):
+    mass = None
+    for cell in CELLS:
+        for x in range(BX):
+            mass = plus(mass, pairs[source_slot(cell), x]) if cell[2] == 0 else mass
     level, error = Kept(lref), Kept(eref)
     near = iota((BY, LANES), 0) < 4
     for x in range(-3, BX + 3):
-        value = coarsened(field, source, x)
+        value = given[x + 3]
         top, rim = value[:BY], value[BY:]
         level.put(x, jnp.concatenate([top, jnp.where(near, rim, 0.0), jnp.where(near, 0.0, rim)], 0))
     masks = [red_of((24, LANES), x) for x in (0, 1)]
@@ -257,40 +279,34 @@
     summed = jnp.where((rows == 15) & (cols >= 64), 0.0, summed)
     sent = dot_nt(jnp.where(pick, 1.0, 0.0), summed)
     flat = sent[0:1] + roll(sent[1:2], 16, 1) + roll(sent[2:3], 32, 1)
+    for peer in range(GY):
+        out[peer] = flat
+
+
+def along_y_kernel(got, out):
+    values = got[:, 0, :]
+    lane = iota((GY, LANES), 1)
+    slot = lane % 16
+    total = jnp.where((slot % 3 == 0) | (slot == 15), values, 0.0)
+    total = total + roll(jnp.where(slot % 3 == 1, values, 0.0), 1, 0)
+    total = total + roll(jnp.where(slot % 3 == 2, values, 0.0), -1, 0)
+    rows, cols = iota((LANES, LANES), 0), iota((LANES, LANES), 1)
+    kind = jnp.where(rows % 16 == 15, 15, (rows // 16) * 5 + (rows % 16) // 3)
+    take = (rows < 48) & (cols % 16 == kind) & ((rows % 16 < 15) | (rows == 15))
+    tiled = dot(total, jnp.where(take, 1.0, 0.0))
+    picked = jnp.where(lane // 16 == iota((GY, LANES), 0) % 8, tiled, 0.0)
+    sent = [jnp.sum(picked[8 * r : 8 * r + 8], axis=0, keepdims=True) for r in (0, 1)]
+    sent = jnp.concatenate(sent, 0)
     for peer in range(GX * GZ):
-        out[peer] = flat
-
-
-def along_xz_kernel(got, out):
-    values = got[:, 0, :]
-    lane = iota((GZ, LANES), 1)
-    part, slot = lane // 16, lane % 16
-    lines = []
-    for i in range(GX):
-        line = values[GZ * i : GZ * i + GZ]
-        total = jnp.where(part == 0, line, 0.0)
-        total = total + roll(jnp.where(part == 1, line, 0.0), 1, 0)
-        lines.append(total + roll(jnp.where(part == 2, line, 0.0), -1, 0))
-    rows = []
-    for i in range(GX):
-        total = jnp.where(slot == 15, lines[i], 0.0)
-        for r in range(5):
-            total = jnp.where((slot < 15) & (slot // 3 == r), lines[(i - (r - 2)) % GX], total)
-        rows.append(total)
-    total = jnp.concatenate(rows + rows, 0)
-    row, col = iota((8, LANES), 0), iota((8, LANES), 1)
-    take = (col < 48) & (col % 16 < 15) & ((col % 16) % 3 == row)
-    take = take | ((row == 3) & (col == 15))
-    sums = dot_nt(jnp.where(take, 1.0, 0.0), total)
-    first = iota((1, LANES), 1) < 64
-    sent = [jnp.where(first, sums[0:1], sums[1:2]), jnp.where(first, sums[2:3], sums[3:4])]
-    sent = jnp.concatenate(sent, 0)
-    for peer in range(GY):
         out[peer] = sent
 
 
-def sides(axis, first, second):
-    odd = lax.axis_index(axis) % 2 == 1
+def upper_half(axis, step):
+    return (lax.axis_index(axis) // step) % 2 == 1
+
+
+def sides(axis, first, second, step=1):
+    odd = upper_half(axis, step)
 
     def pick(swap):
         return lambda *at: jnp.where(odd != swap, first[at], second[at])
@@ -298,119 +314,197 @@
     return pick(False), pick(True)
 
 
-def for_swaps(axis, low, high):
-    odd = lax.axis_index(axis) % 2 == 1
+def for_swaps(axis, low, high, step=1):
+    odd = upper_half(axis, step)
     return jnp.where(odd, low, high), jnp.where(odd, high, low)
 
 
-def wide_x(own, left, right, array, x):
+RAW = range(-4, BX + 4)
+FAR = {"up": (5, 6, 7, 0), "down": (7, 0, 1, 2)}
+
+
+def lies(shape, rows):
+    row = iota(shape, 0)
+    return functools.reduce(lambda a, b: a | b, [row == r for r in rows])
+
+
+def wide_raw(own, left, right, array, x):
     if x < 0:
-        return left(array, x + BX)
+        return left(24 + 4 * array + x + 4)
     if x >= BX:
-        return right(array, x - BX)
+        return right(24 + 4 * array + x - BX)
     return own[array, x]
 
 
-def rim_y_kernel(own, xa, xb, ya, yb):
+def join_x_kernel(own, level, xa, xb, xxa, xxb, wide, ya, yb, yya, yyb):
     left, right = sides("gx", xa, xb)
+    left2, right2 = sides("gx", xxa, xxb, 2)
+    for x in range(-9, BX + 9):
+        for t in (0, 1):
+            value = level[x + 3, pl.ds(8 * t, 8), :] if -3 <= x < 9 else None
+            if x < 3:
+                value = plus(value, left(2 * (x + 9) + t))
+            else:
+                value = plus(value, right(2 * (x - 3) + t))
+            if x < -3:
+                value = value + left2(2 * (x + 9) + t)
+            if x >= 9:
+                value = value + right2(2 * (x - 9) + t)
+            wide[x + 9, pl.ds(8 * t, 8), :] = value
+            ya[2 * (x + 9) + t] = value
+            yb[2 * (x + 9) + t] = value
+    shape = (8, LANES)
+    near = iota(shape, 0) < 4
     for array in range(6):
-        for x in range(-BX, 2 * BX):
-            value = wide_x(own, left, right, array, x)
-            ya[array, x + BX], yb[array, x + BX] = for_swaps("gy", value[:4], value[4:])
-
-
-def tall(own, left, right, below, above, array, x):
-    value = wide_x(own, left, right, array, x)
-    rim = jnp.concatenate([above(array, x + BX), below(array, x + BX)], 0)
-    return jnp.concatenate([value, rim], 0)
-
-
-def groups():
-    made = []
-    for x in range(-BX, 2 * BX):
-        made.append((x + BX, [(i, x) for i in range(4)]))
-    for x in range(-BX, 3):
-        made.append((18 + x + BX, [(4, x), (5, x), (4, x + 9), (5, x + 9)]))
-    return made
-
-
-def rim_z_kernel(own, xa, xb, ya, yb, za, zb):
+        for n in range(7):
+            one = wide_raw(own, left, right, array, 2 * n - 4)
+            two = wide_raw(own, left, right, array, 2 * n - 3)
+            low = jnp.where(near, one, roll(two, 4, 0))
+            high = jnp.where(near, roll(one, 4, 0), two)
+            at = 48 + 7 * array + n
+            ya[at], yb[at] = for_swaps("gy", low, high)
+    first = iota(shape, 0) == 0
+    last = iota(shape, 0) == 7
+    kept = {side: lies(shape, FAR[side]) for side in FAR}
+    for n in range(7):
+        rows = [[wide[2 * n + 5 + m, pl.ds(8 * t, 8), :] for t in (0, 1)] for m in (0, 1)]
+        low = [jnp.where(first, top, rim) for top, rim in rows]
+        high = [jnp.where(last, top, rim) for top, rim in rows]
+        low = jnp.where(kept["up"], low[0], roll(low[1], 4, 0))
+        high = jnp.where(kept["down"], high[0], roll(high[1], 4, 0))
+        yya[n], yyb[n] = for_swaps("gy", low, high, 2)
+
+
+def raw_rim(below, above, array, x):
+    n, odd = divmod(x + 4, 2)
+    at = 48 + 7 * array + n
+    near = iota((8, LANES), 0) < 4
+    if odd:
+        return jnp.where(near, roll(above(at), 4, 0), below(at))
+    return jnp.where(near, above(at), roll(below(at), 4, 0))
+
+
+def raw_items():
+    items = [(array, x) for array in range(6) for x in RAW]
+    return [items[16 * n : 16 * n + 16] for n in range(6)]
+
+
+def join_y_kernel(own, xa, xb, wide, ya, yb, yya, yyb, tall, raw, za, zb):
     left, right = sides("gx", xa, xb)
     below, above = sides("gy", ya, yb)
+    below2, above2 = sides("gy", yya, yyb, 2)
+    shape = (8, LANES)
+    row = iota(shape, 0)
+    zero = jnp.zeros(shape, F32)
+    for x in range(-9, BX + 9):
+        at = x + 9
+        mine = [wide[at, pl.ds(8 * t, 8), :] for t in (0, 1)]
+        up = [above(2 * at + t) for t in (0, 1)]
+        down = [below(2 * at + t) for t in (0, 1)]
+        far_up = far_down = zero
+        if x in RAW:
+            n, odd = divmod(x + 4, 2)
+            far_up, far_down = above2(n), below2(n)
+            if odd:
+                far_up, far_down = roll(far_up, 4, 0), roll(far_down, 4, 0)
+        tiles = [
+            mine[0] + jnp.where(row >= 5, up[1], jnp.where(row < 3, down[1], 0.0)),
+            up[0] + jnp.where(row < 4, mine[1], jnp.where(row >= 5, far_up, 0.0)),
+            jnp.where(row == 0, up[1] + far_up, jnp.where(row == 7, down[1] + far_down, 0.0)),
+            down[0] + jnp.where(row >= 4, mine[1], jnp.where(row < 3, far_down, 0.0)),
+        ]
+        tall[at] = jnp.concatenate(tiles, 0)
+    lane = iota((32, LANES), 1)
+    for slot in range(3):
+        low = high = None
+        for g in range(8):
+            value = tall[8 * slot + g]
+            one, two = roll(value, 16 * g + 3, 1), roll(value, 16 * g - 55, 1)
+            low = one if low is None else jnp.where(lane // 16 == g, one, low)
+            high = two if high is None else jnp.where(lane // 16 == g, two, high)
+        for t in range(4):
+            rows = slice(8 * t, 8 * t + 8)
+            za[4 * slot + t], zb[4 * slot + t] = for_swaps("gz", low[rows], high[rows])
     lane = iota((16, LANES), 1)
-    for slot, members in groups():
-        lows = highs = None
-        for i, (array, x) in enumerate(members):
-            value = tall(own, left, right, below, above, array, x)
-            down = roll(value, 16 * i, 1)
-            up = roll(value, 16 * (i + 1), 1)
-            lows = down if lows is None else jnp.where((lane % 64) // 16 == i, down, lows)
-            highs = up if highs is None else jnp.where((lane % 64) // 16 == i, up, highs)
-        za[slot], zb[slot] = for_swaps("gz", lows, highs)
-
-
-def fine_kernel(own, xa, xb, ya, yb, za, zb, level, fine, kept, fref, sref):
-    left, right = sides("gx", xa, xb)
-    below, above = sides("gy", ya, yb)
+    for slot, items in enumerate(raw_items()):
+        low = high = None
+        for i, (array, x) in enumerate(items):
+            body = [wide_raw(own, left, right, array, x), raw_rim(below, above, array, x)]
+            value = jnp.concatenate(body, 0)
+            raw[array, x + 4] = value
+            one, two = roll(value, 4 * i, 1), roll(value, 4 * i + 4, 1)
+            low = one if low is None else jnp.where((lane % 64) // 4 == i, one, low)
+            high = two if high is None else jnp.where((lane % 64) // 4 == i, two, high)
+        for t in (0, 1):
+            rows = slice(8 * t, 8 * t + 8)
+            at = 12 + 2 * slot + t
+            za[at], zb[at] = for_swaps("gz", low[rows], high[rows])
+
+
+def field_slot(cell, x):
+    return CELLS.index(cell) * len(RAW) + x + 4
+
+
+class Lattice:
+    def __init__(self, ref):
+        self.ref = ref
+
+    def get(self, key):
+        return self.ref[field_slot(*key)] if key[1] in RAW else None
+
+    def put(self, key, value):
+        self.ref[field_slot(*key)] = value
+
+
+def fine_kernel(raw, za, zb, fine, kept):
     before, after = sides("gz", za, zb)
-    source, field = Kept(sref), Kept(fref)
+    source, field = Lattice(kept), Known(fine)
     lane = iota((16, LANES), 1)
-    home = {}
-    for slot, members in groups():
-        for i, key in enumerate(members):
-            home[key] = (slot, i)
-    for array in range(6):
-        for x in range(-BX, 2 * BX):
-            value = tall(own, left, right, below, above, array, x)
-            slot, i = home[(array, x)]
-            up, down = after(slot), before(slot)
+    for slot, items in enumerate(raw_items()):
+        pair = (12 + 2 * slot, 13 + 2 * slot)
+        up = jnp.concatenate([after(at) for at in pair], 0)
+        down = jnp.concatenate([before(at) for at in pair], 0)
+        for i, (array, x) in enumerate(items):
+            value = raw[array, x + 4]
             for c in (0, 1):
                 mine = roll(value, 64, 1) if c else value
-                right_rim = roll(up, 64 - 16 * i - 64 * c, 1)
-                left_rim = roll(down, 48 - 16 * i + 64 * c, 1)
                 full = jnp.where(lane < 64, mine, 0.0)
-                full = jnp.where((lane >= 64) & (lane < 80), right_rim, full)
-                full = jnp.where(lane >= 112, left_rim, full)
+                full = jnp.where((lane >= 64) & (lane < 68), roll(up, 64 - 4 * i - 64 * c, 1), full)
+                full = jnp.where(lane >= 124, roll(down, 60 - 4 * i + 64 * c, 1), full)
                 if array < 4:
                     source.put(((array // 2, array % 2, c), x), full)
                 else:
                     a = array - 4
-                    b = (1 + a + c) % 2
-                    field.put(((a, b, c), x), full)
-    for step, depth in enumerate((10, 9, 8, 7)):
+                    field.put(((a, (1 + a + c) % 2, c), x), full)
+    for step, depth in enumerate((7, 6, 5, 4)):
         fine_half(field, source, step % 2, depth)
-    for x in range(-3, BX + 3):
-        level[x + 3] = coarsened(field, source, x)
-    for n, cell in enumerate(CELLS):
-        for x in range(-2, BX + 2):
-            fine[n, x + 2] = field.get((cell, x))
-            kept[n, x + 2] = source.get((cell, x))
-
-
-def level_y_kernel(own, ya, yb, wide, xa, xb):
-    below, above = sides("gy", ya, yb)
-    first = iota((8, LANES), 0) == 0
-    last = iota((8, LANES), 0) == 7
-    for x in range(12):
-        mine, down, up = own[x], below(x), above(x)
-        tail = jnp.where(first, up[8:16], 0.0)
-        lead = jnp.where(last, down[8:16], 0.0)
-        value = jnp.concatenate([mine[:8], up[:8], tail + lead, down[:8]], 0)
-        wide[x] = value
-    for x in range(9):
-        xa[x], xb[x] = for_swaps("gx", wide[x + 3], wide[x])
-
-
-def mid_kernel(wide, xa, xb, level, mid, eref):
-    left, right = sides("gx", xa, xb)
-    for x in range(-9, BX + 9):
-        if x < 0:
-            value = left(x + 9)
-        elif x >= BX:
-            value = right(x - BX)
-        else:
-            value = wide[x + 3]
-        level[x + 9] = value
+
+
+class Known(Lattice):
+    def __init__(self, ref):
+        super().__init__(ref)
+        self.put_keys = set()
+
+    def get(self, key):
+        return super().get(key) if key in self.put_keys else None
+
+    def put(self, key, value):
+        self.put_keys.add(key)
+        super().put(key, value)
+
+
+def mid_kernel(tall, za, zb, level, mid, eref):
+    before, after = sides("gz", za, zb)
+    lane = iota((32, LANES), 1)
+    own = (lane < 67) | (lane >= 125)
+    for slot in range(3):
+        up = jnp.concatenate([after(4 * slot + t) for t in range(4)], 0)
+        down = jnp.concatenate([before(4 * slot + t) for t in range(4)], 0)
+        for g in range(8):
+            value = jnp.where(own, tall[8 * slot + g], 0.0)
+            value = value + jnp.where((lane >= 61) & (lane < 73), roll(up, 61 - 16 * g, 1), 0.0)
+            value = value + jnp.where((lane < 3) | (lane >= 119), roll(down, 119 - 16 * g, 1), 0.0)
+            level[8 * slot + g] = value
     source = Given(level, 9, 24)
     error = Kept(eref)
     masks = [red_of((32, LANES), x) for x in (0, 1)]
@@ -431,12 +525,31 @@
         self.ref[x + self.start] = value
 
 
-def last_kernel(got, qxz, inverse, tx, ty, tz, level, mid, fine, kept, out, eref, fref, oref, *, axes):
-    one, two = got[:, 0, :], got[:, 1, :]
-    blocks = one + roll(roll(one, 64, 1), 1, 0) + roll(two, -1, 0)
+def solve_kernel(got, qxz, inverse, tx, ty, tz, coarse, constant):
+    lane = iota((GZ, LANES), 1)
+    kind = lane % 16
+    row, col = iota((8, LANES), 0), iota((8, LANES), 1)
+    pick = jnp.where((col // 16 == row) & (col % 16 < 15), 1.0, 0.0)
+    halves_of, mean = [], 0.0
+    for r in (0, 1):
+        values = got[:, r, :]
+        lines = []
+        for i in range(GX):
+            line = values[GZ * i : GZ * i + GZ]
+            mean = mean + jnp.where(kind == 15, line, 0.0)
+            total = jnp.where(kind // 5 == 0, line, 0.0)
+            total = total + roll(jnp.where(kind // 5 == 1, line, 0.0), 1, 0)
+            lines.append(total + roll(jnp.where(kind // 5 == 2, line, 0.0), -1, 0))
+        rows = []
+        for i in range(GX):
+            total = lines[(i + 2) % GX]
+            for d in range(1, 5):
+                total = jnp.where(kind % 5 == d, lines[(i - (d - 2)) % GX], total)
+            rows.append(total)
+        halves_of.append(dot_nt(pick, jnp.concatenate(rows + rows, 0)))
+    blocks = jnp.concatenate(halves_of, 0)
     inside = iota((GY, LANES), 1) < GX * GZ
-    mean = jnp.sum(jnp.where(inside, 0.0, two), keepdims=True)
-    mean = mean * (1.0 / (GX * GY * GZ * 8 * BX * BY * BZ))
+    mean = jnp.sum(mean, keepdims=True) * (1.0 / (GX * GY * GZ * 8 * BX * BY * BZ))
     blocks = jnp.where(inside, blocks, 0.0)
     level_out = jnp.sum(blocks, keepdims=True) * (1.0 / (GX * GY * GZ))
     blocks = jnp.where(inside, blocks - level_out, 0.0)
@@ -445,7 +558,7 @@
     for y in range(GY):
         modes = plus(modes, half[y : y + 1, :] * ty[y + 1])
     modes = modes * inverse[...]
-    ix, iy, iz = axes
+    ix, iy, iz = (lax.axis_index(axis) for axis in ("gx", "gy", "gz"))
     own_lane = iota((LANES, LANES), 0)
     zrow = lambda d: tz[pl.ds(iz + 1 + d, 1), :]
     spread_z = jnp.where(own_lane < 64, zrow(0), jnp.where(own_lane < 96, zrow(1), zrow(-1)))
@@ -456,7 +569,12 @@
         for dx in (-1, 0, 1):
             both = line * tx[pl.ds(ix + 1 + dx, 1), :]
             stacked = jnp.where(place == 3 * (dx + 1) + dy + 1, both, stacked)
-    coarse = dot_nt(stacked, spread_z)
+    coarse[...] = dot_nt(stacked, spread_z)
+    constant[...] = jnp.broadcast_to(mean, (8, LANES))
+
+
+def place_kernel(solved, constant, level, mid, fine, kept, out, eref, fref, oref):
+    coarse, mean = solved[...], constant[...]
     row = iota((32, LANES), 0)
     error = Given(eref, 6, 18)
     for dx in (-1, 0, 1):
@@ -469,12 +587,12 @@
     for step, depth in enumerate((5, 4, 3, 2)):
         one_half(error, source, step % 2, -depth, BX + depth, masks)
     near = iota((8, LANES), 0) < 4
-    field, terms = Kept(fref), Sources(kept)
+    field, terms = Kept(fref), Lattice(kept)
     for x in range(-2, BX + 2):
         e = error.get(x)
         e = jnp.concatenate([e[:8], jnp.where(near, e[8:16], e[24:])], 0)
-        for n, cell in enumerate(CELLS):
-            field.put((cell, x), fine[n, x + 2] + e)
+        for cell in CELLS:
+            field.put((cell, x), fine[field_slot(cell, x)] + e)
     for step, depth in enumerate((3, 2, 1, 0)):
         fine_half(field, terms, step % 2, depth)
     v = unit_response()
@@ -494,15 +612,6 @@
     out[...] = dot_nt(oref[...], parting()).reshape(12, 16, LANES)
 
 
-class Sources:
-    def __init__(self, ref):
-        self.ref = ref
-
-    def get(self, key):
-        cell, x = key
-        return self.ref[CELLS.index(cell), x + 2] if -2 <= x < BX + 2 else None
-
-
 def run(kernel, shapes, args, scratch=(), flops=500000000):
     space = pl.BlockSpec(memory_space=pltpu.VMEM)
     moved = 4 * sum(int(np.prod(s)) for s in shapes)
@@ -517,15 +626,10 @@
     )(*args)
 
 
-def place_kernel(*refs):
-    axes = (lax.axis_index("gx"), lax.axis_index("gy"), lax.axis_index("gz"))
-    last_kernel(*refs, axes=axes)
-
-
-def swapped(first, second, axis):
+def swapped(first, second, axis, step=1):
     count = lax.axis_size(axis)
-    one = [(i, i ^ 1) for i in range(count)]
-    two = [(i, (i + 1 if i % 2 else i - 1) % count) for i in range(count)]
+    one = [(i, i ^ step) for i in range(count)]
+    two = [(i, (i + step if (i // step) % 2 else i - step) % count) for i in range(count)]
     got = lax.ppermute(first, axis, one)
     return got, lax.ppermute(second, axis, two)
 
@@ -537,35 +641,44 @@
 def steps(density, potential):
     tables = [jnp.asarray(t) for t in coarse_tables()]
     (own,) = run(part_kernel, [(6, 6, 8, LANES)], [density, potential], [(192, LANES)] * 2)
-    xs = swapped(own, own, "gx")
-    (shares,) = run(
+    level, xa, xb, xxa, xxb = run(
+        spread_kernel,
+        [(12, 16, LANES), (48, 8, LANES), (48, 8, LANES), (12, 8, LANES), (12, 8, LANES)],
+        [own],
+        [(96, 16, LANES), (48, 16, LANES)],
+    )
+    xx = swapped(xxa, xxb, "gx", 2)
+    xs = swapped(xa, xb, "gx")
+    (share,) = run(
         share_kernel,
-        [(GX * GZ, 1, LANES)],
-        [own],
-        [(96, 16, LANES), (48, 16, LANES), (20, 24, LANES), (12, 24, LANES), (LANES, LANES)],
+        [(GY, 1, LANES)],
+        [own, level],
+        [(20, 24, LANES), (12, 24, LANES), (LANES, LANES)],
     )
-    (plane,) = run(along_xz_kernel, [(GY, 2, LANES)], [everyone(shares, ("gx", "gz"))])
-    blocks = everyone(plane, "gy")
-    ys = swapped(*run(rim_y_kernel, [(6, 18, 4, LANES)] * 2, [own, *xs]), "gy")
-    zs = swapped(*run(rim_z_kernel, [(27, 16, LANES)] * 2, [own, *xs, *ys]), "gz")
-    level, fine, kept = run(
-        fine_kernel,
-        [(12, 16, LANES), (8, 10, 16, LANES), (8, 10, 16, LANES)],
-        [own, *xs, *ys, *zs],
-        [(144, 16, LANES), (144, 16, LANES)],
+    (line,) = run(along_y_kernel, [(GX * GZ, 2, LANES)], [everyone(share, "gy")])
+    blocks = everyone(line, ("gx", "gz"))
+    wide, ya, yb, yya, yyb = run(
+        join_x_kernel,
+        [(24, 16, LANES), (90, 8, LANES), (90, 8, LANES), (7, 8, LANES), (7, 8, LANES)],
+        [own, level, *xs, *xx],
     )
-    ys = swapped(level, level, "gy")
-    wide, xa, xb = run(
-        level_y_kernel, [(12, 32, LANES), (9, 32, LANES), (9, 32, LANES)], [level, *ys]
+    yy = swapped(yya, yyb, "gy", 2)
+    ys = swapped(ya, yb, "gy")
+    tall, raw, za, zb = run(
+        join_y_kernel,
+        [(24, 32, LANES), (6, 14, 16, LANES), (24, 8, LANES), (24, 8, LANES)],
+        [own, *xs, wide, *ys, *yy],
     )
-    xs = swapped(xa, xb, "gx")
+    zs = swapped(za, zb, "gz")
     level, mid = run(
-        mid_kernel, [(24, 32, LANES), (18, 32, LANES)], [wide, *xs], [(24, 32, LANES)]
+        mid_kernel, [(24, 32, LANES), (18, 32, LANES)], [tall, *zs], [(24, 32, LANES)]
     )
+    fine, kept = run(fine_kernel, [(112, 16, LANES)] * 2, [raw, *zs])
+    solved = run(solve_kernel, [(16, LANES), (8, LANES)], [blocks, *tables])
     (out,) = run(
         place_kernel,
         [(12, 16, LANES)],
-        [blocks, *tables, level, mid, fine, kept],
+        [*solved, level, mid, fine, kept],
         [(18, 32, LANES), (80, 16, LANES), (192, LANES)],
     )
     return out

time: 109 us -> 95.8 us (0.88)
  the two profiles are of different devices: /device:TPU:1 before, /device:TPU:7 now
where the time goes in v5:
time: 95.8 us; the launch traced here: 95.3 us
  starting transfers between devices  57.4 us (60%)
  blocking collectives  15.8 us (16%)
  waiting for transfers between devices  11.6 us (12%)
  Pallas kernels  8.48 us (9%)
  local copies, waits for them, and re-layouts  1.82 us (2%)
    ppermute x5, starting transfers between devices, swapped(): return (got, lax.ppermute(second, axis, two))  29.1 us
    all_to_all x1, blocking collectives, everyone(): return lax.all_to_all(array, axis, 0, 0, tiled=True)  15.8 us
    ppermute x5, starting transfers between devices, swapped(): got = lax.ppermute(first, axis, one)  15 us
    all_to_all x1, starting transfers between devices, everyone(): return lax.all_to_all(array, axis, 0, 0, tiled=True)  13.2 us
    ppermute x5, waiting for transfers between devices, swapped(): return (got, lax.ppermute(second, axis, two))  9.85 us
    pallas_call x10, Pallas kernels, run(): pl.pallas_call(kernel, out_shape=[jax.ShapeDtypeStruct(s, F32) for s in s...  8.48 us
  transfers between devices with their start and end apart: 11, of which 5 were waited for; matrix products, arithmetic and copies ran while one was open for 0% of the time, Pallas kernels for 4%

profile of v5, /device:TPU:7, one launch (start us, length us, event | category | flops | bytes accessed | tf_op | source)
XLA Modules:
  0.0 95.3 jit_solution(16681407368012252261)
XLA Ops:
  0.0 0.9 copy-done
  0.9 0.9 copy-done.1
  1.8 0.3 shard_map.73.pairs.own
  2.1 0.6 shard_map.74
  2.8 3.2 %collective-permute-start = (f32[48,8,128]{2,1,0:T(8,128)S(1)}, f32[48,8,128]{2,1,0:T(8,128)S(1)}, u32[]{:S(2)}, u32[]{:S(2)}) collective-permute-start(f32[48,8,128]{2,1,0:T(8,128)S(1)} %get-tuple-element.28), channel_id=1, source_target_pairs={{0,128},{128,0},{256,384},{384,256},{512,640},{640,512},{768,896},... | collective-permute-start | bytes 589832 | tf_op jit(solution)/shard_map/ppermute | solution.py:633
  6.0 4.9 %collective-permute-start.1 = (f32[48,8,128]{2,1,0:T(8,128)S(1)}, f32[48,8,128]{2,1,0:T(8,128)S(1)}, u32[]{:S(2)}, u32[]{:S(2)}) collective-permute-start(f32[48,8,128]{2,1,0:T(8,128)S(1)} %get-tuple-element.29), channel_id=1, source_target_pairs={{0,896},{128,256},{256,128},{384,512},{512,384},{640,768},{768,640... | collective-permute-start | bytes 589832 | tf_op jit(solution)/shard_map/ppermute | solution.py:634
  10.9 1.9 %collective-permute-start.2 = (f32[12,8,128]{2,1,0:T(8,128)S(1)}, f32[12,8,128]{2,1,0:T(8,128)S(1)}, u32[]{:S(2)}, u32[]{:S(2)}) collective-permute-start(f32[12,8,128]{2,1,0:T(8,128)S(1)} %get-tuple-element.30), channel_id=1, source_target_pairs={{0,256},{128,384},{256,0},{384,128},{512,768},{640,896},{768,512},... | collective-permute-start | bytes 147464 | tf_op jit(solution)/shard_map/ppermute | solution.py:633
  12.8 3.9 %collective-permute-start.3 = (f32[12,8,128]{2,1,0:T(8,128)S(1)}, f32[12,8,128]{2,1,0:T(8,128)S(1)}, u32[]{:S(2)}, u32[]{:S(2)}) collective-permute-start(f32[12,8,128]{2,1,0:T(8,128)S(1)} %get-tuple-element.31), channel_id=1, source_target_pairs={{0,768},{128,896},{256,512},{384,640},{512,256},{640,384},{768,0},... | collective-permute-start | bytes 147464 | tf_op jit(solution)/shard_map/ppermute | solution.py:634
  16.7 0.1 collective-permute-done.2.xxa
  16.7 3.0 %collective-permute-done.3.xxb = f32[12,8,128]{2,1,0:T(8,128)S(1)} collective-permute-done((f32[12,8,128]{2,1,0:T(8,128)S(1)}, f32[12,8,128]{2,1,0:T(8,128)S(1)}, u32[]{:S(2)}, u32[]{:S(2)}) %collective-permute-start.3) | collective-permute-done | bytes 49184 | tf_op jit(solution)/shard_map/ppermute | solution.py:634
  19.7 0.1 shard_map.78
  19.8 4.0 %collective-permute-start.4 = (f32[90,8,128]{2,1,0:T(8,128)S(1)}, f32[90,8,128]{2,1,0:T(8,128)S(1)}, u32[]{:S(2)}, u32[]{:S(2)}) collective-permute-start(f32[90,8,128]{2,1,0:T(8,128)S(1)} %get-tuple-element.33), channel_id=1, source_target_pairs={{0,8},{8,0},{16,24},{24,16},{32,40},{40,32},{48,56},{56,48},{64,72... | collective-permute-start | bytes 1105928 | tf_op jit(solution)/shard_map/ppermute | solution.py:633
  23.9 16.1 %collective-permute-start.5 = (f32[90,8,128]{2,1,0:T(8,128)S(1)}, f32[90,8,128]{2,1,0:T(8,128)S(1)}, u32[]{:S(2)}, u32[]{:S(2)}) collective-permute-start(f32[90,8,128]{2,1,0:T(8,128)S(1)} %get-tuple-element.34), channel_id=1, source_target_pairs={{0,120},{8,16},{16,8},{24,32},{32,24},{40,48},{48,40},{56,64},{64,... | collective-permute-start | bytes 1105928 | tf_op jit(solution)/shard_map/ppermute | solution.py:634
  40.0 1.1 %shard_map.75 = f32[16,1,128]{2,1,0:T(1,128)S(1)} custom-call(f32[6,6,8,128]{3,2,1,0:T(8,128)S(1)} %shard_map.73.pairs.own, f32[12,16,128]{2,1,0:T(8,128)S(1)} %get-tuple-element.25.given.level), custom_call_target="tpu_custom_call" | custom-call | flops 500000000 | bytes 8192 | tf_op jit(solution)/shard_map/pallas_call | solution.py:618
  41.1 15.8 %all_to_all.10.got = f32[16,1,128]{2,1,0:T(1,128)S(1)} all-to-all(f32[16,1,128]{2,1,0:T(1,128)S(1)} %shard_map.75), channel_id=1, replica_groups=mesh['gx'=8,'gy'=16,'gz'=8] {'gy'}, dimensions={0} | all-to-all | bytes 16384 | tf_op jit(solution)/shard_map/all_to_all | solution.py:638
  56.9 0.8 shard_map.76
  57.7 13.2 %all-to-all-start.1 = ((f32[64,2,128]{2,1,0:T(2,128)}), f32[64,2,128]{2,1,0:T(2,128)S(1)}, u32[]{:S(2)}, u32[]{:S(2)}) async-start(f32[64,2,128]{2,1,0:T(2,128)} %shard_map.76), calls=%async_computation.1 | async-start | bytes 131072 | tf_op jit(solution)/shard_map/all_to_all | solution.py:638
  71.0 2.2 %collective-permute-start.6 = (f32[7,8,128]{2,1,0:T(8,128)S(1)}, f32[7,8,128]{2,1,0:T(8,128)S(1)}, u32[]{:S(2)}, u32[]{:S(2)}) collective-permute-start(f32[7,8,128]{2,1,0:T(8,128)S(1)} %get-tuple-element.35), channel_id=1, source_target_pairs={{0,16},{8,24},{16,0},{24,8},{32,48},{40,56},{48,32},{56,40},{64,80... | collective-permute-start | bytes 86024 | tf_op jit(solution)/shard_map/ppermute | solution.py:633
  73.1 2.3 %collective-permute-start.7 = (f32[7,8,128]{2,1,0:T(8,128)S(1)}, f32[7,8,128]{2,1,0:T(8,128)S(1)}, u32[]{:S(2)}, u32[]{:S(2)}) collective-permute-start(f32[7,8,128]{2,1,0:T(8,128)S(1)} %get-tuple-element.36), channel_id=1, source_target_pairs={{0,112},{8,120},{16,32},{24,40},{32,16},{40,24},{48,64},{56,72},{6... | collective-permute-start | bytes 86024 | tf_op jit(solution)/shard_map/ppermute | solution.py:634
  75.4 1.7 %collective-permute-done.6.yya = f32[7,8,128]{2,1,0:T(8,128)S(1)} collective-permute-done((f32[7,8,128]{2,1,0:T(8,128)S(1)}, f32[7,8,128]{2,1,0:T(8,128)S(1)}, u32[]{:S(2)}, u32[]{:S(2)}) %collective-permute-start.6) | collective-permute-done | bytes 28704 | tf_op jit(solution)/shard_map/ppermute | solution.py:633
  77.1 2.8 %collective-permute-done.7.yyb = f32[7,8,128]{2,1,0:T(8,128)S(1)} collective-permute-done((f32[7,8,128]{2,1,0:T(8,128)S(1)}, f32[7,8,128]{2,1,0:T(8,128)S(1)}, u32[]{:S(2)}, u32[]{:S(2)}) %collective-permute-start.7) | collective-permute-done | bytes 28704 | tf_op jit(solution)/shard_map/ppermute | solution.py:634
  79.9 0.0 copy-start.4
  79.9 0.0 copy-start.5
  79.9 0.0 copy-start.6
  79.9 0.6 shard_map.79
  80.6 3.7 %collective-permute-start.8 = (f32[24,8,128]{2,1,0:T(8,128)S(1)}, f32[24,8,128]{2,1,0:T(8,128)S(1)}, u32[]{:S(2)}, u32[]{:S(2)}) collective-permute-start(f32[24,8,128]{2,1,0:T(8,128)S(1)} %get-tuple-element.38), channel_id=1, source_target_pairs={{0,1},{1,0},{2,3},{3,2},{4,5},{5,4},{6,7},{7,6},{8,9},{9,8},{10,11... | collective-permute-start | bytes 294920 | tf_op jit(solution)/shard_map/ppermute | solution.py:633
  84.3 2.0 %collective-permute-start.9 = (f32[24,8,128]{2,1,0:T(8,128)S(1)}, f32[24,8,128]{2,1,0:T(8,128)S(1)}, u32[]{:S(2)}, u32[]{:S(2)}) collective-permute-start(f32[24,8,128]{2,1,0:T(8,128)S(1)} %get-tuple-element.39), channel_id=1, source_target_pairs={{0,7},{1,2},{2,1},{3,4},{4,3},{5,6},{6,5},{7,0},{8,15},{9,10},{10,... | collective-permute-start | bytes 294920 | tf_op jit(solution)/shard_map/ppermute | solution.py:634
  86.3 1.0 %shard_map.77 = (f32[16,128]{1,0:T(8,128)S(1)}, f32[8,128]{1,0:T(8,128)S(1)}) custom-call(f32[64,2,128]{2,1,0:T(2,128)S(1)} %all-to-all-done.1.got, f32[128,128]{1,0:T(8,128)S(1)} %copy-done.3, f32[16,128]{1,0:T(8,128)S(1)} %copy-done.4, f32[10,128]{1,0:T(8,128)S(1)} %copy-done.5, f32[18,16,128]{2,1,0:T(8,128)S(1)} %copy-done.2, f32[10,128]{1,0:T(8,128)S(1)} %copy-done.6), custom_call_target="tpu_custom_call" | custom-call | flops 500000000 | bytes 12288 | tf_op jit(solution)/shard_map/pallas_call | solution.py:618
  87.4 4.1 %collective-permute-done.9.zb = f32[24,8,128]{2,1,0:T(8,128)S(1)} collective-permute-done((f32[24,8,128]{2,1,0:T(8,128)S(1)}, f32[24,8,128]{2,1,0:T(8,128)S(1)}, u32[]{:S(2)}, u32[]{:S(2)}) %collective-permute-start.9) | collective-permute-done | bytes 98336 | tf_op jit(solution)/shard_map/ppermute | solution.py:634
  91.4 1.4 %shard_map.81 = (f32[112,16,128]{2,1,0:T(8,128)S(1)}, f32[112,16,128]{2,1,0:T(8,128)S(1)}) custom-call(f32[6,14,16,128]{3,2,1,0:T(8,128)S(1)} %get-tuple-element.42.raw, f32[24,8,128]{2,1,0:T(8,128)S(1)} %collective-permute-done.8.za, f32[24,8,128]{2,1,0:T(8,128)S(1)} %collective-permute-done.9.zb), custom_call_target="tpu_custom_call" | custom-call | flops 500000000 | bytes 1835008 | tf_op jit(solution)/shard_map/pallas_call | solution.py:618
  92.8 0.8 shard_map.80
  93.6 1.7 %shard_map.82 = f32[12,16,128]{2,1,0:T(8,128)} custom-call(f32[16,128]{1,0:T(8,128)S(1)} %get-tuple-element.26.solved, f32[8,128]{1,0:T(8,128)S(1)} %get-tuple-element.27.constant, f32[24,32,128]{2,1,0:T(8,128)S(1)} %get-tuple-element.40.level, f32[18,32,128]{2,1,0:T(8,128)S(1)} %get-tuple-element.41.mid, f32[112,16,128]{2,1,0:T(8,128)S(1)} %get-tuple-element.43.fine, ...), custom_call_target="tpu_custom_call" | custom-call | flops 500000000 | bytes 98304 | tf_op jit(solution)/shard_map/pallas_call | solution.py:618
  (15 shorter events, 0.0 us)
Async XLA Ops:
  0.0 0.9 copy-start
  0.9 0.9 copy-start.1
  2.8 17.0 %collective-permute-start = (f32[48,8,128]{2,1,0:T(8,128)S(1)}, f32[48,8,128]{2,1,0:T(8,128)S(1)}, u32[]{:S(2)}, u32[]{:S(2)}) collective-permute-start(f32[48,8,128]{2,1,0:T(8,128)S(1)} %get-tuple-element.28), channel_id=1, source_target_pairs={{0,128},{128,0},{256,384},{384,256},{512,640},{640,512},{768,896},... | collective-permute-start | bytes 589832 | tf_op jit(solution)/shard_map/ppermute | solution.py:633
  6.0 13.8 %collective-permute-start.1 = (f32[48,8,128]{2,1,0:T(8,128)S(1)}, f32[48,8,128]{2,1,0:T(8,128)S(1)}, u32[]{:S(2)}, u32[]{:S(2)}) collective-permute-start(f32[48,8,128]{2,1,0:T(8,128)S(1)} %get-tuple-element.29), channel_id=1, source_target_pairs={{0,896},{128,256},{256,128},{384,512},{512,384},{640,768},{768,640... | collective-permute-start | bytes 589832 | tf_op jit(solution)/shard_map/ppermute | solution.py:634
  10.9 5.9 %collective-permute-start.2 = (f32[12,8,128]{2,1,0:T(8,128)S(1)}, f32[12,8,128]{2,1,0:T(8,128)S(1)}, u32[]{:S(2)}, u32[]{:S(2)}) collective-permute-start(f32[12,8,128]{2,1,0:T(8,128)S(1)} %get-tuple-element.30), channel_id=1, source_target_pairs={{0,256},{128,384},{256,0},{384,128},{512,768},{640,896},{768,512},... | collective-permute-start | bytes 147464 | tf_op jit(solution)/shard_map/ppermute | solution.py:633
  12.8 6.9 %collective-permute-start.3 = (f32[12,8,128]{2,1,0:T(8,128)S(1)}, f32[12,8,128]{2,1,0:T(8,128)S(1)}, u32[]{:S(2)}, u32[]{:S(2)}) collective-permute-start(f32[12,8,128]{2,1,0:T(8,128)S(1)} %get-tuple-element.31), channel_id=1, source_target_pairs={{0,768},{128,896},{256,512},{384,640},{512,256},{640,384},{768,0},... | collective-permute-start | bytes 147464 | tf_op jit(solution)/shard_map/ppermute | solution.py:634
  19.8 60.0 %collective-permute-start.4 = (f32[90,8,128]{2,1,0:T(8,128)S(1)}, f32[90,8,128]{2,1,0:T(8,128)S(1)}, u32[]{:S(2)}, u32[]{:S(2)}) collective-permute-start(f32[90,8,128]{2,1,0:T(8,128)S(1)} %get-tuple-element.33), channel_id=1, source_target_pairs={{0,8},{8,0},{16,24},{24,16},{32,40},{40,32},{48,56},{56,48},{64,72... | collective-permute-start | bytes 1105928 | tf_op jit(solution)/shard_map/ppermute | solution.py:633
  23.9 56.0 %collective-permute-start.5 = (f32[90,8,128]{2,1,0:T(8,128)S(1)}, f32[90,8,128]{2,1,0:T(8,128)S(1)}, u32[]{:S(2)}, u32[]{:S(2)}) collective-permute-start(f32[90,8,128]{2,1,0:T(8,128)S(1)} %get-tuple-element.34), channel_id=1, source_target_pairs={{0,120},{8,16},{16,8},{24,32},{32,24},{40,48},{48,40},{56,64},{64,... | collective-permute-start | bytes 1105928 | tf_op jit(solution)/shard_map/ppermute | solution.py:634
  57.7 28.6 %all-to-all-start.1 = ((f32[64,2,128]{2,1,0:T(2,128)}), f32[64,2,128]{2,1,0:T(2,128)S(1)}, u32[]{:S(2)}, u32[]{:S(2)}) async-start(f32[64,2,128]{2,1,0:T(2,128)} %shard_map.76), calls=%async_computation.1 | async-start | bytes 131072 | tf_op jit(solution)/shard_map/all_to_all | solution.py:638
  71.0 6.1 %collective-permute-start.6 = (f32[7,8,128]{2,1,0:T(8,128)S(1)}, f32[7,8,128]{2,1,0:T(8,128)S(1)}, u32[]{:S(2)}, u32[]{:S(2)}) collective-permute-start(f32[7,8,128]{2,1,0:T(8,128)S(1)} %get-tuple-element.35), channel_id=1, source_target_pairs={{0,16},{8,24},{16,0},{24,8},{32,48},{40,56},{48,32},{56,40},{64,80... | collective-permute-start | bytes 86024 | tf_op jit(solution)/shard_map/ppermute | solution.py:633
  73.1 6.7 %collective-permute-start.7 = (f32[7,8,128]{2,1,0:T(8,128)S(1)}, f32[7,8,128]{2,1,0:T(8,128)S(1)}, u32[]{:S(2)}, u32[]{:S(2)}) collective-permute-start(f32[7,8,128]{2,1,0:T(8,128)S(1)} %get-tuple-element.36), channel_id=1, source_target_pairs={{0,112},{8,120},{16,32},{24,40},{32,16},{40,24},{48,64},{56,72},{6... | collective-permute-start | bytes 86024 | tf_op jit(solution)/shard_map/ppermute | solution.py:634
  79.9 6.4 %copy-start.2 = (f32[18,16,128]{2,1,0:T(8,128)S(1)}, f32[18,16,128]{2,1,0:T(8,128)}, u32[]{:S(2)}) copy-start(f32[18,16,128]{2,1,0:T(8,128)} %constant.13.clone.ty) | copy-start | bytes 442372
  79.9 6.4 %copy-start.3 = (f32[128,128]{1,0:T(8,128)S(1)}, f32[128,128]{1,0:T(8,128)}, u32[]{:S(2)}) copy-start(f32[128,128]{1,0:T(8,128)} %constant.10.clone.qxz) | copy-start | bytes 196612
  79.9 6.4 %copy-start.4 = (f32[16,128]{1,0:T(8,128)S(1)}, f32[16,128]{1,0:T(8,128)}, u32[]{:S(2)}) copy-start(f32[16,128]{1,0:T(8,128)} %constant.11.clone.inverse) | copy-start | bytes 24580
  79.9 6.4 %copy-start.5 = (f32[10,128]{1,0:T(8,128)S(1)}, f32[10,128]{1,0:T(8,128)}, u32[]{:S(2)}) copy-start(f32[10,128]{1,0:T(8,128)} %constant.12.clone.tx) | copy-start | bytes 15364
  79.9 6.4 %copy-start.6 = (f32[10,128]{1,0:T(8,128)S(1)}, f32[10,128]{1,0:T(8,128)}, u32[]{:S(2)}) copy-start(f32[10,128]{1,0:T(8,128)} %constant.14.clone.tz) | copy-start | bytes 15364
  80.6 6.8 %collective-permute-start.8 = (f32[24,8,128]{2,1,0:T(8,128)S(1)}, f32[24,8,128]{2,1,0:T(8,128)S(1)}, u32[]{:S(2)}, u32[]{:S(2)}) collective-permute-start(f32[24,8,128]{2,1,0:T(8,128)S(1)} %get-tuple-element.38), channel_id=1, source_target_pairs={{0,1},{1,0},{2,3},{3,2},{4,5},{5,4},{6,7},{7,6},{8,9},{9,8},{10,11... | collective-permute-start | bytes 294920 | tf_op jit(solution)/shard_map/ppermute | solution.py:633
  84.3 7.1 %collective-permute-start.9 = (f32[24,8,128]{2,1,0:T(8,128)S(1)}, f32[24,8,128]{2,1,0:T(8,128)S(1)}, u32[]{:S(2)}, u32[]{:S(2)}) collective-permute-start(f32[24,8,128]{2,1,0:T(8,128)S(1)} %get-tuple-element.39), channel_id=1, source_target_pairs={{0,7},{1,2},{2,1},{3,4},{4,3},{5,6},{6,5},{7,0},{8,15},{9,10},{10,... | collective-permute-start | bytes 294920 | tf_op jit(solution)/shard_map/ppermute | solution.py:634
